TPU v7x, 8 devices: a whole 2x2x1 slice. The times are simulated.
8 devices in a mesh: dp: 1 (over z), tp: 8 (over y, x, core).
Axes of the slice: x: 2, y: 2, z: 1, core: 2. Of those that a mesh axis runs over, the one named last changes fastest.
Arguments:
- tokens: bfloat16 [3, 1024, 4096], P('dp', 'tp')
- start_pos: int32 [3], P('dp')
- cos_tab: float32 [3, 1024, 128], P('dp')
- sin_tab: float32 [3, 1024, 128], P('dp')
- key_cache: bfloat16 [2, 3, 4096, 8, 128], P(None, 'dp', None, 'tp')
- value_cache: bfloat16 [2, 3, 4096, 8, 128], P(None, 'dp', None, 'tp')
- slot_pos: int32 [3, 4096], P('dp')
- norm_params: bfloat16 [2, 4, 4096], replicated
- w_q: bfloat16 [2, 4096, 4096], P(None, None, 'tp')
- b_q: bfloat16 [2, 4096], P(None, 'tp')
- w_k: bfloat16 [2, 4096, 1024], P(None, None, 'tp')
- b_k: bfloat16 [2, 1024], P(None, 'tp')
- w_v: bfloat16 [2, 4096, 1024], P(None, None, 'tp')
- b_v: bfloat16 [2, 1024], P(None, 'tp')
- w_o: bfloat16 [2, 4096, 4096], P(None, 'tp')
- b_o: bfloat16 [2, 4096], replicated
- w_up: bfloat16 [2, 4096, 14336], P(None, None, 'tp')
- b_up: bfloat16 [2, 14336], P(None, 'tp')
- w_down: bfloat16 [2, 14336, 4096], P(None, 'tp')
- b_down: bfloat16 [2, 4096], replicated
Outputs:
- output 1: bfloat16 [3, 1024, 4096], P('dp', 'tp')
- output 2: bfloat16 [2, 3, 4096, 8, 128], P(None, 'dp', None, 'tp')
- output 3: bfloat16 [2, 3, 4096, 8, 128], P(None, 'dp', None, 'tp')
- output 4: int32 [3, 4096], P('dp')
All inputs are finite; a program needn't handle non-finite values.
Results may differ from a plain program's by a relative error of at most 0.02.
Values are sent between devices in bfloat16 or wider.
A program may use at most 1 GiB of HBM per device.

v0:
```python
import jax
import jax.numpy as jnp
from jax import lax
from jax.sharding import PartitionSpec as P

NORM_EPS = 1e-5


def layer_norm(hidden, gain, shift):
    values = hidden.astype(jnp.float32)
    centered = values - jnp.mean(values, axis=-1, keepdims=True)
    variance = jnp.mean(centered * centered, axis=-1, keepdims=True)
    scaled = centered * lax.rsqrt(variance + NORM_EPS)
    return (scaled * gain.astype(jnp.float32) + shift.astype(jnp.float32)).astype(jnp.bfloat16)


def apply_rotary(values, cos_b, sin_b):
    half = values.shape[-1] // 2
    turned = jnp.concatenate([-values[..., half:], values[..., :half]], axis=-1)
    return (values * cos_b + turned * sin_b).astype(jnp.bfloat16)


def write_chunk(cache, fresh, first_slot):
    window = cache.shape[0]
    length = fresh.shape[0]
    filler = jnp.zeros((window - length,) + fresh.shape[1:], fresh.dtype)
    placed = jnp.roll(jnp.concatenate([fresh, filler], axis=0), first_slot, axis=0)
    offset = (jnp.arange(window) - first_slot) % window
    keep = (offset >= length).reshape((window,) + (1,) * (cache.ndim - 1))
    return jnp.where(keep, cache, placed)


def project(acts, weight, bias):
    return jnp.einsum('bcm,mn->bcn', acts, weight, preferred_element_type=jnp.float32) + bias.astype(jnp.float32)


def local_attention(query, key_new, value_new, key_old, value_old, slot_pos, start_pos):
    chunk = query.shape[1]
    window = key_old.shape[1]
    scale = query.shape[-1] ** -0.5
    score_old = jnp.einsum('bckgd,bwkd->bkgcw', query, key_old, preferred_element_type=jnp.float32) * scale
    score_new = jnp.einsum('bckgd,bjkd->bkgcj', query, key_new, preferred_element_type=jnp.float32) * scale
    positions = start_pos[:, None] + jnp.arange(chunk)[None, :]
    held = slot_pos[:, None, :]
    old_ok = (held >= 0) & (held > positions[:, :, None] - window) & (held <= positions[:, :, None])
    new_ok = jnp.arange(chunk)[None, :] <= jnp.arange(chunk)[:, None]
    score_old = jnp.where(old_ok[:, None, None, :, :], score_old, -jnp.inf)
    score_new = jnp.where(new_ok, score_new, -jnp.inf)
    top = jnp.maximum(jnp.max(score_old, axis=-1, keepdims=True), jnp.max(score_new, axis=-1, keepdims=True))
    exp_old = jnp.exp(score_old - top)
    exp_new = jnp.exp(score_new - top)
    total = jnp.sum(exp_old, axis=-1) + jnp.sum(exp_new, axis=-1)
    mixed = jnp.einsum('bkgcw,bwkd->bckgd', exp_old.astype(jnp.bfloat16), value_old, preferred_element_type=jnp.float32)
    mixed = mixed + jnp.einsum('bkgcj,bjkd->bckgd', exp_new.astype(jnp.bfloat16), value_new, preferred_element_type=jnp.float32)
    return (mixed / jnp.transpose(total, (0, 3, 1, 2))[..., None]).astype(jnp.bfloat16)


def solution(mesh):
    row_spec = P('dp', 'tp', None)
    cache_spec = P(None, 'dp', None, 'tp', None)
    col_spec = P(None, None, 'tp')
    bias_spec = P(None, 'tp')
    in_specs = (row_spec, P('dp'), P('dp', None, None), P('dp', None, None), cache_spec, cache_spec, P('dp', None), P(), col_spec, bias_spec, col_spec, bias_spec, col_spec, bias_spec, P(None, 'tp', None), P(), col_spec, bias_spec, P(None, 'tp', None), P())
    out_specs = (row_spec, cache_spec, cache_spec, P('dp', None))

    def device_step(tokens, start_pos, cos_tab, sin_tab, key_cache, value_cache, slot_pos, norm_params, w_q, b_q, w_k, b_k, w_v, b_v, w_o, b_o, w_up, b_up, w_down, b_down):
        num_seqs = tokens.shape[0]
        chunk = cos_tab.shape[1]
        head_dim = cos_tab.shape[2]
        kv_local = w_k.shape[2] // head_dim
        group = w_q.shape[2] // w_k.shape[2]
        cos_b = cos_tab[:, :, None, :]
        sin_b = sin_tab[:, :, None, :]
        hidden = tokens
        fresh_keys = []
        fresh_values = []
        for layer in range(key_cache.shape[0]):
            normed = layer_norm(hidden, norm_params[layer, 0], norm_params[layer, 1])
            gathered = lax.all_gather(normed, 'tp', axis=1, tiled=True)
            query = apply_rotary(project(gathered, w_q[layer], b_q[layer]).reshape(num_seqs, chunk, kv_local * group, head_dim), cos_b, sin_b)
            key_new = apply_rotary(project(gathered, w_k[layer], b_k[layer]).reshape(num_seqs, chunk, kv_local, head_dim), cos_b, sin_b)
            value_new = project(gathered, w_v[layer], b_v[layer]).astype(jnp.bfloat16).reshape(num_seqs, chunk, kv_local, head_dim)
            mixed = local_attention(query.reshape(num_seqs, chunk, kv_local, group, head_dim), key_new, value_new, key_cache[layer], value_cache[layer], slot_pos, start_pos)
            part_sum = jnp.einsum('bcn,nm->bcm', mixed.reshape(num_seqs, chunk, -1), w_o[layer], preferred_element_type=jnp.float32).astype(jnp.bfloat16)
            summed = lax.psum_scatter(part_sum, 'tp', scatter_dimension=1, tiled=True)
            middle = (hidden.astype(jnp.float32) + summed.astype(jnp.float32) + b_o[layer].astype(jnp.float32)).astype(jnp.bfloat16)
            normed = layer_norm(middle, norm_params[layer, 2], norm_params[layer, 3])
            gathered = lax.all_gather(normed, 'tp', axis=1, tiled=True)
            active = jax.nn.gelu(project(gathered, w_up[layer], b_up[layer]), approximate=True).astype(jnp.bfloat16)
            part_sum = jnp.einsum('bcf,fm->bcm', active, w_down[layer], preferred_element_type=jnp.float32).astype(jnp.bfloat16)
            summed = lax.psum_scatter(part_sum, 'tp', scatter_dimension=1, tiled=True)
            hidden = (middle.astype(jnp.float32) + summed.astype(jnp.float32) + b_down[layer].astype(jnp.float32)).astype(jnp.bfloat16)
            fresh_keys.append(key_new)
            fresh_values.append(value_new)
        first_slot = start_pos % key_cache.shape[2]
        write_all = jax.vmap(jax.vmap(write_chunk), in_axes=(0, 0, None))
        key_out = write_all(key_cache, jnp.stack(fresh_keys), first_slot)
        value_out = write_all(value_cache, jnp.stack(fresh_values), first_slot)
        positions = start_pos[:, None] + jnp.arange(chunk)[None, :]
        pos_out = jax.vmap(write_chunk)(slot_pos, positions, first_slot)
        return hidden, key_out, value_out, pos_out

    return jax.shard_map(device_step, mesh=mesh, in_specs=in_specs, out_specs=out_specs, check_vma=False)
```

profile of v0, /device:TPU:0, one launch (start us, length us, event | category | flops | bytes accessed | tf_op | source)
XLA Modules:
  0.0 2083.9 jit_solution(17400838072629671390)
XLA Ops:
  25.3 15.7 compare_and_fusion
  40.9 98.4 %all-gather.5.cloned.1.call-done = bf16[3,1024,4096]{2,1,0:T(8,128)(2,1)} async-done(((bf16[3,128,4096]{2,1,0:T(8,128)(2,1)}), bf16[3,1024,4096]{2,1,0:T(8,128)(2,1)}) %all-gather.5.cloned.1.call-update) | async-done | bytes 25165840 | tf_op jit(solution)/shard_map/all_gather | solution.py:79
  139.3 19.5 broadcast_add_fusion.1
  165.5 14.4 fusion.140
  199.8 18.9 fusion.18
  218.7 75.6 %fusion.4 = (f32[3,4,1024]{2,1,0:T(4,128)S(1)}, f32[3,1024,4,4096]{3,1,2,0:T(8,128)}) fusion(pred[3,1024,4096]{2,1,0:T(8,128)(4,1)} %compare_and_fusion, bf16[3,1024,4,128]{3,1,2,0:T(8,128)(2,1)} %copy-done.21, bf16[2,3,4096,1,128]{4,2,1,3,0:T(8,128)(2,1)} %bitcast.372), kind=kOutput, calls=%fused_computation.14 | convolution fusion | flops 13035884544 | bytes 220250112 | tf_op jit(solution)/shard_map/bckgd,bwkd->bkgcw/dot_general | solution.py:41
  294.4 21.6 %fusion.14 = f32[3,4,1024]{2,1,0:T(4,128)} fusion(f32[3,1024,1024,4]{2,1,3,0:T(8,128)} %get-tuple-element.118, f32[3,4,1024]{2,1,0:T(4,128)S(1)} %max.16, pred[1024,1024]{0,1:T(8,128)(4,1)S(1)} %copy-done.16), kind=kLoop, calls=%fused_computation.27 | loop fusion | flops 50319360 | bytes 51478528 | tf_op jit(solution)/shard_map/reduce_sum | solution.py:52
  316.0 65.4 %fusion = f32[3,4,1024]{2,1,0:T(4,128)S(1)} fusion(f32[3,1024,4,4096]{3,1,2,0:T(8,128)} %get-tuple-element.116, f32[3,4,1024]{2,1,0:T(4,128)S(1)} %max.16, pred[3,1024,4096]{2,1,0:T(8,128)(4,1)} %compare_and_fusion), kind=kLoop, calls=%fused_computation.10 | loop fusion | flops 201314304 | bytes 214007808 | tf_op jit(solution)/shard_map/reduce_sum | solution.py:52
  381.4 71.0 %fusion.8 = f32[3,4,1024,128]{2,3,1,0:T(8,128)} fusion(f32[3,1024,4,4096]{3,1,2,0:T(8,128)} %get-tuple-element.116, f32[3,4,1024]{2,1,0:T(4,128)S(1)} %max.16, pred[3,1024,4096]{2,1,0:T(8,128)(4,1)} %compare_and_fusion, bf16[2,3,4096,1,128]{4,2,3,1,0:T(8,128)(2,1)} %param.27), kind=kOutput, calls=%fused_computation.18 | convolution fusion | flops 13086228480 | bytes 223395840 | tf_op jit(solution)/shard_map/bkgcw,bwkd->bckgd/dot_general | solution.py:53
  464.4 22.5 %fusion.109 = bf16[3,1024,1,4,128]{1,4,3,0,2:T(8,128)(2,1)} fusion(f32[3,4,1024,128]{2,3,1,0:T(8,128)S(1)} %copy-done.64, f32[3,1024,4]{1,2,0:T(4,128)S(1)} %add_bitcast_fusion.3, f32[3,1024,1024,4]{2,1,3,0:T(8,128)} %get-tuple-element.118, f32[3,4,1024]{2,1,0:T(4,128)S(1)} %max.16, pred[1024,1024]{0,1:T(8,128)(4,1)S(1)} %copy-done.17, ...), kind=kOutput, calls=%fused_computation.138 | convolution fusion | flops 3276275712 | bytes 61702144 | tf_op jit(solution)/shard_map/bkgcj,bjkd->bckgd/dot_general | solution.py:54
  486.9 20.7 convolution_convert_fusion.1
  508.9 145.3 %reduce-scatter.5.cloned.1.call-done = bf16[3,128,4096]{2,1,0:T(8,128)(2,1)} async-done(((bf16[3,1024,4096]{2,1,0:T(8,128)(2,1)}), bf16[3,128,4096]{2,1,0:T(8,128)(2,1)}) %reduce-scatter.5.cloned.1.call-update) | async-done | bytes 3145744 | tf_op jit(solution)/shard_map/reduce_scatter | solution.py:85
  663.8 118.7 %all-gather.7.cloned.1.call-done = bf16[3,1024,4096]{2,1,0:T(8,128)(2,1)} async-done(((bf16[3,128,4096]{2,1,0:T(8,128)(2,1)}), bf16[3,1024,4096]{2,1,0:T(8,128)(2,1)}) %all-gather.7.cloned.1.call-update) | async-done | bytes 25165840 | tf_op jit(solution)/shard_map/all_gather | solution.py:88
  782.5 57.6 %fusion.35 = bf16[3,1024,1792]{2,1,0:T(8,128)(2,1)} fusion(bf16[3,1024,4096]{2,1,0:T(8,128)(2,1)} %all-gather.7.cloned.1.call-done, bf16[2,4096,1792]{2,1,0:T(8,128)(2,1)} %param.38, f32[1792]{0:T(1024)S(1)} %get-tuple-element.46), kind=kOutput, calls=%fused_computation.48 | convolution fusion | flops 45152206848 | bytes 50863104 | tf_op jit(solution)/shard_map/bcm,mn->bcn/dot_general | solution.py:34
  840.1 53.6 %fusion.60 = bf16[3,1024,4096]{2,1,0:T(8,128)(2,1)} fusion(bf16[3,1024,1792]{2,1,0:T(8,128)(2,1)} %fusion.35, bf16[2,1792,4096]{2,1,0:T(8,128)(2,1)} %param.40), kind=kOutput, calls=%fused_computation.71 | convolution fusion | flops 45109739520 | bytes 50855936 | tf_op jit(solution)/shard_map/bcf,fm->bcm/dot_general | solution.py:90
  895.1 145.3 %reduce-scatter.7.cloned.1.call-done = bf16[3,128,4096]{2,1,0:T(8,128)(2,1)} async-done(((bf16[3,1024,4096]{2,1,0:T(8,128)(2,1)}), bf16[3,128,4096]{2,1,0:T(8,128)(2,1)}) %reduce-scatter.7.cloned.1.call-update) | async-done | bytes 3145744 | tf_op jit(solution)/shard_map/reduce_scatter | solution.py:91
  1048.8 119.8 %all-gather.9.cloned.1.call-done = bf16[3,1024,4096]{2,1,0:T(8,128)(2,1)} async-done(((bf16[3,128,4096]{2,1,0:T(8,128)(2,1)}), bf16[3,1024,4096]{2,1,0:T(8,128)(2,1)}) %all-gather.9.cloned.1.call-update) | async-done | bytes 25165840 | tf_op jit(solution)/shard_map/all_gather | solution.py:79
  1168.6 19.5 broadcast_add_fusion
  1228.2 76.0 %fusion.5 = (f32[3,4,1024]{2,1,0:T(4,128)S(1)}, f32[3,1024,4,4096]{3,1,2,0:T(8,128)}) fusion(pred[3,1024,4096]{2,1,0:T(8,128)(4,1)} %compare_and_fusion, bf16[3,1024,4,128]{3,1,2,0:T(8,128)(2,1)} %fusion.107, bf16[2,3,4096,1,128]{4,2,1,3,0:T(8,128)(2,1)} %bitcast.373), kind=kOutput, calls=%fused_computation.15 | convolution fusion | flops 13035884544 | bytes 220250112 | tf_op jit(solution)/shard_map/bckgd,bwkd->bkgcw/dot_general | solution.py:41
  1307.4 18.9 fusion.19
  1326.4 65.0 %fusion.2 = f32[3,4,1024]{2,1,0:T(4,128)S(1)} fusion(f32[3,1024,4,4096]{3,1,2,0:T(8,128)} %get-tuple-element.120, f32[3,4,1024]{2,1,0:T(4,128)S(1)} %max.17, pred[3,1024,4096]{2,1,0:T(8,128)(4,1)} %compare_and_fusion), kind=kLoop, calls=%fused_computation.12 | loop fusion | flops 201314304 | bytes 214007808 | tf_op jit(solution)/shard_map/reduce_sum | solution.py:52
  1391.4 71.5 %fusion.10 = f32[3,4,1024,128]{2,3,1,0:T(8,128)} fusion(f32[3,1024,4,4096]{3,1,2,0:T(8,128)} %get-tuple-element.120, f32[3,4,1024]{2,1,0:T(4,128)S(1)} %max.17, pred[3,1024,4096]{2,1,0:T(8,128)(4,1)} %compare_and_fusion, bf16[2,3,4096,1,128]{4,2,3,1,0:T(8,128)(2,1)} %param.27), kind=kOutput, calls=%fused_computation.19 | convolution fusion | flops 13086228480 | bytes 223395840 | tf_op jit(solution)/shard_map/bkgcw,bwkd->bckgd/dot_general | solution.py:53
  1462.8 21.1 %fusion.16 = f32[3,4,1024]{2,1,0:T(4,128)S(1)} fusion(f32[3,1024,1024,4]{2,1,3,0:T(8,128)} %get-tuple-element.122, f32[3,4,1024]{2,1,0:T(4,128)S(1)} %max.17, pred[1024,1024]{0,1:T(8,128)(4,1)S(1)} %copy-done.19), kind=kLoop, calls=%fused_computation.29 | loop fusion | flops 50319360 | bytes 51478528 | tf_op jit(solution)/shard_map/reduce_sum | solution.py:52
  1495.9 22.6 %fusion.108 = bf16[3,1024,1,4,128]{1,4,3,0,2:T(8,128)(2,1)} fusion(f32[3,4,1024,128]{2,3,1,0:T(8,128)S(1)} %copy-done.63, f32[3,1024,4]{1,2,0:T(4,128)S(1)} %add_bitcast_fusion.2, f32[3,1024,1024,4]{2,1,3,0:T(8,128)} %get-tuple-element.122, f32[3,4,1024]{2,1,0:T(4,128)S(1)} %max.17, pred[1024,1024]{0,1:T(8,128)(4,1)S(1)} %copy-done.19, ...), kind=kOutput, calls=%fused_computation.136 | convolution fusion | flops 3276275712 | bytes 61702144 | tf_op jit(solution)/shard_map/bkgcj,bjkd->bckgd/dot_general | solution.py:54
  1518.4 20.7 convolution_convert_fusion
  1539.2 146.6 %reduce-scatter.9.cloned.1.call-done = bf16[3,128,4096]{2,1,0:T(8,128)(2,1)} async-done(((bf16[3,1024,4096]{2,1,0:T(8,128)(2,1)}), bf16[3,128,4096]{2,1,0:T(8,128)(2,1)}) %reduce-scatter.9.cloned.1.call-update) | async-done | bytes 3145744 | tf_op jit(solution)/shard_map/reduce_scatter | solution.py:85
  1694.5 119.5 %all-gather.11.cloned.1.call-done = bf16[3,1024,4096]{2,1,0:T(8,128)(2,1)} async-done(((bf16[3,128,4096]{2,1,0:T(8,128)(2,1)}), bf16[3,1024,4096]{2,1,0:T(8,128)(2,1)}) %all-gather.11.cloned.1.call-update) | async-done | bytes 25165840 | tf_op jit(solution)/shard_map/all_gather | solution.py:88
  1814.0 57.5 %fusion.43 = bf16[3,1024,1792]{2,1,0:T(8,128)(2,1)} fusion(bf16[3,1024,4096]{2,1,0:T(8,128)(2,1)} %all-gather.11.cloned.1.call-done, bf16[2,4096,1792]{2,1,0:T(8,128)(2,1)} %param.38, f32[1792]{0:T(1024)S(1)} %copy-done.52), kind=kOutput, calls=%fused_computation.56 | convolution fusion | flops 45152206848 | bytes 50863104 | tf_op jit(solution)/shard_map/bcm,mn->bcn/dot_general | solution.py:34
  1871.6 53.6 %fusion.63 = bf16[3,1024,4096]{2,1,0:T(8,128)(2,1)} fusion(bf16[3,1024,1792]{2,1,0:T(8,128)(2,1)} %fusion.43, bf16[2,1792,4096]{2,1,0:T(8,128)(2,1)} %param.40), kind=kOutput, calls=%fused_computation.72 | convolution fusion | flops 45109739520 | bytes 50855936 | tf_op jit(solution)/shard_map/bcf,fm->bcm/dot_general | solution.py:90
  1948.9 15.8 while.10
  1968.2 30.4 %while.9 = (s32[]{:T(128)}, bf16[2,3,8192,1,128]{2,4,1,3,0:T(8,128)(2,1)}, s32[3,4]{1,0:T(4,128)S(1)}, bf16[3,2,4096,1,128]{4,2,3,0,1:T(8,128)(2,1)}) while((s32[]{:T(128)}, bf16[2,3,8192,1,128]{2,4,1,3,0:T(8,128)(2,1)}, s32[3,4]{1,0:T(4,128)S(1)}, bf16[3,2,4096,1,128]{4,2,3,0,1:T(8,128)(2,1)}) %tuple.123), condition=%wide.while_cond.clone.1, body=%wide.while_body.sunk.clone | while | flops 2 | bytes 12583037 | solution.py:27
  2012.2 59.7 %reduce-scatter.11.cloned.1.call-done = bf16[3,128,4096]{2,1,0:T(8,128)(2,1)} async-done(((bf16[3,1024,4096]{2,1,0:T(8,128)(2,1)}), bf16[3,128,4096]{2,1,0:T(8,128)(2,1)}) %reduce-scatter.11.cloned.1.call-update) | async-done | bytes 3145744 | tf_op jit(solution)/shard_map/reduce_scatter | solution.py:91
  (253 shorter events, 238.7 us)
Async XLA Ops:
  7.2 132.1 %all-gather.5.cloned.1.call-start = ((), (), s32[]{:S(2)}) async-start(), calls=%async_computation.4 | async-start | bytes 28311552 | tf_op jit(solution)/shard_map/all_gather | solution.py:79
  16.7 637.6 %reduce-scatter.5.cloned.1.call-start = ((), (), s32[]{:S(2)}) async-start(), calls=%async_computation.5 | async-start | bytes 28311552 | tf_op jit(solution)/shard_map/reduce_scatter | solution.py:85
  197.7 21.0 %copy-start.21 = (bf16[3,1024,4,128]{3,1,2,0:T(8,128)(2,1)}, bf16[3,1024,4,128]{3,1,2,0:T(8,128)(2,1)S(1)}, u32[]{:S(2)}) copy-start(bf16[3,1024,4,128]{3,1,2,0:T(8,128)(2,1)S(1)} %fusion.105) | copy-start | bytes 9437188
  199.8 18.9 copy-start.24
  381.4 71.0 %copy-start.37 = (f32[3,4,1024]{2,1,0:T(4,128)S(1)}, f32[3,4,1024]{2,1,0:T(4,128)}, u32[]{:S(2)}) copy-start(f32[3,4,1024]{2,1,0:T(4,128)} %fusion.14) | copy-start | bytes 147460
  381.4 71.0 %copy-start.60 = (f32[128]{0:T(128)S(1)}, f32[128]{0:T(128)}, u32[]{:S(2)}) copy-start(f32[128]{0:T(128)} %get-tuple-element.110) | copy-start | bytes 1540
  381.4 71.0 %copy-start.61 = (bf16[2,4096,128]{2,1,0:T(8,128)(2,1)S(1)}, bf16[2,4096,128]{2,1,0:T(8,128)(2,1)}, u32[]{:S(2)}) copy-start(bf16[2,4096,128]{2,1,0:T(8,128)(2,1)} %param.34) | copy-start | bytes 6291460
  452.5 11.9 copy-start.17
  452.5 11.9 copy-start.64
  464.4 22.5 %copy-start.30 = (bf16[3,1024,128]{2,1,0:T(8,128)(2,1)}, bf16[3,1024,128]{2,1,0:T(8,128)(2,1)S(1)}, u32[]{:S(2)}) copy-start(bf16[3,1024,128]{2,1,0:T(8,128)(2,1)S(1)} %add_convert_fusion.1) | copy-start | bytes 2359300
  507.6 146.7 %copy-start.3 = (bf16[3,128,4096]{2,1,0:T(8,128)(2,1)S(1)}, bf16[3,128,4096]{2,1,0:T(8,128)(2,1)}, u32[]{:S(2)}) copy-start(bf16[3,128,4096]{2,1,0:T(8,128)(2,1)} %param.22) | copy-start | bytes 9437188
  507.6 274.9 %all-gather.7.cloned.1.call-start = ((), (), s32[]{:S(2)}) async-start(), calls=%async_computation.6 | async-start | bytes 28311552 | tf_op jit(solution)/shard_map/all_gather | solution.py:88
  662.7 377.8 %reduce-scatter.7.cloned.1.call-start = ((), (), s32[]{:S(2)}) async-start(), calls=%async_computation.7 | async-start | bytes 28311552 | tf_op jit(solution)/shard_map/reduce_scatter | solution.py:91
  893.7 146.7 %copy-start.9 = (bf16[3,128,4096]{2,1,0:T(8,128)(2,1)S(1)}, bf16[3,128,4096]{2,1,0:T(8,128)(2,1)}, u32[]{:S(2)}) copy-start(bf16[3,128,4096]{2,1,0:T(8,128)(2,1)} %copy-done.8) | copy-start | bytes 9437188
  893.8 274.8 %all-gather.9.cloned.1.call-start = ((), (), s32[]{:S(2)}) async-start(), calls=%async_computation.8 | async-start | bytes 28311552 | tf_op jit(solution)/shard_map/all_gather | solution.py:79
  1043.8 124.8 %copy-start.56 = (f32[1,512]{1,0:T(1,128)S(1)}, f32[1,512]{1,0:T(1,128)}, u32[]{:S(2)}) copy-start(f32[1,512]{1,0:T(1,128)} %get-tuple-element.108) | copy-start | bytes 6148
  1048.8 637.0 %reduce-scatter.9.cloned.1.call-start = ((), (), s32[]{:S(2)}) async-start(), calls=%async_computation.9 | async-start | bytes 28311552 | tf_op jit(solution)/shard_map/reduce_scatter | solution.py:85
  1194.8 14.4 copy-start.53
  1228.2 76.0 %copy-start.12 = (f32[3,1024,128]{1,2,0:T(8,128)S(1)}, f32[3,1024,128]{1,2,0:T(8,128)}, u32[]{:S(2)}) copy-start(f32[3,1024,128]{1,2,0:T(8,128)} %copy.62) | copy-start | bytes 4718596
  1228.2 76.0 %copy-start.14 = (f32[3,1024,128]{1,2,0:T(8,128)S(1)}, f32[3,1024,128]{1,2,0:T(8,128)}, u32[]{:S(2)}) copy-start(f32[3,1024,128]{1,2,0:T(8,128)} %copy.63) | copy-start | bytes 4718596
  1307.4 19.0 copy-start.26
  1391.4 71.5 %copy-start.19 = (pred[1024,1024]{0,1:T(8,128)(4,1)S(1)}, pred[1024,1024]{0,1:T(8,128)(4,1)}, u32[]{:S(2)}) copy-start(pred[1024,1024]{0,1:T(8,128)(4,1)} %iota_compare_fusion.2) | copy-start | bytes 3145732
  1462.8 21.1 %copy-start.59 = (f32[128]{0:T(128)S(1)}, f32[128]{0:T(128)}, u32[]{:S(2)}) copy-start(f32[128]{0:T(128)} %get-tuple-element.109) | copy-start | bytes 1540
  1462.8 21.1 %copy-start.62 = (bf16[2,4096,128]{2,1,0:T(8,128)(2,1)S(1)}, bf16[2,4096,128]{2,1,0:T(8,128)(2,1)}, u32[]{:S(2)}) copy-start(bf16[2,4096,128]{2,1,0:T(8,128)(2,1)} %param.34) | copy-start | bytes 6291460
  1495.9 22.6 %copy-start.32 = (bf16[3,1024,128]{2,1,0:T(8,128)(2,1)}, bf16[3,1024,128]{2,1,0:T(8,128)(2,1)S(1)}, u32[]{:S(2)}) copy-start(bf16[3,1024,128]{2,1,0:T(8,128)(2,1)S(1)} %add_convert_fusion) | copy-start | bytes 2359300
  1539.1 146.7 %copy-start.7 = (bf16[3,128,4096]{2,1,0:T(8,128)(2,1)S(1)}, bf16[3,128,4096]{2,1,0:T(8,128)(2,1)}, u32[]{:S(2)}) copy-start(bf16[3,128,4096]{2,1,0:T(8,128)(2,1)} %copy-done.6) | copy-start | bytes 9437188
  1539.1 146.7 %copy-start.49 = (f32[1,4096]{1,0:T(1,128)S(1)}, f32[1,4096]{1,0:T(1,128)}, u32[]{:S(2)}) copy-start(f32[1,4096]{1,0:T(1,128)} %get-tuple-element.106) | copy-start | bytes 49156
  1539.2 274.9 %all-gather.11.cloned.1.call-start = ((), (), s32[]{:S(2)}) async-start(), calls=%async_computation.10 | async-start | bytes 28311552 | tf_op jit(solution)/shard_map/all_gather | solution.py:88
  1689.2 124.8 %copy-start.52 = (f32[1792]{0:T(1024)S(1)}, f32[1792]{0:T(1024)}, u32[]{:S(2)}) copy-start(f32[1792]{0:T(1024)} %get-tuple-element.45) | copy-start | bytes 21508
  1694.2 377.6 %reduce-scatter.11.cloned.1.call-start = ((), (), s32[]{:S(2)}) async-start(), calls=%async_computation.11 | async-start | bytes 28311552 | tf_op jit(solution)/shard_map/reduce_scatter | solution.py:91
  1998.6 73.3 %copy-start.5 = (bf16[3,128,4096]{2,1,0:T(8,128)(2,1)S(1)}, bf16[3,128,4096]{2,1,0:T(8,128)(2,1)}, u32[]{:S(2)}) copy-start(bf16[3,128,4096]{2,1,0:T(8,128)(2,1)} %copy-done.4) | copy-start | bytes 9437188
  1998.6 73.3 %copy-start.46 = (f32[1,4096]{1,0:T(1,128)S(1)}, f32[1,4096]{1,0:T(1,128)}, u32[]{:S(2)}) copy-start(f32[1,4096]{1,0:T(1,128)} %get-tuple-element.103) | copy-start | bytes 49156
  (41 other events, 214.4 us)
Sparse Core Ops, SparseCore 0:
  16.8 122.4 all-gather.4
  507.7 146.4 reduce-scatter.4
  662.8 119.6 all-gather.6
  893.9 146.4 reduce-scatter.6
  1048.9 119.6 all-gather.8
  1539.3 146.4 reduce-scatter.8
  1694.4 119.6 all-gather.10
  1925.4 146.4 reduce-scatter.10
where the time goes:
time: 2090 us; the launch traced here: 2080 us
  waiting for transfers between devices  953 us (46%)
  matrix products  732 us (35%)
  other arithmetic  296 us (14%)
  local copies, waits for them, and re-layouts  85.3 us (4%)
    reduce_scatter x4, waiting for transfers between devices, device_step(): summed = lax.psum_scatter(part_sum, 'tp', scatter_dimension=1, tiled=True)  497 us
    all_gather x4, waiting for transfers between devices, device_step(): gathered = lax.all_gather(normed, 'tp', axis=1, tiled=True)  456 us
    dot_general x8, matrix products, project(): jnp.einsum('bcm,mn->bcn', acts, weight, preferred_element_type=jnp.float32)  207 us
    reduce_sum x4, other arithmetic, local_attention(): total = jnp.sum(exp_old, axis=-1) + jnp.sum(exp_new, axis=-1)  173 us
    dot_general x2, matrix products, local_attention(): jnp.einsum('bckgd,bwkd->bkgcw', query, key_old, preferred_element_type=jn...  152 us
    dot_general x2, matrix products, local_attention(): jnp.einsum('bkgcw,bwkd->bckgd', exp_old.astype(jnp.bfloat16), value_old,...  142 us
    dot_general x2, matrix products, device_step(): jnp.einsum('bcf,fm->bcm', active, w_down[layer], preferred_element_type=j...  107 us
    another operation x28, local copies, waits for them, and re-layouts, write_chunk(): jnp.roll(jnp.concatenate([fresh, filler], axis=0), first_slot, axis=0)  53.3 us
  transfers between devices with their start and end apart: 8, of which 8 were waited for; matrix products, arithmetic and copies ran while one was open for 5% of the time, Pallas kernels for 0%

commit v1 on v0

v1 whole, which is shorter than its diff:
```python
import functools

import jax
import jax.numpy as jnp
from jax import lax
from jax.experimental import pallas as pl
from jax.experimental.pallas import tpu as pltpu
from jax.sharding import PartitionSpec as P


NORM_EPS = 1e-5
LOG2E = 1.4426950408889634
HIDE = -(1 << 30)
TURNS = [int(c) for c in '012010120201120210120021120210120101220210120210122']


def norm_kernel(*refs, joined):
    if joined:
        base_ref, pair_ref, came_ref, last_ref, bias_ref, gain_ref, shift_ref, sum_ref, norm_ref = refs
        summed = pair_ref[...].astype(jnp.float32) + came_ref[...].astype(jnp.float32) + last_ref[...].astype(jnp.float32)
        kept = (base_ref[...].astype(jnp.float32) + summed + bias_ref[...].astype(jnp.float32)).astype(jnp.bfloat16)
        sum_ref[...] = kept
    else:
        base_ref, gain_ref, shift_ref, norm_ref = refs
        kept = base_ref[...]
    values = kept.astype(jnp.float32)
    centered = values - jnp.mean(values, axis=-1, keepdims=True)
    variance = jnp.mean(centered * centered, axis=-1, keepdims=True)
    scaled = centered * lax.rsqrt(variance + NORM_EPS)
    norm_ref[...] = (scaled * gain_ref[...].astype(jnp.float32) + shift_ref[...].astype(jnp.float32)).astype(jnp.bfloat16)


def normalize(base, seq, terms, bias, norms, layer, which, rows=32):
    part, model = base.shape[-2:]
    line = pl.BlockSpec((rows, model), lambda i: (i, 0))
    first = line if base.ndim == 2 else pl.BlockSpec((None, rows, model), lambda i: (seq, i, 0))
    vector = lambda at: pl.BlockSpec((None, 1, model), lambda i: (at, 0, 0))
    scale_specs = [vector(4 * layer + which), vector(4 * layer + which + 1)]
    scales = [norms, norms]
    whole = jax.ShapeDtypeStruct((part, model), jnp.bfloat16)
    if terms is None:
        specs, args, outs = [first], [base], [whole]
    else:
        bias, bias_at = bias
        specs, args, outs = [first, line, line, line, vector(bias_at)], [base, *terms, bias], [whole, whole]
    return pl.pallas_call(
        functools.partial(norm_kernel, joined=terms is not None),
        grid=(part // rows,),
        in_specs=specs + scale_specs,
        out_specs=[line] * len(outs),
        out_shape=outs,
        compiler_params=pltpu.CompilerParams(dimension_semantics=('arbitrary',), vmem_limit_bytes=16 << 20),
        cost_estimate=pl.CostEstimate(flops=8 * part * model, bytes_accessed=2 * (len(args) + len(outs)) * part * model, transcendentals=0),
        name='norm',
    )(*args, *scales)


def qkv_kernel(x_ref, cos_ref, sin_ref, wq_ref, wk_ref, wv_ref, bq_ref, bk_ref, bv_ref, q_ref, k_ref, v_ref):
    head_dim = cos_ref.shape[-1]
    acts = x_ref[...]
    cos_b = cos_ref[...]
    lane = lax.broadcasted_iota(jnp.int32, cos_b.shape, 1)
    sin_b = jnp.where(lane < head_dim // 2, -sin_ref[...], sin_ref[...])

    def rotary(values):
        return (values * cos_b + pltpu.roll(values, head_dim // 2, 1) * sin_b).astype(jnp.bfloat16)

    query = jnp.dot(acts, wq_ref[...], preferred_element_type=jnp.float32) + bq_ref[...].astype(jnp.float32)
    for head in range(query.shape[1] // head_dim):
        cols = slice(head * head_dim, (head + 1) * head_dim)
        q_ref[:, cols] = rotary(query[:, cols])
    weight_kv = jnp.concatenate([wk_ref[...], wv_ref[...]], axis=1)
    key_value = jnp.dot(acts, weight_kv, preferred_element_type=jnp.float32)
    k_ref[...] = rotary(key_value[:, :head_dim] + bk_ref[...].astype(jnp.float32))
    v_ref[...] = (key_value[:, head_dim:] + bv_ref[...].astype(jnp.float32)).astype(jnp.bfloat16)


def qkv_project(acts, cos_tab, sin_tab, w_q, w_k, w_v, b_q, b_k, b_v, layer, seq, rows=256):
    chunk, model = acts.shape
    head_dim = cos_tab.shape[-1]
    q_cols = w_q.shape[2]
    kv_cols = w_k.shape[2]
    row_block = lambda cols: pl.BlockSpec((rows, cols), lambda i: (i, 0))
    table = pl.BlockSpec((None, rows, head_dim), lambda i: (seq, i, 0))
    weight = lambda cols: pl.BlockSpec((None, model, cols), lambda i: (layer, 0, 0))
    bias = lambda cols: pl.BlockSpec((None, 1, cols), lambda i: (layer, 0, 0))
    return pl.pallas_call(
        qkv_kernel,
        grid=(chunk // rows,),
        in_specs=[row_block(model), table, table, weight(q_cols), weight(kv_cols), weight(kv_cols), bias(q_cols), bias(kv_cols), bias(kv_cols)],
        out_specs=[row_block(q_cols), row_block(kv_cols), row_block(kv_cols)],
        out_shape=[jax.ShapeDtypeStruct((chunk, cols), jnp.bfloat16) for cols in (q_cols, kv_cols, kv_cols)],
        compiler_params=pltpu.CompilerParams(dimension_semantics=('arbitrary',), vmem_limit_bytes=40 << 20),
        cost_estimate=pl.CostEstimate(flops=2 * chunk * model * (q_cols + 2 * kv_cols), bytes_accessed=2 * (chunk + q_cols + 2 * kv_cols) * model, transcendentals=0),
        name='qkv_rotary',
    )(acts, cos_tab, sin_tab, w_q, w_k, w_v, b_q[:, None, :], b_k[:, None, :], b_v[:, None, :])


def attention_kernel(place_ref, start_ref, q_ref, kn_ref, vn_ref, ko_ref, vo_ref, held_ref, o_ref, score_ref, *, seq, group, key_block):
    rows = q_ref.shape[0]
    head_dim = kn_ref.shape[1]
    window = ko_ref.shape[0]
    block = pl.program_id(0)
    start = start_ref[seq]
    scale = head_dim ** -0.5 * LOG2E
    query = jnp.concatenate([q_ref[:, g * head_dim:(g + 1) * head_dim] for g in range(group)], axis=0)
    token = block * rows + lax.broadcasted_iota(jnp.int32, (rows, 1), 0)
    token = jnp.concatenate([token] * group, axis=0)
    oldest = start + token - window
    top_shape = (rows * group, 128)

    def lane_max(values, top):
        for i in range(values.shape[1] // 128):
            top = jnp.maximum(top, values[:, i * 128:(i + 1) * 128])
        return top

    def lane_sum(values, total):
        for i in range(values.shape[1] // 128):
            total = total + values[:, i * 128:(i + 1) * 128]
        return total

    contract = (((1,), (1,)), ((), ()))

    def score_old(step, top):
        at = pl.multiple_of(step * key_block, key_block)
        values = lax.dot_general(query, ko_ref[pl.ds(at, key_block), :], contract, preferred_element_type=jnp.float32)
        held = held_ref[:, pl.ds(at, key_block)]
        held = jnp.where((held >= 0) & (held < start), held, HIDE)
        values = jnp.where(held > oldest, values, -jnp.inf)
        score_ref[:, pl.ds(at, key_block)] = values
        return lane_max(values, top)

    def score_new(step, top):
        at = pl.multiple_of(step * key_block, key_block)
        values = lax.dot_general(query, kn_ref[pl.ds(at, key_block), :], contract, preferred_element_type=jnp.float32)
        fresh = at + lax.broadcasted_iota(jnp.int32, (1, key_block), 1)
        values = jnp.where(fresh <= token, values, -jnp.inf)
        score_ref[:, pl.ds(pl.multiple_of(window + at, key_block), key_block)] = values
        return lane_max(values, top)

    new_steps = (block * rows + rows + key_block - 1) // key_block
    top = jnp.full(top_shape, -jnp.inf, jnp.float32)
    top = lax.fori_loop(0, window // key_block, score_old, top)
    top = lax.fori_loop(0, new_steps, score_new, top)
    top = jnp.max(top, axis=1, keepdims=True)

    def weigh(at, value_ref, value_at, carry):
        total, mixed = carry
        weights = jnp.exp2((score_ref[:, pl.ds(at, key_block)] - top) * scale)
        total = lane_sum(weights, total)
        mixed = mixed + jnp.dot(weights.astype(jnp.bfloat16), value_ref[pl.ds(value_at, key_block), :], preferred_element_type=jnp.float32)
        return total, mixed

    def mix_old(step, carry):
        at = pl.multiple_of(step * key_block, key_block)
        return weigh(at, vo_ref, at, carry)

    def mix_new(step, carry):
        at = pl.multiple_of(step * key_block, key_block)
        return weigh(pl.multiple_of(window + at, key_block), vn_ref, at, carry)

    carry = (jnp.zeros(top_shape, jnp.float32), jnp.zeros((rows * group, head_dim), jnp.float32))
    carry = lax.fori_loop(0, window // key_block, mix_old, carry)
    total, mixed = lax.fori_loop(0, new_steps, mix_new, carry)
    mixed = (mixed / jnp.sum(total, axis=1, keepdims=True)).astype(jnp.bfloat16)
    for g in range(group):
        o_ref[:, g * head_dim:(g + 1) * head_dim] = mixed[g * rows:(g + 1) * rows]


def attend(query, key_new, value_new, key_cache, value_cache, held, place, start_pos, layer, seq, rows=128, key_block=512):
    chunk, q_cols = query.shape
    window, head_dim = key_cache.shape[2:]
    group = q_cols // head_dim
    keys = window + chunk
    whole = pl.BlockSpec((chunk, head_dim), lambda i, *_: (0, 0))
    cache = pl.BlockSpec((None, None, window, head_dim), lambda i, *_: (layer, seq, 0, 0))
    return pl.pallas_call(
        functools.partial(attention_kernel, seq=seq, group=group, key_block=key_block),
        grid_spec=pltpu.PrefetchScalarGridSpec(
            num_scalar_prefetch=2,
            grid=(chunk // rows,),
            in_specs=[pl.BlockSpec((rows, q_cols), lambda i, *_: (i, 0)), whole, whole, cache, cache, pl.BlockSpec((None, 1, window), lambda i, *_: (seq, 0, 0))],
            out_specs=pl.BlockSpec((rows, q_cols), lambda i, place, start: (place[i], 0)),
            scratch_shapes=[pltpu.VMEM((rows * group, keys), jnp.float32)],
        ),
        out_shape=jax.ShapeDtypeStruct((chunk, q_cols), jnp.bfloat16),
        compiler_params=pltpu.CompilerParams(dimension_semantics=('arbitrary',), vmem_limit_bytes=40 << 20),
        cost_estimate=pl.CostEstimate(flops=8 * chunk * q_cols * keys, bytes_accessed=4 * (window + chunk) * head_dim + 4 * chunk * q_cols, transcendentals=0),
        name='attend',
    )(place, start_pos, query, key_new, value_new, key_cache, value_cache, held)


def cache_kernel(start_ref, ko_ref, vo_ref, kn_ref, vn_ref, kout_ref, vout_ref, ring_ref):
    window, head_dim = ko_ref.shape
    chunk = kn_ref.shape[0]
    pad = 16
    span = chunk + pad
    first = lax.rem(start_ref[pl.program_id(1)], window)
    base = pl.multiple_of((first // pad) * pad, pad)
    inner = first - base
    line = lax.broadcasted_iota(jnp.int32, (span, head_dim), 0)
    for old_ref, new_ref, out_ref in ((ko_ref, kn_ref, kout_ref), (vo_ref, vn_ref, vout_ref)):
        ring_ref[0:window] = old_ref[...]
        ring_ref[window:window + span] = old_ref[0:span]
        fresh = jnp.concatenate([new_ref[...].astype(jnp.float32), jnp.zeros((pad, head_dim), jnp.float32)], axis=0)
        fresh = pltpu.roll(fresh, inner, 0)
        kept = ring_ref[pl.ds(base, span), :].astype(jnp.float32)
        mine = (line >= inner) & (line < inner + chunk)
        ring_ref[pl.ds(base, span), :] = jnp.where(mine, fresh, kept).astype(jnp.bfloat16)
        out_ref[span:window] = ring_ref[span:window]
        wrapped = ring_ref[window:window + span].astype(jnp.float32)
        plain = ring_ref[0:span].astype(jnp.float32)
        out_ref[0:span] = jnp.where(line < first + chunk - window, wrapped, plain).astype(jnp.bfloat16)


def update_caches(start_pos, key_cache, value_cache, key_new, value_new):
    layers, seqs, window, head_dim = key_cache.shape
    chunk = key_new.shape[2]
    old = pl.BlockSpec((None, None, window, head_dim), lambda i, j, *_: (i, j, 0, 0))
    new = pl.BlockSpec((None, None, chunk, head_dim), lambda i, j, *_: (i, j, 0, 0))
    return pl.pallas_call(
        cache_kernel,
        grid_spec=pltpu.PrefetchScalarGridSpec(
            num_scalar_prefetch=1,
            grid=(layers, seqs),
            in_specs=[old, old, new, new],
            out_specs=[old, old],
            scratch_shapes=[pltpu.VMEM((window + chunk + 16, head_dim), jnp.bfloat16)],
        ),
        out_shape=[jax.ShapeDtypeStruct(key_cache.shape, jnp.bfloat16)] * 2,
        compiler_params=pltpu.CompilerParams(dimension_semantics=('arbitrary', 'arbitrary'), vmem_limit_bytes=32 << 20),
        cost_estimate=pl.CostEstimate(flops=1 << 24, bytes_accessed=8 * layers * seqs * window * head_dim, transcendentals=0),
        name='write_caches',
    )(start_pos, key_cache, value_cache, key_new, value_new)


def solution(mesh):
    row_spec = P('dp', 'tp', None)
    cache_spec = P(None, 'dp', None, 'tp', None)
    col_spec = P(None, None, 'tp')
    bias_spec = P(None, 'tp')
    in_specs = (row_spec, P('dp'), P('dp', None, None), P('dp', None, None), cache_spec, cache_spec, P('dp', None), P(), col_spec, bias_spec, col_spec, bias_spec, col_spec, bias_spec, P(None, 'tp', None), P(), col_spec, bias_spec, P(None, 'tp', None), P())
    out_specs = (row_spec, cache_spec, cache_spec, P('dp', None))
    count = mesh.shape['tp']
    first_axis = lambda core: 1 + core
    pairs_core = [(d, d ^ 1) for d in range(count)]
    pairs_first = [(d, ((d // 2) ^ first_axis(d % 2)) * 2 + d % 2) for d in range(count)]
    pairs_second = [(d, ((d // 2) ^ (3 - first_axis(d % 2))) * 2 + d % 2) for d in range(count)]

    def device_step(tokens, start_pos, cos_tab, sin_tab, key_cache, value_cache, slot_pos, norm_params, w_q, b_q, w_k, b_k, w_v, b_v, w_o, b_o, w_up, b_up, w_down, b_down):
        num_seqs, part, model = tokens.shape
        chunk = cos_tab.shape[1]
        head_dim = cos_tab.shape[2]
        layers = key_cache.shape[0]
        window = key_cache.shape[2]
        keys_in = key_cache.reshape(layers, num_seqs, window, head_dim)
        values_in = value_cache.reshape(layers, num_seqs, window, head_dim)
        held = slot_pos[:, None, :]
        me = lax.axis_index('tp')
        chip, core = me // 2, me % 2
        near, far = 1 + core, 2 - core
        mine = [chip ^ flip for flip in (0, far, near, 3)]
        theirs = [chip ^ flip for flip in (0, near, far, 3)]
        order = [c * 2 + core for c in mine] + [c * 2 + 1 - core for c in theirs]
        table = jnp.stack(order).astype(jnp.int32)
        place = jnp.sum(jnp.where(table[None, :] == jnp.arange(count)[:, None], jnp.arange(count)[None, :], 0), axis=1).astype(jnp.int32)
        half = chunk // 2

        norms = norm_params.reshape(-1, 1, model)
        out_bias = b_o[:, None, :]
        down_bias = b_down[:, None, :]
        latest = [None]
        turn = [0]

        def item(compute, *values):
            if latest[0] is not None:
                values = lax.optimization_barrier((*values, latest[0]))[:-1]
            results = compute(*values)
            latest[0] = results[0]
            return results

        def send(value, pairs):
            return lax.ppermute(value, 'tp', pairs)

        def gather(value):
            return lax.all_gather(value, 'tp', axis=0, tiled=True)

        def add_lead(own, lead, weight):
            return ((jnp.dot(own, weight, preferred_element_type=jnp.float32) + lead.astype(jnp.float32)).astype(jnp.bfloat16),)

        def add_came(pair, came):
            return ((pair[part:2 * part].astype(jnp.float32) + came[part:].astype(jnp.float32)).astype(jnp.bfloat16),)

        def scatter_sum(lead, own, weight):
            lead = send(lead, pairs_core)
            yield
            pair, = item(functools.partial(add_lead, weight=weight), own, lead)
            came = send(pair[2 * part:], pairs_first)
            yield
            onward, = item(add_came, pair, came)
            last = send(onward, pairs_second)
            yield
            return pair, came, last

        def attention(gathered, layer, seq):
            query, key_new, value_new = qkv_project(gathered, cos_tab, sin_tab, w_q, w_k, w_v, b_q, b_k, b_v, layer, seq)
            fresh_keys[layer][seq] = key_new
            fresh_values[layer][seq] = value_new
            mixed = attend(query, key_new, value_new, keys_in, values_in, held, place, start_pos, layer, seq)
            lead = jnp.dot(mixed[half:], w_o[layer], preferred_element_type=jnp.float32).astype(jnp.bfloat16)
            return lead, mixed[:half]

        def expand(gathered, layer):
            lifted = jnp.dot(gathered, w_up[layer], preferred_element_type=jnp.float32) + b_up[layer].astype(jnp.float32)
            active = jax.nn.gelu(lifted, approximate=True).astype(jnp.bfloat16)
            pick = lambda indices: jnp.concatenate([lax.dynamic_slice_in_dim(active, index * part, part, 0) for index in indices], axis=0)
            lead = jnp.dot(pick(order[4:]), w_down[layer], preferred_element_type=jnp.float32).astype(jnp.bfloat16)
            return lead, pick(order[:4])

        def finish(middle, pair, came, last):
            summed = pair[:part].astype(jnp.float32) + came[:part].astype(jnp.float32) + last.astype(jnp.float32)
            return ((middle.astype(jnp.float32) + summed + b_down[layers - 1].astype(jnp.float32)).astype(jnp.bfloat16),)

        def join(base, *terms, bias, layer, which):
            middle, normed = normalize(base, seq_of[0], terms, (bias, layer), norms, layer + which // 4, which % 4)
            return normed, middle

        seq_of = [0]
        fresh_keys = [[None] * num_seqs for _ in range(layers)]
        fresh_values = [[None] * num_seqs for _ in range(layers)]
        hidden_out = [None] * num_seqs

        def stream(seq):
            base = tokens
            normed, = item(lambda: normalize(base, seq, None, None, norms, 0, 0))
            for layer in range(layers):
                gathered = gather(normed)
                yield
                lead, own = item(functools.partial(attention, layer=layer, seq=seq), gathered)
                terms = yield from scatter_sum(lead, own, w_o[layer])
                seq_of[0] = seq
                normed, middle = item(lambda *terms: join(base, *terms, bias=out_bias, layer=layer, which=2), *terms)
                gathered = gather(normed)
                yield
                lead, own = item(functools.partial(expand, layer=layer), gathered)
                terms = yield from scatter_sum(lead, own, w_down[layer])
                if layer + 1 < layers:
                    seq_of[0] = seq
                    normed, base = item(lambda *terms: join(middle, *terms, bias=down_bias, layer=layer, which=4), *terms)
                else:
                    hidden_out[seq], = item(finish, middle, *terms)
            yield

        streams = [stream(seq) for seq in range(num_seqs)]
        for step, seq in enumerate(TURNS):
            turn[0] = step
            next(streams[seq])
        fresh_keys = [jnp.stack(k) for k in fresh_keys]
        fresh_values = [jnp.stack(v) for v in fresh_values]
        key_out, value_out = update_caches(start_pos, keys_in, values_in, jnp.stack(fresh_keys), jnp.stack(fresh_values))
        first_slot = start_pos % window
        offset = (jnp.arange(window)[None, :] - first_slot[:, None]) % window
        pos_out = jnp.where(offset < chunk, start_pos[:, None] + offset, slot_pos)
        return jnp.stack(hidden_out), key_out.reshape(key_cache.shape), value_out.reshape(value_cache.shape), pos_out

    return jax.shard_map(device_step, mesh=mesh, in_specs=in_specs, out_specs=out_specs, check_vma=False)
```

time: 2090 us -> 1450 us (0.69)
  waiting for transfers between devices: 953 us -> 480 us
  Pallas kernels: 0 us -> 447 us
  matrix products: 732 us -> 349 us
  other arithmetic: 296 us -> 24.3 us
  starting transfers between devices: 1.12 us -> 30 us
    reduce_scatter x4 -> x0, waiting for transfers between devices: 497 us -> none  [device_step(): summed = lax.psum_scatter(part_sum, 'tp', scatter_dimension=1, tiled=True)]
    pallas_call x0 -> x25, Pallas kernels: none -> 447 us  [the longest x6 335 us: attend(): pl.pallas_call(functools.partial(attention_kernel, seq=seq, group=group,...]
    ppermute x0 -> x36, waiting for transfers between devices: none -> 434 us  [send(): return lax.ppermute(value, 'tp', pairs)]
    all_gather x4 -> x12, waiting for transfers between devices: 456 us -> 46.2 us  [gather(): return lax.all_gather(value, 'tp', axis=0, tiled=True)]
    dot_general x20 -> x30, matrix products: 732 us -> 349 us  [the longest x6 140 us: expand(): jnp.dot(gathered, w_up[layer], preferred_element_type=jnp.float32)]
    reduce_sum x12 -> x1, other arithmetic: 191 us -> 0.12 us  [device_step(): jnp.sum(jnp.where(table[None, :] == jnp.arange(count)[:, None], jnp.arang...]
    unnamed x133 -> x300, local copies, waits for them, and re-layouts: 12.2 us -> 77.5 us
    another operation x28 -> x1, local copies, waits for them, and re-layouts: 53.3 us -> 0.09 us  [device_step(): table = jnp.stack(order).astype(jnp.int32)]
  transfers between devices with their start and end apart: 8 -> 48, of which waited for: 8 -> 19; matrix products, arithmetic and copies ran while one was open for 5% -> 24% of each run, Pallas kernels for 0% -> 26%
where the time goes in v1:
time: 1450 us
  waiting for transfers between devices  480 us (33%)
  Pallas kernels  447 us (31%)
  matrix products  349 us (24%)
  local copies, waits for them, and re-layouts  99.1 us (7%)
  starting transfers between devices  30 us (2%)
  other arithmetic  24.3 us (2%)
  between operations  16.4 us (1%)
    ppermute x36, waiting for transfers between devices, send(): return lax.ppermute(value, 'tp', pairs)  434 us
    pallas_call x6, Pallas kernels, attend(): pl.pallas_call(functools.partial(attention_kernel, seq=seq, group=group,...  335 us
    dot_general x6, matrix products, expand(): jnp.dot(gathered, w_up[layer], preferred_element_type=jnp.float32)  140 us
    dot_general x12, matrix products, add_lead(): jnp.dot(own, weight, preferred_element_type=jnp.float32)  112 us
    unnamed x300, local copies, waits for them, and re-layouts  77.5 us
    dot_general x6, matrix products, expand(): jnp.dot(pick(order[4:]), w_down[layer], preferred_element_type=jnp.float32)  74.4 us
    pallas_call x6, Pallas kernels, qkv_project(): pl.pallas_call(qkv_kernel, grid=(chunk // rows,), in_specs=[row_block(mod...  65.6 us
    all_gather x12, waiting for transfers between devices, gather(): return lax.all_gather(value, 'tp', axis=0, tiled=True)  46.2 us
  transfers between devices with their start and end apart: 48, of which 19 were waited for; matrix products, arithmetic and copies ran while one was open for 24% of the time, Pallas kernels for 26%

profile of v1, /device:TPU:0, one launch (start us, length us, event | category | flops | bytes accessed | tf_op | source)
XLA Modules:
  0.0 1446.2 jit_solution(13558546642457442062)
XLA Ops:
  18.1 46.2 %all-gather.13.cloned.1.call-done.x_ref = bf16[1024,4096]{1,0:T(8,128)(2,1)} async-done(((bf16[128,4096]{1,0:T(8,128)(2,1)}), bf16[1024,4096]{1,0:T(8,128)(2,1)}) %all-gather.13.cloned.1.call-update) | async-done | bytes 8388624 | tf_op jit(solution)/shard_map/all_gather | solution.py:286
  81.6 55.6 %attend.6 = bf16[1024,512]{1,0:T(8,128)(2,1)S(1)} custom-call(s32[8]{0:T(128)S(1)} %select_reduce_fusion.place_ref, s32[3]{0:T(128)S(1)} %copy-done.108, bf16[1024,512]{1,0:T(8,128)(2,1)S(1)} %get-tuple-element.142.q_ref, bf16[1024,128]{1,0:T(8,128)(2,1)S(1)} %get-tuple-element.143.kn_ref, bf16[1024,128]{1,0:T(8,128)(2,1)S(1)} %get-tuple-element.144.vn_ref, ...), custom_call_target="tpu_custom_call" | custom-call | flops 21474836480 | bytes 4718592 | tf_op jit(solution)/shard_map/attend/pallas_call | solution.py:177
  164.1 56.0 %attend.7 = bf16[1024,512]{1,0:T(8,128)(2,1)S(1)} custom-call(s32[8]{0:T(128)S(1)} %select_reduce_fusion.place_ref, s32[3]{0:T(128)S(1)} %copy-done.108, bf16[1024,512]{1,0:T(8,128)(2,1)S(1)} %get-tuple-element.146.q_ref, bf16[1024,128]{1,0:T(8,128)(2,1)S(1)} %get-tuple-element.147.kn_ref, bf16[1024,128]{1,0:T(8,128)(2,1)S(1)} %get-tuple-element.148.vn_ref, ...), custom_call_target="tpu_custom_call" | custom-call | flops 21474836480 | bytes 4718592 | tf_op jit(solution)/shard_map/attend/pallas_call | solution.py:177
  253.8 55.9 %attend.8 = bf16[1024,512]{1,0:T(8,128)(2,1)S(1)} custom-call(s32[8]{0:T(128)S(1)} %select_reduce_fusion.place_ref, s32[3]{0:T(128)S(1)} %copy-done.108, bf16[1024,512]{1,0:T(8,128)(2,1)S(1)} %get-tuple-element.154.q_ref, bf16[1024,128]{1,0:T(8,128)(2,1)S(1)} %get-tuple-element.155.kn_ref, bf16[1024,128]{1,0:T(8,128)(2,1)S(1)} %get-tuple-element.156.vn_ref, ...), custom_call_target="tpu_custom_call" | custom-call | flops 21474836480 | bytes 4718592 | tf_op jit(solution)/shard_map/attend/pallas_call | solution.py:177
  314.3 24.7 %collective-permute-done.1.refs_2_ = bf16[256,4096]{1,0:T(8,128)(2,1)S(1)} collective-permute-done((bf16[256,4096]{1,0:T(8,128)(2,1)S(1)}, bf16[256,4096]{1,0:T(8,128)(2,1)S(1)}, u32[]{:S(2)}, u32[]{:S(2)}) %collective-permute-start.1) | collective-permute-done | bytes 2097184 | tf_op jit(solution)/shard_map/ppermute | solution.py:283
  361.7 57.3 %collective-permute-done.6.refs_2_ = bf16[256,4096]{1,0:T(8,128)(2,1)S(1)} collective-permute-done((bf16[256,4096]{1,0:T(8,128)(2,1)S(1)}, bf16[256,4096]{1,0:T(8,128)(2,1)S(1)}, u32[]{:S(2)}, u32[]{:S(2)}) %collective-permute-start.6) | collective-permute-done | bytes 2097184 | tf_op jit(solution)/shard_map/ppermute | solution.py:283
  419.3 14.8 %collective-permute-done.7.refs_3_ = bf16[128,4096]{1,0:T(8,128)(2,1)S(1)} collective-permute-done((bf16[128,4096]{1,0:T(8,128)(2,1)S(1)}, bf16[128,4096]{1,0:T(8,128)(2,1)S(1)}, u32[]{:S(2)}, u32[]{:S(2)}) %collective-permute-start.7) | collective-permute-done | bytes 1048608 | tf_op jit(solution)/shard_map/ppermute | solution.py:283
  444.7 60.1 %collective-permute-done.5.refs_2_ = bf16[256,4096]{1,0:T(8,128)(2,1)} collective-permute-done((bf16[256,4096]{1,0:T(8,128)(2,1)}, bf16[256,4096]{1,0:T(8,128)(2,1)}, u32[]{:S(2)}, u32[]{:S(2)}) %collective-permute-start.5) | collective-permute-done | bytes 2097184 | tf_op jit(solution)/shard_map/ppermute | solution.py:283
  507.5 23.1 %fusion.49 = bf16[1024,1792]{1,0:T(8,128)(2,1)S(1)} fusion(bf16[1024,4096]{1,0:T(8,128)(2,1)} %all-gather.19.cloned.1.call-done, bf16[2,4096,1792]{2,1,0:T(8,128)(2,1)} %param.36, f32[1792]{0:T(1024)S(1)} %get-tuple-element.291), kind=kOutput, calls=%fused_computation.67 | convolution fusion | flops 15050735616 | bytes 26745856 | tf_op jit(solution)/shard_map/dot_general | solution.py:314
  550.5 23.4 %fusion.57 = bf16[1024,1792]{1,0:T(8,128)(2,1)S(1)} fusion(bf16[1024,4096]{1,0:T(8,128)(2,1)} %all-gather.21.cloned.1.call-done, bf16[2,4096,1792]{2,1,0:T(8,128)(2,1)} %param.36, f32[1792]{0:T(1024)S(1)} %get-tuple-element.291), kind=kOutput, calls=%fused_computation.75 | convolution fusion | flops 15050735616 | bytes 26745856 | tf_op jit(solution)/shard_map/dot_general | solution.py:314
  574.2 12.7 fusion.105
  604.9 15.8 %add_convert_fusion.7.refs_1_ = bf16[512,4096]{1,0:T(8,128)(2,1)} fusion(bf16[512,4096]{1,0:T(8,128)(2,1)} %collective-permute-done.11, bf16[512,1792]{1,0:T(8,128)(2,1)S(1)} %pad_maximum_fusion.2, bf16[2,1792,4096]{2,1,0:T(8,128)(2,1)} %param.38), kind=kOutput, calls=%fused_computation.55 | convolution fusion | flops 7522484224 | bytes 24903680 | tf_op jit(solution)/shard_map/dot_general | solution.py:289
  620.7 22.8 %fusion.65 = bf16[1024,1792]{1,0:T(8,128)(2,1)S(1)} fusion(bf16[1024,4096]{1,0:T(8,128)(2,1)} %all-gather.23.cloned.1.call-done, bf16[2,4096,1792]{2,1,0:T(8,128)(2,1)} %param.36, f32[1792]{0:T(1024)S(1)} %get-tuple-element.291), kind=kOutput, calls=%fused_computation.83 | convolution fusion | flops 15050735616 | bytes 26745856 | tf_op jit(solution)/shard_map/dot_general | solution.py:314
  659.7 12.9 collective-permute-done.12.refs_3_
  684.3 12.8 add_convert_fusion.6.refs_1_
  697.1 35.9 %collective-permute-done.15.refs_2_ = bf16[256,4096]{1,0:T(8,128)(2,1)S(1)} collective-permute-done((bf16[256,4096]{1,0:T(8,128)(2,1)S(1)}, bf16[256,4096]{1,0:T(8,128)(2,1)S(1)}, u32[]{:S(2)}, u32[]{:S(2)}) %collective-permute-start.15) | collective-permute-done | bytes 2097184 | tf_op jit(solution)/shard_map/ppermute | solution.py:283
  736.1 13.3 collective-permute-done.16.refs_3_
  755.6 54.5 %collective-permute-done.14.refs_2_ = bf16[256,4096]{1,0:T(8,128)(2,1)S(1)} collective-permute-done((bf16[256,4096]{1,0:T(8,128)(2,1)S(1)}, bf16[256,4096]{1,0:T(8,128)(2,1)S(1)}, u32[]{:S(2)}, u32[]{:S(2)}) %collective-permute-start.14) | collective-permute-done | bytes 2097184 | tf_op jit(solution)/shard_map/ppermute | solution.py:283
  834.3 55.7 %attend.9 = bf16[1024,512]{1,0:T(8,128)(2,1)S(1)} custom-call(s32[8]{0:T(128)S(1)} %copy-done.111, s32[3]{0:T(128)S(1)} %copy-done.109, bf16[1024,512]{1,0:T(8,128)(2,1)S(1)} %get-tuple-element.204.q_ref, bf16[1024,128]{1,0:T(8,128)(2,1)S(1)} %get-tuple-element.205.kn_ref, bf16[1024,128]{1,0:T(8,128)(2,1)S(1)} %get-tuple-element.206.vn_ref, ...), custom_call_target="tpu_custom_call" | custom-call | flops 21474836480 | bytes 4718592 | tf_op jit(solution)/shard_map/attend/pallas_call | solution.py:177
  919.5 55.7 %attend.10 = bf16[1024,512]{1,0:T(8,128)(2,1)S(1)} custom-call(s32[8]{0:T(128)S(1)} %copy-done.111, s32[3]{0:T(128)S(1)} %copy-done.109, bf16[1024,512]{1,0:T(8,128)(2,1)S(1)} %get-tuple-element.213.q_ref, bf16[1024,128]{1,0:T(8,128)(2,1)S(1)} %get-tuple-element.214.kn_ref, bf16[1024,128]{1,0:T(8,128)(2,1)S(1)} %get-tuple-element.215.vn_ref, ...), custom_call_target="tpu_custom_call" | custom-call | flops 21474836480 | bytes 4718592 | tf_op jit(solution)/shard_map/attend/pallas_call | solution.py:177
  1010.3 56.0 %attend.11 = bf16[1024,512]{1,0:T(8,128)(2,1)S(1)} custom-call(s32[8]{0:T(128)S(1)} %copy-done.111, s32[3]{0:T(128)S(1)} %copy-done.109, bf16[1024,512]{1,0:T(8,128)(2,1)S(1)} %get-tuple-element.221.q_ref, bf16[1024,128]{1,0:T(8,128)(2,1)S(1)} %get-tuple-element.222.kn_ref, bf16[1024,128]{1,0:T(8,128)(2,1)S(1)} %get-tuple-element.223.vn_ref, ...), custom_call_target="tpu_custom_call" | custom-call | flops 21474836480 | bytes 4718592 | tf_op jit(solution)/shard_map/attend/pallas_call | solution.py:177
  1093.2 25.0 %collective-permute-done.24.refs_3_ = bf16[128,4096]{1,0:T(8,128)(2,1)S(1)} collective-permute-done((bf16[128,4096]{1,0:T(8,128)(2,1)}, bf16[128,4096]{1,0:T(8,128)(2,1)S(1)}, u32[]{:S(2)}, u32[]{:S(2)}) %collective-permute-start.24) | collective-permute-done | bytes 1048608 | tf_op jit(solution)/shard_map/ppermute | solution.py:283
  1133.2 44.9 %collective-permute-done.25.refs_2_ = bf16[256,4096]{1,0:T(8,128)(2,1)S(1)} collective-permute-done((bf16[256,4096]{1,0:T(8,128)(2,1)S(1)}, bf16[256,4096]{1,0:T(8,128)(2,1)S(1)}, u32[]{:S(2)}, u32[]{:S(2)}) %collective-permute-start.25) | collective-permute-done | bytes 2097184 | tf_op jit(solution)/shard_map/ppermute | solution.py:283
  1180.8 23.8 %fusion.73 = bf16[1024,1792]{1,0:T(8,128)(2,1)S(1)} fusion(bf16[1024,4096]{1,0:T(8,128)(2,1)} %all-gather.31.cloned.1.call-done, bf16[2,4096,1792]{2,1,0:T(8,128)(2,1)} %param.36, f32[1792]{0:T(1024)S(1)} %copy-done.132), kind=kOutput, calls=%fused_computation.91 | convolution fusion | flops 15050735616 | bytes 26745856 | tf_op jit(solution)/shard_map/dot_general | solution.py:314
  1224.2 24.1 %fusion.81 = bf16[1024,1792]{1,0:T(8,128)(2,1)S(1)} fusion(bf16[1024,4096]{1,0:T(8,128)(2,1)} %all-gather.33.cloned.1.call-done, bf16[2,4096,1792]{2,1,0:T(8,128)(2,1)} %param.36, f32[1792]{0:T(1024)S(1)} %copy-done.132), kind=kOutput, calls=%fused_computation.99 | convolution fusion | flops 15050735616 | bytes 26745856 | tf_op jit(solution)/shard_map/dot_general | solution.py:314
  1260.8 15.7 %add_convert_fusion.2 = bf16[512,4096]{1,0:T(8,128)(2,1)} fusion(bf16[512,4096]{1,0:T(8,128)(2,1)} %collective-permute-done.26, bf16[512,1792]{1,0:T(8,128)(2,1)S(1)} %pad_maximum_fusion.4, bf16[2,1792,4096]{2,1,0:T(8,128)(2,1)} %param.38), kind=kOutput, calls=%fused_computation.50 | convolution fusion | flops 7522484224 | bytes 24903680 | tf_op jit(solution)/shard_map/dot_general | solution.py:289
  1289.1 22.9 %fusion.89 = bf16[1024,1792]{1,0:T(8,128)(2,1)S(1)} fusion(bf16[1024,4096]{1,0:T(8,128)(2,1)} %all-gather.35.cloned.1.call-done, bf16[2,4096,1792]{2,1,0:T(8,128)(2,1)} %param.36, f32[1792]{0:T(1024)S(1)} %copy-done.132), kind=kOutput, calls=%fused_computation.107 | convolution fusion | flops 15050735616 | bytes 26745856 | tf_op jit(solution)/shard_map/dot_general | solution.py:314
  1312.4 12.7 fusion.117
  1329.7 21.7 %collective-permute-done.28 = bf16[256,4096]{1,0:T(8,128)(2,1)S(1)} collective-permute-done((bf16[256,4096]{1,0:T(8,128)(2,1)S(1)}, bf16[256,4096]{1,0:T(8,128)(2,1)S(1)}, u32[]{:S(2)}, u32[]{:S(2)}) %collective-permute-start.28) | collective-permute-done | bytes 2097184 | tf_op jit(solution)/shard_map/ppermute | solution.py:283
  1368.2 17.0 %collective-permute-done.31 = bf16[256,4096]{1,0:T(8,128)(2,1)S(1)} collective-permute-done((bf16[256,4096]{1,0:T(8,128)(2,1)}, bf16[256,4096]{1,0:T(8,128)(2,1)S(1)}, u32[]{:S(2)}, u32[]{:S(2)}) %collective-permute-start.31) | collective-permute-done | bytes 2097184 | tf_op jit(solution)/shard_map/ppermute | solution.py:283
  1388.5 23.0 %collective-permute-done.33 = bf16[128,4096]{1,0:T(8,128)(2,1)S(1)} collective-permute-done((bf16[128,4096]{1,0:T(8,128)(2,1)S(1)}, bf16[128,4096]{1,0:T(8,128)(2,1)S(1)}, u32[]{:S(2)}, u32[]{:S(2)}) %collective-permute-start.33) | collective-permute-done | bytes 1048608 | tf_op jit(solution)/shard_map/ppermute | solution.py:283
  1423.4 13.1 write_caches.1
  (507 shorter events, 420.7 us)
Async XLA Ops:
  7.2 57.0 %all-gather.13.cloned.1.call-start = ((), (), s32[]{:S(2)}) async-start(), calls=%async_computation | async-start | bytes 9437184 | tf_op jit(solution)/shard_map/all_gather | solution.py:286
  12.5 131.9 %all-gather.15.cloned.1.call-start = ((), (), s32[]{:S(2)}) async-start(), calls=%async_computation.1 | async-start | bytes 9437184 | tf_op jit(solution)/shard_map/all_gather | solution.py:286
  15.1 219.1 %all-gather.17.cloned.1.call-start = ((), (), s32[]{:S(2)}) async-start(), calls=%async_computation.2 | async-start | bytes 9437184 | tf_op jit(solution)/shard_map/all_gather | solution.py:286
  17.6 489.9 %all-gather.19.cloned.1.call-start = ((), (), s32[]{:S(2)}) async-start(), calls=%async_computation.3 | async-start | bytes 9437184 | tf_op jit(solution)/shard_map/all_gather | solution.py:286
  144.2 78.8 %collective-permute-start = (bf16[512,4096]{1,0:T(8,128)(2,1)}, bf16[512,4096]{1,0:T(8,128)(2,1)}, u32[]{:S(2)}, u32[]{:S(2)}) collective-permute-start(bf16[512,4096]{1,0:T(8,128)(2,1)} %convolution_convert_fusion.5), channel_id=1, source_target_pairs={{0,1},{1,0},{2,3},{3,2},{4,5},{5,4},{6,7},{7,6}} | collective-permute-start | bytes 12582920 | tf_op jit(solution)/shard_map/ppermute | solution.py:283
  358.3 192.2 %all-gather.21.cloned.1.call-start = ((), (), s32[]{:S(2)}) async-start(), calls=%async_computation.4 | async-start | bytes 9437184 | tf_op jit(solution)/shard_map/all_gather | solution.py:286
  360.3 58.7 %collective-permute-start.6 = (bf16[256,4096]{1,0:T(8,128)(2,1)S(1)}, bf16[256,4096]{1,0:T(8,128)(2,1)S(1)}, u32[]{:S(2)}, u32[]{:S(2)}) collective-permute-start(bf16[256,4096]{1,0:T(8,128)(2,1)S(1)} %slice.290), channel_id=1, source_target_pairs={{0,2},{1,5},{2,0},{3,7},{4,6},{5,1},{6,4},{7,3}} | collective-permute-start | bytes 6291464 | tf_op jit(solution)/shard_map/ppermute | solution.py:283
  438.4 182.3 %all-gather.23.cloned.1.call-start = ((), (), s32[]{:S(2)}) async-start(), calls=%async_computation.5 | async-start | bytes 9437184 | tf_op jit(solution)/shard_map/all_gather | solution.py:286
  441.6 63.2 %collective-permute-start.5 = (bf16[256,4096]{1,0:T(8,128)(2,1)}, bf16[256,4096]{1,0:T(8,128)(2,1)}, u32[]{:S(2)}, u32[]{:S(2)}) collective-permute-start(bf16[256,4096]{1,0:T(8,128)(2,1)} %slice.289), channel_id=1, source_target_pairs={{0,2},{1,5},{2,0},{3,7},{4,6},{5,1},{6,4},{7,3}} | collective-permute-start | bytes 6291464 | tf_op jit(solution)/shard_map/ppermute | solution.py:283
  507.5 37.0 %collective-permute-start.9 = (bf16[128,4096]{1,0:T(8,128)(2,1)}, bf16[128,4096]{1,0:T(8,128)(2,1)}, u32[]{:S(2)}, u32[]{:S(2)}) collective-permute-start(bf16[128,4096]{1,0:T(8,128)(2,1)} %add_convert_fusion.24), channel_id=1, source_target_pairs={{0,4},{1,3},{2,6},{3,1},{4,0},{5,7},{6,2},{7,5}} | collective-permute-start | bytes 3145736 | tf_op jit(solution)/shard_map/ppermute | solution.py:283
  550.4 265.9 %all-gather.25.cloned.1.call-start = ((), (), s32[]{:S(2)}) async-start(), calls=%async_computation.6 | async-start | bytes 9437184 | tf_op jit(solution)/shard_map/all_gather | solution.py:286
  550.4 37.3 %collective-permute-start.8 = (bf16[512,4096]{1,0:T(8,128)(2,1)}, bf16[512,4096]{1,0:T(8,128)(2,1)}, u32[]{:S(2)}, u32[]{:S(2)}) collective-permute-start(bf16[512,4096]{1,0:T(8,128)(2,1)} %fusion.102), channel_id=1, source_target_pairs={{0,1},{1,0},{2,3},{3,2},{4,5},{5,4},{6,7},{7,6}} | collective-permute-start | bytes 12582920 | tf_op jit(solution)/shard_map/ppermute | solution.py:283
  603.1 54.3 %collective-permute-start.10 = (bf16[256,4096]{1,0:T(8,128)(2,1)}, bf16[256,4096]{1,0:T(8,128)(2,1)S(1)}, u32[]{:S(2)}, u32[]{:S(2)}) collective-permute-start(bf16[256,4096]{1,0:T(8,128)(2,1)} %slice.291), channel_id=1, source_target_pairs={{0,2},{1,5},{2,0},{3,7},{4,6},{5,1},{6,4},{7,3}} | collective-permute-start | bytes 6291464 | tf_op jit(solution)/shard_map/ppermute | solution.py:283
  676.9 223.4 %all-gather.27.cloned.1.call-start = ((), (), s32[]{:S(2)}) async-start(), calls=%async_computation.7 | async-start | bytes 9437184 | tf_op jit(solution)/shard_map/all_gather | solution.py:286
  678.8 54.3 %collective-permute-start.15 = (bf16[256,4096]{1,0:T(8,128)(2,1)S(1)}, bf16[256,4096]{1,0:T(8,128)(2,1)S(1)}, u32[]{:S(2)}, u32[]{:S(2)}) collective-permute-start(bf16[256,4096]{1,0:T(8,128)(2,1)S(1)} %slice.293), channel_id=1, source_target_pairs={{0,2},{1,5},{2,0},{3,7},{4,6},{5,1},{6,4},{7,3}} | collective-permute-start | bytes 6291464 | tf_op jit(solution)/shard_map/ppermute | solution.py:283
  753.5 238.8 %all-gather.29.cloned.1.call-start = ((), (), s32[]{:S(2)}) async-start(), calls=%async_computation.8 | async-start | bytes 9437184 | tf_op jit(solution)/shard_map/all_gather | solution.py:286
  755.4 54.7 %collective-permute-start.14 = (bf16[256,4096]{1,0:T(8,128)(2,1)S(1)}, bf16[256,4096]{1,0:T(8,128)(2,1)S(1)}, u32[]{:S(2)}, u32[]{:S(2)}) collective-permute-start(bf16[256,4096]{1,0:T(8,128)(2,1)S(1)} %slice.292), channel_id=1, source_target_pairs={{0,2},{1,5},{2,0},{3,7},{4,6},{5,1},{6,4},{7,3}} | collective-permute-start | bytes 6291464 | tf_op jit(solution)/shard_map/ppermute | solution.py:283
  813.9 80.6 %collective-permute-start.18 = (bf16[128,4096]{1,0:T(8,128)(2,1)}, bf16[128,4096]{1,0:T(8,128)(2,1)}, u32[]{:S(2)}, u32[]{:S(2)}) collective-permute-start(bf16[128,4096]{1,0:T(8,128)(2,1)} %add_convert_fusion.21), channel_id=1, source_target_pairs={{0,4},{1,3},{2,6},{3,1},{4,0},{5,7},{6,2},{7,5}} | collective-permute-start | bytes 3145736 | tf_op jit(solution)/shard_map/ppermute | solution.py:283
  900.2 280.5 %all-gather.31.cloned.1.call-start = ((), (), s32[]{:S(2)}) async-start(), calls=%async_computation.9 | async-start | bytes 9437184 | tf_op jit(solution)/shard_map/all_gather | solution.py:286
  900.3 77.9 %collective-permute-start.17 = (bf16[512,4096]{1,0:T(8,128)(2,1)}, bf16[512,4096]{1,0:T(8,128)(2,1)}, u32[]{:S(2)}, u32[]{:S(2)}) collective-permute-start(bf16[512,4096]{1,0:T(8,128)(2,1)} %convolution_convert_fusion.2), channel_id=1, source_target_pairs={{0,1},{1,0},{2,3},{3,2},{4,5},{5,4},{6,7},{7,6}} | collective-permute-start | bytes 12582920 | tf_op jit(solution)/shard_map/ppermute | solution.py:283
  984.3 86.4 %collective-permute-start.19 = (bf16[256,4096]{1,0:T(8,128)(2,1)}, bf16[256,4096]{1,0:T(8,128)(2,1)}, u32[]{:S(2)}, u32[]{:S(2)}) collective-permute-start(bf16[256,4096]{1,0:T(8,128)(2,1)} %slice.297), channel_id=1, source_target_pairs={{0,2},{1,5},{2,0},{3,7},{4,6},{5,1},{6,4},{7,3}} | collective-permute-start | bytes 6291464 | tf_op jit(solution)/shard_map/ppermute | solution.py:283
  991.2 82.3 %collective-permute-start.22 = (bf16[256,4096]{1,0:T(8,128)(2,1)}, bf16[256,4096]{1,0:T(8,128)(2,1)}, u32[]{:S(2)}, u32[]{:S(2)}) collective-permute-start(bf16[256,4096]{1,0:T(8,128)(2,1)} %slice.300), channel_id=1, source_target_pairs={{0,2},{1,5},{2,0},{3,7},{4,6},{5,1},{6,4},{7,3}} | collective-permute-start | bytes 6291464 | tf_op jit(solution)/shard_map/ppermute | solution.py:283
  1091.9 132.4 %all-gather.33.cloned.1.call-start = ((), (), s32[]{:S(2)}) async-start(), calls=%async_computation.10 | async-start | bytes 9437184 | tf_op jit(solution)/shard_map/all_gather | solution.py:286
  1091.9 34.3 %collective-permute-start.23 = (bf16[512,4096]{1,0:T(8,128)(2,1)}, bf16[512,4096]{1,0:T(8,128)(2,1)}, u32[]{:S(2)}, u32[]{:S(2)}) collective-permute-start(bf16[512,4096]{1,0:T(8,128)(2,1)} %convolution_convert_fusion), channel_id=1, source_target_pairs={{0,1},{1,0},{2,3},{3,2},{4,5},{5,4},{6,7},{7,6}} | collective-permute-start | bytes 12582920 | tf_op jit(solution)/shard_map/ppermute | solution.py:283
  1126.2 162.9 %all-gather.35.cloned.1.call-start = ((), (), s32[]{:S(2)}) async-start(), calls=%async_computation.11 | async-start | bytes 9437184 | tf_op jit(solution)/shard_map/all_gather | solution.py:286
  1132.4 45.7 %collective-permute-start.25 = (bf16[256,4096]{1,0:T(8,128)(2,1)S(1)}, bf16[256,4096]{1,0:T(8,128)(2,1)S(1)}, u32[]{:S(2)}, u32[]{:S(2)}) collective-permute-start(bf16[256,4096]{1,0:T(8,128)(2,1)S(1)} %slice.302), channel_id=1, source_target_pairs={{0,2},{1,5},{2,0},{3,7},{4,6},{5,1},{6,4},{7,3}} | collective-permute-start | bytes 6291464 | tf_op jit(solution)/shard_map/ppermute | solution.py:283
  1179.3 39.2 %collective-permute-start.27 = (bf16[128,4096]{1,0:T(8,128)(2,1)}, bf16[128,4096]{1,0:T(8,128)(2,1)}, u32[]{:S(2)}, u32[]{:S(2)}) collective-permute-start(bf16[128,4096]{1,0:T(8,128)(2,1)} %add_convert_fusion.18), channel_id=1, source_target_pairs={{0,4},{1,3},{2,6},{3,1},{4,0},{5,7},{6,2},{7,5}} | collective-permute-start | bytes 3145736 | tf_op jit(solution)/shard_map/ppermute | solution.py:283
  1224.2 36.6 %collective-permute-start.26 = (bf16[512,4096]{1,0:T(8,128)(2,1)}, bf16[512,4096]{1,0:T(8,128)(2,1)}, u32[]{:S(2)}, u32[]{:S(2)}) collective-permute-start(bf16[512,4096]{1,0:T(8,128)(2,1)} %fusion.111), channel_id=1, source_target_pairs={{0,1},{1,0},{2,3},{3,2},{4,5},{5,4},{6,7},{7,6}} | collective-permute-start | bytes 12582920 | tf_op jit(solution)/shard_map/ppermute | solution.py:283
  1325.1 30.3 %collective-permute-start.32 = (bf16[512,4096]{1,0:T(8,128)(2,1)}, bf16[512,4096]{1,0:T(8,128)(2,1)}, u32[]{:S(2)}, u32[]{:S(2)}) collective-permute-start(bf16[512,4096]{1,0:T(8,128)(2,1)} %fusion.117), channel_id=1, source_target_pairs={{0,1},{1,0},{2,3},{3,2},{4,5},{5,4},{6,7},{7,6}} | collective-permute-start | bytes 12582920 | tf_op jit(solution)/shard_map/ppermute | solution.py:283
  1328.7 56.5 %collective-permute-start.31 = (bf16[256,4096]{1,0:T(8,128)(2,1)}, bf16[256,4096]{1,0:T(8,128)(2,1)S(1)}, u32[]{:S(2)}, u32[]{:S(2)}) collective-permute-start(bf16[256,4096]{1,0:T(8,128)(2,1)} %slice.304), channel_id=1, source_target_pairs={{0,2},{1,5},{2,0},{3,7},{4,6},{5,1},{6,4},{7,3}} | collective-permute-start | bytes 6291464 | tf_op jit(solution)/shard_map/ppermute | solution.py:283
  1352.9 33.6 %collective-permute-start.30 = (bf16[128,4096]{1,0:T(8,128)(2,1)}, bf16[128,4096]{1,0:T(8,128)(2,1)}, u32[]{:S(2)}, u32[]{:S(2)}) collective-permute-start(bf16[128,4096]{1,0:T(8,128)(2,1)} %add_convert_fusion.17), channel_id=1, source_target_pairs={{0,4},{1,3},{2,6},{3,1},{4,0},{5,7},{6,2},{7,5}} | collective-permute-start | bytes 3145736 | tf_op jit(solution)/shard_map/ppermute | solution.py:283
  1367.9 51.0 %collective-permute-start.34 = (bf16[256,4096]{1,0:T(8,128)(2,1)S(1)}, bf16[256,4096]{1,0:T(8,128)(2,1)S(1)}, u32[]{:S(2)}, u32[]{:S(2)}) collective-permute-start(bf16[256,4096]{1,0:T(8,128)(2,1)S(1)} %slice.305), channel_id=1, source_target_pairs={{0,2},{1,5},{2,0},{3,7},{4,6},{5,1},{6,4},{7,3}} | collective-permute-start | bytes 6291464 | tf_op jit(solution)/shard_map/ppermute | solution.py:283
  (171 other events, 4016.8 us)
Sparse Core Ops, SparseCore 0:
  12.6 51.5 all-gather.12
  66.6 48.6 all-gather.14
  117.7 48.6 all-gather.16
  358.4 66.8 all-gather.18
  438.5 68.6 all-gather.20
  550.5 51.2 all-gather.22
  677.0 63.7 all-gather.24
  753.6 63.1 all-gather.26
  900.3 48.8 all-gather.28
  1092.0 59.8 all-gather.30
  1153.7 64.9 all-gather.32
  1224.3 48.4 all-gather.34

commit v2 on v1

--- a/solution.py
+++ b/solution.py
@@ -11,7 +11,8 @@
 NORM_EPS = 1e-5
 LOG2E = 1.4426950408889634
 HIDE = -(1 << 30)
-TURNS = [int(c) for c in '012010120201120210120021120210120101220210120210122']
+VMEM_LIMIT = 60 << 20
+TURNS = [int(c) for c in '012001010212102201100121202021010212120201102121202']
 
 
 def norm_kernel(*refs, joined):
@@ -49,7 +50,7 @@
         in_specs=specs + scale_specs,
         out_specs=[line] * len(outs),
         out_shape=outs,
-        compiler_params=pltpu.CompilerParams(dimension_semantics=('arbitrary',), vmem_limit_bytes=16 << 20),
+        compiler_params=pltpu.CompilerParams(dimension_semantics=('arbitrary',), vmem_limit_bytes=VMEM_LIMIT),
         cost_estimate=pl.CostEstimate(flops=8 * part * model, bytes_accessed=2 * (len(args) + len(outs)) * part * model, transcendentals=0),
         name='norm',
     )(*args, *scales)
@@ -90,13 +91,13 @@
         in_specs=[row_block(model), table, table, weight(q_cols), weight(kv_cols), weight(kv_cols), bias(q_cols), bias(kv_cols), bias(kv_cols)],
         out_specs=[row_block(q_cols), row_block(kv_cols), row_block(kv_cols)],
         out_shape=[jax.ShapeDtypeStruct((chunk, cols), jnp.bfloat16) for cols in (q_cols, kv_cols, kv_cols)],
-        compiler_params=pltpu.CompilerParams(dimension_semantics=('arbitrary',), vmem_limit_bytes=40 << 20),
+        compiler_params=pltpu.CompilerParams(dimension_semantics=('arbitrary',), vmem_limit_bytes=VMEM_LIMIT),
         cost_estimate=pl.CostEstimate(flops=2 * chunk * model * (q_cols + 2 * kv_cols), bytes_accessed=2 * (chunk + q_cols + 2 * kv_cols) * model, transcendentals=0),
         name='qkv_rotary',
     )(acts, cos_tab, sin_tab, w_q, w_k, w_v, b_q[:, None, :], b_k[:, None, :], b_v[:, None, :])
 
 
-def attention_kernel(place_ref, start_ref, q_ref, kn_ref, vn_ref, ko_ref, vo_ref, held_ref, o_ref, score_ref, *, seq, group, key_block):
+def attention_kernel(start_ref, q_ref, kn_ref, vn_ref, ko_ref, vo_ref, held_ref, o_ref, score_ref, *, seq, group, key_block, new_block):
     rows = q_ref.shape[0]
     head_dim = kn_ref.shape[1]
     window = ko_ref.shape[0]
@@ -131,43 +132,44 @@
         return lane_max(values, top)
 
     def score_new(step, top):
-        at = pl.multiple_of(step * key_block, key_block)
-        values = lax.dot_general(query, kn_ref[pl.ds(at, key_block), :], contract, preferred_element_type=jnp.float32)
-        fresh = at + lax.broadcasted_iota(jnp.int32, (1, key_block), 1)
+        at = pl.multiple_of(step * new_block, new_block)
+        values = lax.dot_general(query, kn_ref[pl.ds(at, new_block), :], contract, preferred_element_type=jnp.float32)
+        fresh = at + lax.broadcasted_iota(jnp.int32, (1, new_block), 1)
         values = jnp.where(fresh <= token, values, -jnp.inf)
-        score_ref[:, pl.ds(pl.multiple_of(window + at, key_block), key_block)] = values
+        score_ref[:, pl.ds(pl.multiple_of(window + at, new_block), new_block)] = values
         return lane_max(values, top)
 
-    new_steps = (block * rows + rows + key_block - 1) // key_block
+    old_steps = (jnp.minimum(start, window) + key_block - 1) // key_block
+    new_steps = (block * rows + rows + new_block - 1) // new_block
     top = jnp.full(top_shape, -jnp.inf, jnp.float32)
-    top = lax.fori_loop(0, window // key_block, score_old, top)
+    top = lax.fori_loop(0, old_steps, score_old, top)
     top = lax.fori_loop(0, new_steps, score_new, top)
     top = jnp.max(top, axis=1, keepdims=True)
 
-    def weigh(at, value_ref, value_at, carry):
+    def weigh(at, size, value_ref, value_at, carry):
         total, mixed = carry
-        weights = jnp.exp2((score_ref[:, pl.ds(at, key_block)] - top) * scale)
+        weights = jnp.exp2((score_ref[:, pl.ds(at, size)] - top) * scale)
         total = lane_sum(weights, total)
-        mixed = mixed + jnp.dot(weights.astype(jnp.bfloat16), value_ref[pl.ds(value_at, key_block), :], preferred_element_type=jnp.float32)
+        mixed = mixed + jnp.dot(weights.astype(jnp.bfloat16), value_ref[pl.ds(value_at, size), :], preferred_element_type=jnp.float32)
         return total, mixed
 
     def mix_old(step, carry):
         at = pl.multiple_of(step * key_block, key_block)
-        return weigh(at, vo_ref, at, carry)
+        return weigh(at, key_block, vo_ref, at, carry)
 
     def mix_new(step, carry):
-        at = pl.multiple_of(step * key_block, key_block)
-        return weigh(pl.multiple_of(window + at, key_block), vn_ref, at, carry)
+        at = pl.multiple_of(step * new_block, new_block)
+        return weigh(pl.multiple_of(window + at, new_block), new_block, vn_ref, at, carry)
 
     carry = (jnp.zeros(top_shape, jnp.float32), jnp.zeros((rows * group, head_dim), jnp.float32))
-    carry = lax.fori_loop(0, window // key_block, mix_old, carry)
+    carry = lax.fori_loop(0, old_steps, mix_old, carry)
     total, mixed = lax.fori_loop(0, new_steps, mix_new, carry)
     mixed = (mixed / jnp.sum(total, axis=1, keepdims=True)).astype(jnp.bfloat16)
     for g in range(group):
         o_ref[:, g * head_dim:(g + 1) * head_dim] = mixed[g * rows:(g + 1) * rows]
 
 
-def attend(query, key_new, value_new, key_cache, value_cache, held, place, start_pos, layer, seq, rows=128, key_block=512):
+def attend(query, key_new, value_new, key_cache, value_cache, held, start_pos, layer, seq, rows=256, key_block=2048, new_block=512):
     chunk, q_cols = query.shape
     window, head_dim = key_cache.shape[2:]
     group = q_cols // head_dim
@@ -175,19 +177,77 @@
     whole = pl.BlockSpec((chunk, head_dim), lambda i, *_: (0, 0))
     cache = pl.BlockSpec((None, None, window, head_dim), lambda i, *_: (layer, seq, 0, 0))
     return pl.pallas_call(
-        functools.partial(attention_kernel, seq=seq, group=group, key_block=key_block),
+        functools.partial(attention_kernel, seq=seq, group=group, key_block=key_block, new_block=new_block),
         grid_spec=pltpu.PrefetchScalarGridSpec(
-            num_scalar_prefetch=2,
+            num_scalar_prefetch=1,
             grid=(chunk // rows,),
             in_specs=[pl.BlockSpec((rows, q_cols), lambda i, *_: (i, 0)), whole, whole, cache, cache, pl.BlockSpec((None, 1, window), lambda i, *_: (seq, 0, 0))],
-            out_specs=pl.BlockSpec((rows, q_cols), lambda i, place, start: (place[i], 0)),
+            out_specs=pl.BlockSpec((rows, q_cols), lambda i, *_: (i, 0)),
             scratch_shapes=[pltpu.VMEM((rows * group, keys), jnp.float32)],
         ),
         out_shape=jax.ShapeDtypeStruct((chunk, q_cols), jnp.bfloat16),
-        compiler_params=pltpu.CompilerParams(dimension_semantics=('arbitrary',), vmem_limit_bytes=40 << 20),
+        compiler_params=pltpu.CompilerParams(dimension_semantics=('arbitrary',), vmem_limit_bytes=VMEM_LIMIT),
         cost_estimate=pl.CostEstimate(flops=8 * chunk * q_cols * keys, bytes_accessed=4 * (window + chunk) * head_dim + 4 * chunk * q_cols, transcendentals=0),
         name='attend',
-    )(place, start_pos, query, key_new, value_new, key_cache, value_cache, held)
+    )(start_pos, query, key_new, value_new, key_cache, value_cache, held)
+
+
+def project_kernel(table_ref, acts_ref, weight_ref, *refs, shards, joined):
+    part = acts_ref.shape[0] // table_ref.shape[0]
+    first = shards if joined is None else 0
+    rows = [acts_ref[pl.ds(pl.multiple_of(table_ref[first + i] * part, part), part), :] for i in range(shards)]
+    total = jnp.dot(jnp.concatenate(rows, axis=0), weight_ref[...], preferred_element_type=jnp.float32)
+    if joined is None:
+        refs[0][...] = total.astype(jnp.bfloat16)
+    else:
+        lead_ref, kept_ref, sent_ref = refs
+        total = (total + lead_ref[...].astype(jnp.float32)).astype(jnp.bfloat16)
+        kept_ref[...] = total[:total.shape[0] // 2]
+        sent_ref[...] = total[total.shape[0] // 2:]
+
+
+def project_rows(table, acts, weight, layer, lead, cols):
+    chunk, depth = acts.shape
+    model = weight.shape[2]
+    half = chunk // 2
+    out = lambda rows: pl.BlockSpec((rows, cols), lambda i, *_: (0, i))
+    shape = lambda rows: jax.ShapeDtypeStruct((rows, model), jnp.bfloat16)
+    in_specs = [pl.BlockSpec((chunk, depth), lambda i, *_: (0, 0)), pl.BlockSpec((None, depth, cols), lambda i, *_: (layer, 0, i))]
+    args = [table, acts, weight]
+    if lead is None:
+        out_specs, out_shape = [out(half)], [shape(half)]
+    else:
+        in_specs.append(out(half))
+        args.append(lead)
+        out_specs, out_shape = [out(half // 2)] * 2, [shape(half // 2)] * 2
+    return pl.pallas_call(
+        functools.partial(project_kernel, shards=table.shape[0] // 2, joined=None if lead is None else True),
+        grid_spec=pltpu.PrefetchScalarGridSpec(num_scalar_prefetch=1, grid=(model // cols,), in_specs=in_specs, out_specs=out_specs),
+        out_shape=out_shape,
+        compiler_params=pltpu.CompilerParams(dimension_semantics=('arbitrary',), vmem_limit_bytes=VMEM_LIMIT),
+        cost_estimate=pl.CostEstimate(flops=2 * half * depth * model, bytes_accessed=2 * (chunk * depth + depth * model + half * model), transcendentals=0),
+        name='project_rows',
+    )(*args)
+
+
+def expand_kernel(x_ref, weight_ref, bias_ref, out_ref):
+    lifted = jnp.dot(x_ref[...], weight_ref[...], preferred_element_type=jnp.float32) + bias_ref[...].astype(jnp.float32)
+    out_ref[...] = jax.nn.gelu(lifted, approximate=True).astype(jnp.bfloat16)
+
+
+def expand_rows(acts, weight, bias, layer, rows=512, cols=256):
+    chunk, model = acts.shape
+    width = weight.shape[2]
+    return pl.pallas_call(
+        expand_kernel,
+        grid=(chunk // rows, width // cols),
+        in_specs=[pl.BlockSpec((rows, model), lambda i, j: (i, 0)), pl.BlockSpec((None, model, cols), lambda i, j: (layer, 0, j)), pl.BlockSpec((None, 1, cols), lambda i, j: (layer, 0, j))],
+        out_specs=pl.BlockSpec((rows, cols), lambda i, j: (i, j)),
+        out_shape=jax.ShapeDtypeStruct((chunk, width), jnp.bfloat16),
+        compiler_params=pltpu.CompilerParams(dimension_semantics=('arbitrary', 'arbitrary'), vmem_limit_bytes=VMEM_LIMIT),
+        cost_estimate=pl.CostEstimate(flops=2 * chunk * model * width, bytes_accessed=2 * (chunk * model + 2 * model * width + chunk * width), transcendentals=0),
+        name='expand',
+    )(acts, weight, bias)
 
 
 def cache_kernel(start_ref, ko_ref, vo_ref, kn_ref, vn_ref, kout_ref, vout_ref, ring_ref):
@@ -228,7 +288,7 @@
             scratch_shapes=[pltpu.VMEM((window + chunk + 16, head_dim), jnp.bfloat16)],
         ),
         out_shape=[jax.ShapeDtypeStruct(key_cache.shape, jnp.bfloat16)] * 2,
-        compiler_params=pltpu.CompilerParams(dimension_semantics=('arbitrary', 'arbitrary'), vmem_limit_bytes=32 << 20),
+        compiler_params=pltpu.CompilerParams(dimension_semantics=('arbitrary', 'arbitrary'), vmem_limit_bytes=VMEM_LIMIT),
         cost_estimate=pl.CostEstimate(flops=1 << 24, bytes_accessed=8 * layers * seqs * window * head_dim, transcendentals=0),
         name='write_caches',
     )(start_pos, key_cache, value_cache, key_new, value_new)
@@ -263,9 +323,6 @@
         theirs = [chip ^ flip for flip in (0, near, far, 3)]
         order = [c * 2 + core for c in mine] + [c * 2 + 1 - core for c in theirs]
         table = jnp.stack(order).astype(jnp.int32)
-        place = jnp.sum(jnp.where(table[None, :] == jnp.arange(count)[:, None], jnp.arange(count)[None, :], 0), axis=1).astype(jnp.int32)
-        half = chunk // 2
-
         norms = norm_params.reshape(-1, 1, model)
         out_bias = b_o[:, None, :]
         down_bias = b_down[:, None, :]
@@ -285,40 +342,37 @@
         def gather(value):
             return lax.all_gather(value, 'tp', axis=0, tiled=True)
 
-        def add_lead(own, lead, weight):
-            return ((jnp.dot(own, weight, preferred_element_type=jnp.float32) + lead.astype(jnp.float32)).astype(jnp.bfloat16),)
-
-        def add_came(pair, came):
-            return ((pair[part:2 * part].astype(jnp.float32) + came[part:].astype(jnp.float32)).astype(jnp.bfloat16),)
-
-        def scatter_sum(lead, own, weight):
+        up_bias = b_up[:, None, :]
+
+        def add_came(kept, came):
+            return ((kept[part:].astype(jnp.float32) + came[part:].astype(jnp.float32)).astype(jnp.bfloat16),)
+
+        def scatter_sum(lead, acts, weight, layer, cols):
             lead = send(lead, pairs_core)
             yield
-            pair, = item(functools.partial(add_lead, weight=weight), own, lead)
-            came = send(pair[2 * part:], pairs_first)
+            kept, sent = item(lambda lead: project_rows(table, acts, weight, layer, lead, cols), lead)
+            came = send(sent, pairs_first)
             yield
-            onward, = item(add_came, pair, came)
+            onward, = item(add_came, kept, came)
             last = send(onward, pairs_second)
             yield
-            return pair, came, last
+            return kept, came, last
 
         def attention(gathered, layer, seq):
             query, key_new, value_new = qkv_project(gathered, cos_tab, sin_tab, w_q, w_k, w_v, b_q, b_k, b_v, layer, seq)
             fresh_keys[layer][seq] = key_new
             fresh_values[layer][seq] = value_new
-            mixed = attend(query, key_new, value_new, keys_in, values_in, held, place, start_pos, layer, seq)
-            lead = jnp.dot(mixed[half:], w_o[layer], preferred_element_type=jnp.float32).astype(jnp.bfloat16)
-            return lead, mixed[:half]
+            mixed = attend(query, key_new, value_new, keys_in, values_in, held, start_pos, layer, seq)
+            lead, = project_rows(table, mixed, w_o, layer, None, 1024)
+            return lead, mixed
 
         def expand(gathered, layer):
-            lifted = jnp.dot(gathered, w_up[layer], preferred_element_type=jnp.float32) + b_up[layer].astype(jnp.float32)
-            active = jax.nn.gelu(lifted, approximate=True).astype(jnp.bfloat16)
-            pick = lambda indices: jnp.concatenate([lax.dynamic_slice_in_dim(active, index * part, part, 0) for index in indices], axis=0)
-            lead = jnp.dot(pick(order[4:]), w_down[layer], preferred_element_type=jnp.float32).astype(jnp.bfloat16)
-            return lead, pick(order[:4])
-
-        def finish(middle, pair, came, last):
-            summed = pair[:part].astype(jnp.float32) + came[:part].astype(jnp.float32) + last.astype(jnp.float32)
+            active = expand_rows(gathered, w_up, up_bias, layer)
+            lead, = project_rows(table, active, w_down, layer, None, 512)
+            return lead, active
+
+        def finish(middle, kept, came, last):
+            summed = kept[:part].astype(jnp.float32) + came[:part].astype(jnp.float32) + last.astype(jnp.float32)
             return ((middle.astype(jnp.float32) + summed + b_down[layers - 1].astype(jnp.float32)).astype(jnp.bfloat16),)
 
         def join(base, *terms, bias, layer, which):
@@ -337,13 +391,13 @@
                 gathered = gather(normed)
                 yield
                 lead, own = item(functools.partial(attention, layer=layer, seq=seq), gathered)
-                terms = yield from scatter_sum(lead, own, w_o[layer])
+                terms = yield from scatter_sum(lead, own, w_o, layer, 1024)
                 seq_of[0] = seq
                 normed, middle = item(lambda *terms: join(base, *terms, bias=out_bias, layer=layer, which=2), *terms)
                 gathered = gather(normed)
                 yield
                 lead, own = item(functools.partial(expand, layer=layer), gathered)
-                terms = yield from scatter_sum(lead, own, w_down[layer])
+                terms = yield from scatter_sum(lead, own, w_down, layer, 512)
                 if layer + 1 < layers:
                     seq_of[0] = seq
                     normed, base = item(lambda *terms: join(middle, *terms, bias=down_bias, layer=layer, which=4), *terms)

time: 1450 us -> 1360 us (0.938)
  Pallas kernels: 447 us -> 808 us
  matrix products: 349 us -> 0 us
  local copies, waits for them, and re-layouts: 99.1 us -> 25.2 us
  waiting for transfers between devices: 480 us -> 434 us
    pallas_call x0 -> x30, Pallas kernels: none -> 433 us  [the longest x24 274 us: project_rows(): pl.pallas_call(functools.partial(project_kernel, shards=table.shape[0] //...]
    dot_general x30 -> x0, matrix products: 349 us -> none  [the longest x6 140 us: expand(): jnp.dot(gathered, w_up[layer], preferred_element_type=jnp.float32)]
    pallas_call x6, Pallas kernels: 335 us -> 226 us  [attend(): pl.pallas_call(functools.partial(attention_kernel, seq=seq, group=group,...]
    unnamed x300 -> x106, local copies, waits for them, and re-layouts: 77.5 us -> 18.7 us
    ppermute x36, waiting for transfers between devices: 434 us -> 393 us  [send(): return lax.ppermute(value, 'tp', pairs)]
    pallas_call x12, Pallas kernels: 33.7 us -> 57.2 us  [normalize(): pl.pallas_call(functools.partial(norm_kernel, joined=terms is not None),...]
    slice x23 -> x0, local copies, waits for them, and re-layouts: 15.5 us -> none  [the longest x12 15.4 us: scatter_sum(): came = send(pair[2 * part:], pairs_first)]
  transfers between devices with their start and end apart: 48 -> 48, of which waited for: 19 -> 26; matrix products, arithmetic and copies ran while one was open for 24% -> 2% of each run, Pallas kernels for 26% -> 57%
where the time goes in v2:
time: 1360 us; the launch traced here: 1340 us
  Pallas kernels  808 us (59%)
  waiting for transfers between devices  434 us (32%)
  starting transfers between devices  34.6 us (3%)
  other arithmetic  28.5 us (2%)
  local copies, waits for them, and re-layouts  25.2 us (2%)
  between operations  14.9 us (1%)
    ppermute x36, waiting for transfers between devices, send(): return lax.ppermute(value, 'tp', pairs)  393 us
    pallas_call x24, Pallas kernels, project_rows(): pl.pallas_call(functools.partial(project_kernel, shards=table.shape[0] //...  274 us
    pallas_call x6, Pallas kernels, attend(): pl.pallas_call(functools.partial(attention_kernel, seq=seq, group=group,...  226 us
    pallas_call x6, Pallas kernels, expand_rows(): pl.pallas_call(expand_kernel, grid=(chunk // rows, width // cols), in_spe...  159 us
    pallas_call x6, Pallas kernels, qkv_project(): pl.pallas_call(qkv_kernel, grid=(chunk // rows,), in_specs=[row_block(mod...  75.3 us
    pallas_call x12, Pallas kernels, normalize(): pl.pallas_call(functools.partial(norm_kernel, joined=terms is not None),...  57.2 us
    all_gather x12, waiting for transfers between devices, gather(): return lax.all_gather(value, 'tp', axis=0, tiled=True)  40.3 us
    ppermute x36, starting transfers between devices, send(): return lax.ppermute(value, 'tp', pairs)  34.1 us
  transfers between devices with their start and end apart: 48, of which 26 were waited for; matrix products, arithmetic and copies ran while one was open for 2% of the time, Pallas kernels for 57%

profile of v2, /device:TPU:0, one launch (start us, length us, event | category | flops | bytes accessed | tf_op | source)
XLA Modules:
  0.0 1344.7 jit_solution(8444670879111239466)
XLA Ops:
  24.3 40.2 %all-gather.13.cloned.1.call-done.x_ref = bf16[1024,4096]{1,0:T(8,128)(2,1)} async-done(((bf16[128,4096]{1,0:T(8,128)(2,1)}), bf16[1024,4096]{1,0:T(8,128)(2,1)}) %all-gather.13.cloned.1.call-update) | async-done | bytes 8388624 | tf_op jit(solution)/shard_map/all_gather | solution.py:343
  76.7 37.6 %attend.6.acts_ref = bf16[1024,512]{1,0:T(8,128)(2,1)} custom-call(s32[3]{0:T(128)} %start_ref.13, bf16[1024,512]{1,0:T(8,128)(2,1)} %get-tuple-element.154.q_ref, bf16[1024,128]{1,0:T(8,128)(2,1)} %get-tuple-element.155.kn_ref, bf16[1024,128]{1,0:T(8,128)(2,1)} %get-tuple-element.156.vn_ref, bf16[2,3,4096,128]{3,2,1,0:T(8,128)(2,1)} %bitcast.47, ...), custom_call_target="tpu_custom_call" | custom-call | flops 21474836480 | bytes 4718592 | tf_op jit(solution)/shard_map/attend/pallas_call | solution.py:179
  149.2 38.1 %attend.7.acts_ref = bf16[1024,512]{1,0:T(8,128)(2,1)} custom-call(s32[3]{0:T(128)} %start_ref.13, bf16[1024,512]{1,0:T(8,128)(2,1)} %get-tuple-element.161.q_ref, bf16[1024,128]{1,0:T(8,128)(2,1)} %get-tuple-element.162.kn_ref, bf16[1024,128]{1,0:T(8,128)(2,1)} %get-tuple-element.163.vn_ref, bf16[2,3,4096,128]{3,2,1,0:T(8,128)(2,1)} %bitcast.48, ...), custom_call_target="tpu_custom_call" | custom-call | flops 21474836480 | bytes 4718592 | tf_op jit(solution)/shard_map/attend/pallas_call | solution.py:179
  195.7 25.0 %collective-permute-done.1.refs_2_ = bf16[256,4096]{1,0:T(8,128)(2,1)S(1)} collective-permute-done((bf16[256,4096]{1,0:T(8,128)(2,1)}, bf16[256,4096]{1,0:T(8,128)(2,1)S(1)}, u32[]{:S(2)}, u32[]{:S(2)}) %collective-permute-start.1) | collective-permute-done | bytes 2097184 | tf_op jit(solution)/shard_map/ppermute | solution.py:340
  255.2 37.6 %attend.8.acts_ref = bf16[1024,512]{1,0:T(8,128)(2,1)} custom-call(s32[3]{0:T(128)} %start_ref.13, bf16[1024,512]{1,0:T(8,128)(2,1)} %get-tuple-element.175.q_ref, bf16[1024,128]{1,0:T(8,128)(2,1)} %get-tuple-element.176.kn_ref, bf16[1024,128]{1,0:T(8,128)(2,1)} %get-tuple-element.177.vn_ref, bf16[2,3,4096,128]{3,2,1,0:T(8,128)(2,1)} %bitcast.49, ...), custom_call_target="tpu_custom_call" | custom-call | flops 21474836480 | bytes 4718592 | tf_op jit(solution)/shard_map/attend/pallas_call | solution.py:179
  301.2 25.1 %collective-permute-done.4.refs_2_ = bf16[256,4096]{1,0:T(8,128)(2,1)S(1)} collective-permute-done((bf16[256,4096]{1,0:T(8,128)(2,1)}, bf16[256,4096]{1,0:T(8,128)(2,1)S(1)}, u32[]{:S(2)}, u32[]{:S(2)}) %collective-permute-start.4) | collective-permute-done | bytes 2097184 | tf_op jit(solution)/shard_map/ppermute | solution.py:340
  350.3 26.5 %expand.6.acts_ref = bf16[1024,1792]{1,0:T(8,128)(2,1)} custom-call(bf16[1024,4096]{1,0:T(8,128)(2,1)} %all-gather.17.cloned.1.call-done.x_ref, bf16[2,4096,1792]{2,1,0:T(8,128)(2,1)} %weight_ref.57, bf16[2,1,1792]{2,1,0:T(2,128)(2,1)} %copy.47.bias_ref), custom_call_target="tpu_custom_call" | custom-call | flops 15032385536 | bytes 41418752 | tf_op jit(solution)/shard_map/expand/pallas_call | solution.py:241
  376.8 15.3 %project_rows.30 = bf16[512,4096]{1,0:T(8,128)(2,1)} custom-call(s32[8]{0:T(128)} %stack.113.table_ref, bf16[1024,1792]{1,0:T(8,128)(2,1)} %expand.6.acts_ref, bf16[2,1792,4096]{2,1,0:T(8,128)(2,1)} %weight_ref.59), custom_call_target="tpu_custom_call" | custom-call | flops 7516192768 | bytes 22544384 | tf_op jit(solution)/shard_map/project_rows/pallas_call | solution.py:223
  435.0 15.7 %project_rows.31 = (bf16[256,4096]{1,0:T(8,128)(2,1)}, bf16[256,4096]{1,0:T(8,128)(2,1)}) custom-call(s32[8]{0:T(128)} %stack.113.table_ref, bf16[1024,1792]{1,0:T(8,128)(2,1)} %expand.6.acts_ref, bf16[2,1792,4096]{2,1,0:T(8,128)(2,1)} %weight_ref.59, bf16[512,4096]{1,0:T(8,128)(2,1)} %collective-permute-done.7.refs_0_), custom_call_target="tpu_custom_call" | custom-call | flops 7516192768 | bytes 22544384 | tf_op jit(solution)/shard_map/project_rows/pallas_call | solution.py:223
  450.6 26.8 %expand.7.acts_ref = bf16[1024,1792]{1,0:T(8,128)(2,1)} custom-call(bf16[1024,4096]{1,0:T(8,128)(2,1)} %all-gather.21.cloned.1.call-done.x_ref, bf16[2,4096,1792]{2,1,0:T(8,128)(2,1)} %weight_ref.57, bf16[2,1,1792]{2,1,0:T(2,128)(2,1)} %copy.47.bias_ref), custom_call_target="tpu_custom_call" | custom-call | flops 15032385536 | bytes 41418752 | tf_op jit(solution)/shard_map/expand/pallas_call | solution.py:241
  500.0 15.4 %project_rows.33 = (bf16[256,4096]{1,0:T(8,128)(2,1)}, bf16[256,4096]{1,0:T(8,128)(2,1)}) custom-call(s32[8]{0:T(128)} %stack.113.table_ref, bf16[1024,1792]{1,0:T(8,128)(2,1)} %expand.7.acts_ref, bf16[2,1792,4096]{2,1,0:T(8,128)(2,1)} %weight_ref.59, bf16[512,4096]{1,0:T(8,128)(2,1)} %collective-permute-done.11.refs_0_), custom_call_target="tpu_custom_call" | custom-call | flops 7516192768 | bytes 22544384 | tf_op jit(solution)/shard_map/project_rows/pallas_call | solution.py:223
  543.6 52.5 %collective-permute-done.13.refs_2_ = bf16[256,4096]{1,0:T(8,128)(2,1)S(1)} collective-permute-done((bf16[256,4096]{1,0:T(8,128)(2,1)}, bf16[256,4096]{1,0:T(8,128)(2,1)S(1)}, u32[]{:S(2)}, u32[]{:S(2)}) %collective-permute-start.13) | collective-permute-done | bytes 2097184 | tf_op jit(solution)/shard_map/ppermute | solution.py:340
  597.4 26.0 %expand.8.acts_ref = bf16[1024,1792]{1,0:T(8,128)(2,1)} custom-call(bf16[1024,4096]{1,0:T(8,128)(2,1)} %all-gather.25.cloned.1.call-done.x_ref, bf16[2,4096,1792]{2,1,0:T(8,128)(2,1)} %weight_ref.57, bf16[2,1,1792]{2,1,0:T(2,128)(2,1)} %copy.47.bias_ref), custom_call_target="tpu_custom_call" | custom-call | flops 15032385536 | bytes 41418752 | tf_op jit(solution)/shard_map/expand/pallas_call | solution.py:241
  652.1 15.9 %project_rows.35 = (bf16[256,4096]{1,0:T(8,128)(2,1)}, bf16[256,4096]{1,0:T(8,128)(2,1)}) custom-call(s32[8]{0:T(128)} %stack.113.table_ref, bf16[1024,1792]{1,0:T(8,128)(2,1)} %expand.8.acts_ref, bf16[2,1792,4096]{2,1,0:T(8,128)(2,1)} %weight_ref.59, bf16[512,4096]{1,0:T(8,128)(2,1)} %collective-permute-done.14.refs_0_), custom_call_target="tpu_custom_call" | custom-call | flops 7516192768 | bytes 22544384 | tf_op jit(solution)/shard_map/project_rows/pallas_call | solution.py:223
  681.5 37.6 %attend.9.acts_ref = bf16[1024,512]{1,0:T(8,128)(2,1)} custom-call(s32[3]{0:T(128)} %start_ref.13, bf16[1024,512]{1,0:T(8,128)(2,1)} %get-tuple-element.219.q_ref, bf16[1024,128]{1,0:T(8,128)(2,1)} %get-tuple-element.220.kn_ref, bf16[1024,128]{1,0:T(8,128)(2,1)} %get-tuple-element.221.vn_ref, bf16[2,3,4096,128]{3,2,1,0:T(8,128)(2,1)} %bitcast.50, ...), custom_call_target="tpu_custom_call" | custom-call | flops 21474836480 | bytes 4718592 | tf_op jit(solution)/shard_map/attend/pallas_call | solution.py:179
  728.7 24.2 %collective-permute-done.17.refs_2_ = bf16[256,4096]{1,0:T(8,128)(2,1)S(1)} collective-permute-done((bf16[256,4096]{1,0:T(8,128)(2,1)}, bf16[256,4096]{1,0:T(8,128)(2,1)S(1)}, u32[]{:S(2)}, u32[]{:S(2)}) %collective-permute-start.17) | collective-permute-done | bytes 2097184 | tf_op jit(solution)/shard_map/ppermute | solution.py:340
  787.6 37.6 %attend.10.acts_ref = bf16[1024,512]{1,0:T(8,128)(2,1)} custom-call(s32[3]{0:T(128)} %start_ref.13, bf16[1024,512]{1,0:T(8,128)(2,1)} %get-tuple-element.234.q_ref, bf16[1024,128]{1,0:T(8,128)(2,1)} %get-tuple-element.235.kn_ref, bf16[1024,128]{1,0:T(8,128)(2,1)} %get-tuple-element.236.vn_ref, bf16[2,3,4096,128]{3,2,1,0:T(8,128)(2,1)} %bitcast.51, ...), custom_call_target="tpu_custom_call" | custom-call | flops 21474836480 | bytes 4718592 | tf_op jit(solution)/shard_map/attend/pallas_call | solution.py:179
  834.4 24.2 %collective-permute-done.18.refs_2_ = bf16[256,4096]{1,0:T(8,128)(2,1)S(1)} collective-permute-done((bf16[256,4096]{1,0:T(8,128)(2,1)}, bf16[256,4096]{1,0:T(8,128)(2,1)S(1)}, u32[]{:S(2)}, u32[]{:S(2)}) %collective-permute-start.18) | collective-permute-done | bytes 2097184 | tf_op jit(solution)/shard_map/ppermute | solution.py:340
  893.2 37.6 %attend.11.acts_ref = bf16[1024,512]{1,0:T(8,128)(2,1)} custom-call(s32[3]{0:T(128)} %start_ref.13, bf16[1024,512]{1,0:T(8,128)(2,1)} %get-tuple-element.247.q_ref, bf16[1024,128]{1,0:T(8,128)(2,1)} %get-tuple-element.248.kn_ref, bf16[1024,128]{1,0:T(8,128)(2,1)} %get-tuple-element.249.vn_ref, bf16[2,3,4096,128]{3,2,1,0:T(8,128)(2,1)} %bitcast.52, ...), custom_call_target="tpu_custom_call" | custom-call | flops 21474836480 | bytes 4718592 | tf_op jit(solution)/shard_map/attend/pallas_call | solution.py:179
  940.0 24.3 %collective-permute-done.23.refs_2_ = bf16[256,4096]{1,0:T(8,128)(2,1)S(1)} collective-permute-done((bf16[256,4096]{1,0:T(8,128)(2,1)}, bf16[256,4096]{1,0:T(8,128)(2,1)S(1)}, u32[]{:S(2)}, u32[]{:S(2)}) %collective-permute-start.23) | collective-permute-done | bytes 2097184 | tf_op jit(solution)/shard_map/ppermute | solution.py:340
  989.1 51.4 %collective-permute-done.24.refs_2_ = bf16[256,4096]{1,0:T(8,128)(2,1)S(1)} collective-permute-done((bf16[256,4096]{1,0:T(8,128)(2,1)}, bf16[256,4096]{1,0:T(8,128)(2,1)S(1)}, u32[]{:S(2)}, u32[]{:S(2)}) %collective-permute-start.24) | collective-permute-done | bytes 2097184 | tf_op jit(solution)/shard_map/ppermute | solution.py:340
  1042.5 26.2 %expand.9.acts_ref = bf16[1024,1792]{1,0:T(8,128)(2,1)} custom-call(bf16[1024,4096]{1,0:T(8,128)(2,1)} %all-gather.29.cloned.1.call-done.x_ref, bf16[2,4096,1792]{2,1,0:T(8,128)(2,1)} %weight_ref.57, bf16[2,1,1792]{2,1,0:T(2,128)(2,1)} %copy.47.bias_ref), custom_call_target="tpu_custom_call" | custom-call | flops 15032385536 | bytes 41418752 | tf_op jit(solution)/shard_map/expand/pallas_call | solution.py:241
  1068.7 15.1 %project_rows.42 = bf16[512,4096]{1,0:T(8,128)(2,1)} custom-call(s32[8]{0:T(128)} %stack.113.table_ref, bf16[1024,1792]{1,0:T(8,128)(2,1)} %expand.9.acts_ref, bf16[2,1792,4096]{2,1,0:T(8,128)(2,1)} %weight_ref.59), custom_call_target="tpu_custom_call" | custom-call | flops 7516192768 | bytes 22544384 | tf_op jit(solution)/shard_map/project_rows/pallas_call | solution.py:223
  1097.3 15.5 %project_rows.43 = (bf16[256,4096]{1,0:T(8,128)(2,1)}, bf16[256,4096]{1,0:T(8,128)(2,1)}) custom-call(s32[8]{0:T(128)} %stack.113.table_ref, bf16[1024,1792]{1,0:T(8,128)(2,1)} %expand.9.acts_ref, bf16[2,1792,4096]{2,1,0:T(8,128)(2,1)} %weight_ref.59, bf16[512,4096]{1,0:T(8,128)(2,1)} %collective-permute-done.26.refs_0_), custom_call_target="tpu_custom_call" | custom-call | flops 7516192768 | bytes 22544384 | tf_op jit(solution)/shard_map/project_rows/pallas_call | solution.py:223
  1112.8 27.5 %expand.10.acts_ref = bf16[1024,1792]{1,0:T(8,128)(2,1)} custom-call(bf16[1024,4096]{1,0:T(8,128)(2,1)} %all-gather.33.cloned.1.call-done.x_ref, bf16[2,4096,1792]{2,1,0:T(8,128)(2,1)} %weight_ref.57, bf16[2,1,1792]{2,1,0:T(2,128)(2,1)} %copy.47.bias_ref), custom_call_target="tpu_custom_call" | custom-call | flops 15032385536 | bytes 41418752 | tf_op jit(solution)/shard_map/expand/pallas_call | solution.py:241
  1162.9 15.4 %project_rows.45 = (bf16[256,4096]{1,0:T(8,128)(2,1)}, bf16[256,4096]{1,0:T(8,128)(2,1)}) custom-call(s32[8]{0:T(128)} %stack.113.table_ref, bf16[1024,1792]{1,0:T(8,128)(2,1)} %expand.10.acts_ref, bf16[2,1792,4096]{2,1,0:T(8,128)(2,1)} %weight_ref.59, bf16[512,4096]{1,0:T(8,128)(2,1)} %collective-permute-done.29.refs_0_), custom_call_target="tpu_custom_call" | custom-call | flops 7516192768 | bytes 22544384 | tf_op jit(solution)/shard_map/project_rows/pallas_call | solution.py:223
  1184.6 26.0 %expand.11.acts_ref = bf16[1024,1792]{1,0:T(8,128)(2,1)} custom-call(bf16[1024,4096]{1,0:T(8,128)(2,1)} %all-gather.35.cloned.1.call-done.x_ref, bf16[2,4096,1792]{2,1,0:T(8,128)(2,1)} %weight_ref.57, bf16[2,1,1792]{2,1,0:T(2,128)(2,1)} %copy.47.bias_ref), custom_call_target="tpu_custom_call" | custom-call | flops 15032385536 | bytes 41418752 | tf_op jit(solution)/shard_map/expand/pallas_call | solution.py:241
  1210.6 15.2 %project_rows.46 = bf16[512,4096]{1,0:T(8,128)(2,1)} custom-call(s32[8]{0:T(128)} %stack.113.table_ref, bf16[1024,1792]{1,0:T(8,128)(2,1)} %expand.11.acts_ref, bf16[2,1792,4096]{2,1,0:T(8,128)(2,1)} %weight_ref.59), custom_call_target="tpu_custom_call" | custom-call | flops 7516192768 | bytes 22544384 | tf_op jit(solution)/shard_map/project_rows/pallas_call | solution.py:223
  1228.7 23.4 %collective-permute-done.32 = bf16[256,4096]{1,0:T(8,128)(2,1)S(1)} collective-permute-done((bf16[256,4096]{1,0:T(8,128)(2,1)}, bf16[256,4096]{1,0:T(8,128)(2,1)S(1)}, u32[]{:S(2)}, u32[]{:S(2)}) %collective-permute-start.32) | collective-permute-done | bytes 2097184 | tf_op jit(solution)/shard_map/ppermute | solution.py:340
  1257.7 15.4 %project_rows.47 = (bf16[256,4096]{1,0:T(8,128)(2,1)}, bf16[256,4096]{1,0:T(8,128)(2,1)}) custom-call(s32[8]{0:T(128)} %stack.113.table_ref, bf16[1024,1792]{1,0:T(8,128)(2,1)} %expand.11.acts_ref, bf16[2,1792,4096]{2,1,0:T(8,128)(2,1)} %weight_ref.59, bf16[512,4096]{1,0:T(8,128)(2,1)} %collective-permute-done.31.refs_0_), custom_call_target="tpu_custom_call" | custom-call | flops 7516192768 | bytes 22544384 | tf_op jit(solution)/shard_map/project_rows/pallas_call | solution.py:223
  1283.4 27.2 %collective-permute-done.33 = bf16[256,4096]{1,0:T(8,128)(2,1)S(1)} collective-permute-done((bf16[256,4096]{1,0:T(8,128)(2,1)}, bf16[256,4096]{1,0:T(8,128)(2,1)S(1)}, u32[]{:S(2)}, u32[]{:S(2)}) %collective-permute-start.33) | collective-permute-done | bytes 2097184 | tf_op jit(solution)/shard_map/ppermute | solution.py:340
  1314.5 15.7 %write_caches.1 = (bf16[2,3,4096,128]{3,2,1,0:T(8,128)(2,1)}, bf16[2,3,4096,128]{3,2,1,0:T(8,128)(2,1)}) custom-call(s32[3]{0:T(128)} %start_ref.13, bf16[2,3,4096,128]{3,2,1,0:T(8,128)(2,1)} %bitcast.53, bf16[2,3,4096,128]{3,2,1,0:T(8,128)(2,1)} %bitcast.60, bf16[2,3,1024,128]{3,2,1,0:T(8,128)(2,1)} %get-tuple-element.310.kn_ref, ...), custom_call_target="tpu_custom_call" | custom-call | flops 16777216 | bytes 25165824 | tf_op jit(solution)/shard_map/write_caches/pallas_call | solution.py:281
  (270 shorter events, 472.4 us)
Async XLA Ops:
  7.2 57.4 %all-gather.13.cloned.1.call-start = ((), (), s32[]{:S(2)}) async-start(), calls=%async_computation | async-start | bytes 9437184 | tf_op jit(solution)/shard_map/all_gather | solution.py:343
  12.9 123.9 %all-gather.15.cloned.1.call-start = ((), (), s32[]{:S(2)}) async-start(), calls=%async_computation.1 | async-start | bytes 9437184 | tf_op jit(solution)/shard_map/all_gather | solution.py:343
  17.0 225.8 %all-gather.19.cloned.1.call-start = ((), (), s32[]{:S(2)}) async-start(), calls=%async_computation.3 | async-start | bytes 9437184 | tf_op jit(solution)/shard_map/all_gather | solution.py:343
  21.2 329.1 %all-gather.17.cloned.1.call-start = ((), (), s32[]{:S(2)}) async-start(), calls=%async_computation.2 | async-start | bytes 9437184 | tf_op jit(solution)/shard_map/all_gather | solution.py:343
  194.5 29.0 %collective-permute-start.3 = (bf16[512,4096]{1,0:T(8,128)(2,1)}, bf16[512,4096]{1,0:T(8,128)(2,1)}, u32[]{:S(2)}, u32[]{:S(2)}) collective-permute-start(bf16[512,4096]{1,0:T(8,128)(2,1)} %project_rows.26), channel_id=1, source_target_pairs={{0,1},{1,0},{2,3},{3,2},{4,5},{5,4},{6,7},{7,6}} | collective-permute-start | bytes 12582920 | tf_op jit(solution)/shard_map/ppermute | solution.py:340
  194.5 26.2 %collective-permute-start.1 = (bf16[256,4096]{1,0:T(8,128)(2,1)}, bf16[256,4096]{1,0:T(8,128)(2,1)S(1)}, u32[]{:S(2)}, u32[]{:S(2)}) collective-permute-start(bf16[256,4096]{1,0:T(8,128)(2,1)} %get-tuple-element.159), channel_id=1, source_target_pairs={{0,2},{1,5},{2,0},{3,7},{4,6},{5,1},{6,4},{7,3}} | collective-permute-start | bytes 6291464 | tf_op jit(solution)/shard_map/ppermute | solution.py:340
  242.8 207.8 %all-gather.21.cloned.1.call-start = ((), (), s32[]{:S(2)}) async-start(), calls=%async_computation.4 | async-start | bytes 9437184 | tf_op jit(solution)/shard_map/all_gather | solution.py:343
  300.0 28.3 %collective-permute-start.6 = (bf16[512,4096]{1,0:T(8,128)(2,1)}, bf16[512,4096]{1,0:T(8,128)(2,1)}, u32[]{:S(2)}, u32[]{:S(2)}) collective-permute-start(bf16[512,4096]{1,0:T(8,128)(2,1)} %project_rows.28), channel_id=1, source_target_pairs={{0,1},{1,0},{2,3},{3,2},{4,5},{5,4},{6,7},{7,6}} | collective-permute-start | bytes 12582920 | tf_op jit(solution)/shard_map/ppermute | solution.py:340
  300.0 26.2 %collective-permute-start.4 = (bf16[256,4096]{1,0:T(8,128)(2,1)}, bf16[256,4096]{1,0:T(8,128)(2,1)S(1)}, u32[]{:S(2)}, u32[]{:S(2)}) collective-permute-start(bf16[256,4096]{1,0:T(8,128)(2,1)} %get-tuple-element.173), channel_id=1, source_target_pairs={{0,2},{1,5},{2,0},{3,7},{4,6},{5,1},{6,4},{7,3}} | collective-permute-start | bytes 6291464 | tf_op jit(solution)/shard_map/ppermute | solution.py:340
  348.4 249.0 %all-gather.25.cloned.1.call-start = ((), (), s32[]{:S(2)}) async-start(), calls=%async_computation.6 | async-start | bytes 9437184 | tf_op jit(solution)/shard_map/all_gather | solution.py:343
  349.1 56.0 %collective-permute-start.8 = (bf16[256,4096]{1,0:T(8,128)(2,1)}, bf16[256,4096]{1,0:T(8,128)(2,1)}, u32[]{:S(2)}, u32[]{:S(2)}) collective-permute-start(bf16[256,4096]{1,0:T(8,128)(2,1)} %get-tuple-element.187), channel_id=1, source_target_pairs={{0,2},{1,5},{2,0},{3,7},{4,6},{5,1},{6,4},{7,3}} | collective-permute-start | bytes 6291464 | tf_op jit(solution)/shard_map/ppermute | solution.py:340
  427.4 240.6 %all-gather.23.cloned.1.call-start = ((), (), s32[]{:S(2)}) async-start(), calls=%async_computation.5 | async-start | bytes 9437184 | tf_op jit(solution)/shard_map/all_gather | solution.py:343
  492.9 26.4 %collective-permute-start.10 = (bf16[256,4096]{1,0:T(8,128)(2,1)}, bf16[256,4096]{1,0:T(8,128)(2,1)}, u32[]{:S(2)}, u32[]{:S(2)}) collective-permute-start(bf16[256,4096]{1,0:T(8,128)(2,1)} %get-tuple-element.196), channel_id=1, source_target_pairs={{0,2},{1,5},{2,0},{3,7},{4,6},{5,1},{6,4},{7,3}} | collective-permute-start | bytes 6291464 | tf_op jit(solution)/shard_map/ppermute | solution.py:340
  541.7 233.4 %all-gather.27.cloned.1.call-start = ((), (), s32[]{:S(2)}) async-start(), calls=%async_computation.7 | async-start | bytes 9437184 | tf_op jit(solution)/shard_map/all_gather | solution.py:343
  541.7 54.4 %collective-permute-start.13 = (bf16[256,4096]{1,0:T(8,128)(2,1)}, bf16[256,4096]{1,0:T(8,128)(2,1)S(1)}, u32[]{:S(2)}, u32[]{:S(2)}) collective-permute-start(bf16[256,4096]{1,0:T(8,128)(2,1)} %get-tuple-element.207), channel_id=1, source_target_pairs={{0,2},{1,5},{2,0},{3,7},{4,6},{5,1},{6,4},{7,3}} | collective-permute-start | bytes 6291464 | tf_op jit(solution)/shard_map/ppermute | solution.py:340
  597.4 41.1 %collective-permute-start.15 = (bf16[128,4096]{1,0:T(8,128)(2,1)S(1)}, bf16[128,4096]{1,0:T(8,128)(2,1)S(1)}, u32[]{:S(2)}, u32[]{:S(2)}) collective-permute-start(bf16[128,4096]{1,0:T(8,128)(2,1)S(1)} %add_convert_fusion.10), channel_id=1, source_target_pairs={{0,4},{1,3},{2,6},{3,1},{4,0},{5,7},{6,2},{7,5}} | collective-permute-start | bytes 3145736 | tf_op jit(solution)/shard_map/ppermute | solution.py:340
  644.5 236.3 %all-gather.31.cloned.1.call-start = ((), (), s32[]{:S(2)}) async-start(), calls=%async_computation.9 | async-start | bytes 9437184 | tf_op jit(solution)/shard_map/all_gather | solution.py:343
  726.2 29.8 %collective-permute-start.16 = (bf16[512,4096]{1,0:T(8,128)(2,1)}, bf16[512,4096]{1,0:T(8,128)(2,1)}, u32[]{:S(2)}, u32[]{:S(2)}) collective-permute-start(bf16[512,4096]{1,0:T(8,128)(2,1)} %project_rows.36), channel_id=1, source_target_pairs={{0,1},{1,0},{2,3},{3,2},{4,5},{5,4},{6,7},{7,6}} | collective-permute-start | bytes 12582920 | tf_op jit(solution)/shard_map/ppermute | solution.py:340
  726.6 26.3 %collective-permute-start.17 = (bf16[256,4096]{1,0:T(8,128)(2,1)}, bf16[256,4096]{1,0:T(8,128)(2,1)S(1)}, u32[]{:S(2)}, u32[]{:S(2)}) collective-permute-start(bf16[256,4096]{1,0:T(8,128)(2,1)} %get-tuple-element.222), channel_id=1, source_target_pairs={{0,2},{1,5},{2,0},{3,7},{4,6},{5,1},{6,4},{7,3}} | collective-permute-start | bytes 6291464 | tf_op jit(solution)/shard_map/ppermute | solution.py:340
  775.0 267.5 %all-gather.29.cloned.1.call-start = ((), (), s32[]{:S(2)}) async-start(), calls=%async_computation.8 | async-start | bytes 9437184 | tf_op jit(solution)/shard_map/all_gather | solution.py:343
  832.4 29.4 %collective-permute-start.21 = (bf16[512,4096]{1,0:T(8,128)(2,1)}, bf16[512,4096]{1,0:T(8,128)(2,1)}, u32[]{:S(2)}, u32[]{:S(2)}) collective-permute-start(bf16[512,4096]{1,0:T(8,128)(2,1)} %project_rows.38), channel_id=1, source_target_pairs={{0,1},{1,0},{2,3},{3,2},{4,5},{5,4},{6,7},{7,6}} | collective-permute-start | bytes 12582920 | tf_op jit(solution)/shard_map/ppermute | solution.py:340
  832.4 26.2 %collective-permute-start.18 = (bf16[256,4096]{1,0:T(8,128)(2,1)}, bf16[256,4096]{1,0:T(8,128)(2,1)S(1)}, u32[]{:S(2)}, u32[]{:S(2)}) collective-permute-start(bf16[256,4096]{1,0:T(8,128)(2,1)} %get-tuple-element.227), channel_id=1, source_target_pairs={{0,2},{1,5},{2,0},{3,7},{4,6},{5,1},{6,4},{7,3}} | collective-permute-start | bytes 6291464 | tf_op jit(solution)/shard_map/ppermute | solution.py:340
  880.8 232.0 %all-gather.33.cloned.1.call-start = ((), (), s32[]{:S(2)}) async-start(), calls=%async_computation.10 | async-start | bytes 9437184 | tf_op jit(solution)/shard_map/all_gather | solution.py:343
  938.0 29.7 %collective-permute-start.22 = (bf16[512,4096]{1,0:T(8,128)(2,1)}, bf16[512,4096]{1,0:T(8,128)(2,1)}, u32[]{:S(2)}, u32[]{:S(2)}) collective-permute-start(bf16[512,4096]{1,0:T(8,128)(2,1)} %project_rows.40), channel_id=1, source_target_pairs={{0,1},{1,0},{2,3},{3,2},{4,5},{5,4},{6,7},{7,6}} | collective-permute-start | bytes 12582920 | tf_op jit(solution)/shard_map/ppermute | solution.py:340
  987.0 197.6 %all-gather.35.cloned.1.call-start = ((), (), s32[]{:S(2)}) async-start(), calls=%async_computation.11 | async-start | bytes 9437184 | tf_op jit(solution)/shard_map/all_gather | solution.py:343
  987.1 53.5 %collective-permute-start.24 = (bf16[256,4096]{1,0:T(8,128)(2,1)}, bf16[256,4096]{1,0:T(8,128)(2,1)S(1)}, u32[]{:S(2)}, u32[]{:S(2)}) collective-permute-start(bf16[256,4096]{1,0:T(8,128)(2,1)} %get-tuple-element.255), channel_id=1, source_target_pairs={{0,2},{1,5},{2,0},{3,7},{4,6},{5,1},{6,4},{7,3}} | collective-permute-start | bytes 6291464 | tf_op jit(solution)/shard_map/ppermute | solution.py:340
  1041.9 41.9 %collective-permute-start.27 = (bf16[128,4096]{1,0:T(8,128)(2,1)S(1)}, bf16[128,4096]{1,0:T(8,128)(2,1)S(1)}, u32[]{:S(2)}, u32[]{:S(2)}) collective-permute-start(bf16[128,4096]{1,0:T(8,128)(2,1)S(1)} %add_convert_fusion.6), channel_id=1, source_target_pairs={{0,4},{1,3},{2,6},{3,1},{4,0},{5,7},{6,2},{7,5}} | collective-permute-start | bytes 3145736 | tf_op jit(solution)/shard_map/ppermute | solution.py:340
  1155.7 26.4 %collective-permute-start.28 = (bf16[256,4096]{1,0:T(8,128)(2,1)}, bf16[256,4096]{1,0:T(8,128)(2,1)}, u32[]{:S(2)}, u32[]{:S(2)}) collective-permute-start(bf16[256,4096]{1,0:T(8,128)(2,1)} %get-tuple-element.271), channel_id=1, source_target_pairs={{0,2},{1,5},{2,0},{3,7},{4,6},{5,1},{6,4},{7,3}} | collective-permute-start | bytes 6291464 | tf_op jit(solution)/shard_map/ppermute | solution.py:340
  1225.8 31.8 %collective-permute-start.31 = (bf16[512,4096]{1,0:T(8,128)(2,1)}, bf16[512,4096]{1,0:T(8,128)(2,1)}, u32[]{:S(2)}, u32[]{:S(2)}) collective-permute-start(bf16[512,4096]{1,0:T(8,128)(2,1)} %project_rows.46), channel_id=1, source_target_pairs={{0,1},{1,0},{2,3},{3,2},{4,5},{5,4},{6,7},{7,6}} | collective-permute-start | bytes 12582920 | tf_op jit(solution)/shard_map/ppermute | solution.py:340
  1225.9 26.2 %collective-permute-start.32 = (bf16[256,4096]{1,0:T(8,128)(2,1)}, bf16[256,4096]{1,0:T(8,128)(2,1)S(1)}, u32[]{:S(2)}, u32[]{:S(2)}) collective-permute-start(bf16[256,4096]{1,0:T(8,128)(2,1)} %get-tuple-element.278), channel_id=1, source_target_pairs={{0,2},{1,5},{2,0},{3,7},{4,6},{5,1},{6,4},{7,3}} | collective-permute-start | bytes 6291464 | tf_op jit(solution)/shard_map/ppermute | solution.py:340
  1273.1 37.5 %collective-permute-start.33 = (bf16[256,4096]{1,0:T(8,128)(2,1)}, bf16[256,4096]{1,0:T(8,128)(2,1)S(1)}, u32[]{:S(2)}, u32[]{:S(2)}) collective-permute-start(bf16[256,4096]{1,0:T(8,128)(2,1)} %get-tuple-element.283), channel_id=1, source_target_pairs={{0,2},{1,5},{2,0},{3,7},{4,6},{5,1},{6,4},{7,3}} | collective-permute-start | bytes 6291464 | tf_op jit(solution)/shard_map/ppermute | solution.py:340
  1279.9 50.4 %collective-permute-start.30 = (bf16[128,4096]{1,0:T(8,128)(2,1)}, bf16[128,4096]{1,0:T(8,128)(2,1)}, u32[]{:S(2)}, u32[]{:S(2)}) collective-permute-start(bf16[128,4096]{1,0:T(8,128)(2,1)} %add_convert_fusion.5), channel_id=1, source_target_pairs={{0,4},{1,3},{2,6},{3,1},{4,0},{5,7},{6,2},{7,5}} | collective-permute-start | bytes 3145736 | tf_op jit(solution)/shard_map/ppermute | solution.py:340
  (69 other events, 856.8 us)
Sparse Core Ops, SparseCore 0:
  13.0 51.4 all-gather.12
  66.9 48.7 all-gather.14
  117.5 48.6 all-gather.18
  242.9 48.4 all-gather.16
  348.5 65.8 all-gather.20
  427.5 49.6 all-gather.24
  541.8 67.1 all-gather.22
  644.7 51.1 all-gather.26
  775.1 50.2 all-gather.30
  880.9 50.2 all-gather.28
  987.2 66.8 all-gather.32
  1089.9 50.5 all-gather.34

commit v3 on v2

--- a/solution.py
+++ b/solution.py
@@ -31,7 +31,7 @@
     norm_ref[...] = (scaled * gain_ref[...].astype(jnp.float32) + shift_ref[...].astype(jnp.float32)).astype(jnp.bfloat16)
 
 
-def normalize(base, seq, terms, bias, norms, layer, which, rows=32):
+def normalize(base, seq, terms, bias, norms, layer, which, rows=64):
     part, model = base.shape[-2:]
     line = pl.BlockSpec((rows, model), lambda i: (i, 0))
     first = line if base.ndim == 2 else pl.BlockSpec((None, rows, model), lambda i: (seq, i, 0))
@@ -192,12 +192,32 @@
     )(start_pos, query, key_new, value_new, key_cache, value_cache, held)
 
 
-def project_kernel(table_ref, acts_ref, weight_ref, *refs, shards, joined):
-    part = acts_ref.shape[0] // table_ref.shape[0]
-    first = shards if joined is None else 0
-    rows = [acts_ref[pl.ds(pl.multiple_of(table_ref[first + i] * part, part), part), :] for i in range(shards)]
-    total = jnp.dot(jnp.concatenate(rows, axis=0), weight_ref[...], preferred_element_type=jnp.float32)
-    if joined is None:
+def stream_tile(weight_ref, ring_ref, sem_ref, step, steps, layer, tiles):
+    slots, _, cols = ring_ref.shape
+
+    def copy(at):
+        slot = lax.rem(at, slots)
+        columns = pl.ds(pl.multiple_of(lax.rem(at, tiles) * cols, cols), cols)
+        return pltpu.make_async_copy(weight_ref.at[layer, :, columns], ring_ref.at[slot], sem_ref.at[slot])
+
+    @pl.when(step == 0)
+    def _():
+        for i in range(min(slots - 1, steps)):
+            copy(jnp.int32(i)).start()
+
+    @pl.when(step + slots - 1 < steps)
+    def _():
+        copy(step + slots - 1).start()
+
+    copy(step).wait()
+    return ring_ref[lax.rem(step, slots)]
+
+
+def project_kernel(table_ref, *refs, shards, joined, layer, steps):
+    acts_refs, (weight_ref, *refs), (ring_ref, sem_ref) = refs[:shards], refs[shards:-2], refs[-2:]
+    weight = stream_tile(weight_ref, ring_ref, sem_ref, pl.program_id(0), steps, layer, steps)
+    total = jnp.dot(jnp.concatenate([ref[...] for ref in acts_refs], axis=0), weight, preferred_element_type=jnp.float32)
+    if not joined:
         refs[0][...] = total.astype(jnp.bfloat16)
     else:
         lead_ref, kept_ref, sent_ref = refs
@@ -206,14 +226,18 @@
         sent_ref[...] = total[total.shape[0] // 2:]
 
 
-def project_rows(table, acts, weight, layer, lead, cols):
+def project_rows(table, acts, weight, layer, lead, cols, slots=4):
     chunk, depth = acts.shape
     model = weight.shape[2]
     half = chunk // 2
+    shards = table.shape[0] // 2
+    part = half // shards
+    first = shards if lead is None else 0
     out = lambda rows: pl.BlockSpec((rows, cols), lambda i, *_: (0, i))
     shape = lambda rows: jax.ShapeDtypeStruct((rows, model), jnp.bfloat16)
-    in_specs = [pl.BlockSpec((chunk, depth), lambda i, *_: (0, 0)), pl.BlockSpec((None, depth, cols), lambda i, *_: (layer, 0, i))]
-    args = [table, acts, weight]
+    shard = lambda at: pl.BlockSpec((part, depth), lambda i, places: (places[at], 0))
+    in_specs = [shard(first + k) for k in range(shards)] + [pl.BlockSpec(memory_space=pl.ANY)]
+    args = [table] + [acts] * shards + [weight]
     if lead is None:
         out_specs, out_shape = [out(half)], [shape(half)]
     else:
@@ -221,31 +245,41 @@
         args.append(lead)
         out_specs, out_shape = [out(half // 2)] * 2, [shape(half // 2)] * 2
     return pl.pallas_call(
-        functools.partial(project_kernel, shards=table.shape[0] // 2, joined=None if lead is None else True),
-        grid_spec=pltpu.PrefetchScalarGridSpec(num_scalar_prefetch=1, grid=(model // cols,), in_specs=in_specs, out_specs=out_specs),
+        functools.partial(project_kernel, shards=shards, joined=lead is not None, layer=layer, steps=model // cols),
+        grid_spec=pltpu.PrefetchScalarGridSpec(
+            num_scalar_prefetch=1,
+            grid=(model // cols,),
+            in_specs=in_specs,
+            out_specs=out_specs,
+            scratch_shapes=[pltpu.VMEM((slots, depth, cols), jnp.bfloat16), pltpu.SemaphoreType.DMA((slots,))],
+        ),
         out_shape=out_shape,
         compiler_params=pltpu.CompilerParams(dimension_semantics=('arbitrary',), vmem_limit_bytes=VMEM_LIMIT),
-        cost_estimate=pl.CostEstimate(flops=2 * half * depth * model, bytes_accessed=2 * (chunk * depth + depth * model + half * model), transcendentals=0),
+        cost_estimate=pl.CostEstimate(flops=2 * half * depth * model, bytes_accessed=2 * (half * depth + depth * model + half * model), transcendentals=0),
         name='project_rows',
     )(*args)
 
 
-def expand_kernel(x_ref, weight_ref, bias_ref, out_ref):
-    lifted = jnp.dot(x_ref[...], weight_ref[...], preferred_element_type=jnp.float32) + bias_ref[...].astype(jnp.float32)
+def expand_kernel(x_ref, weight_ref, bias_ref, out_ref, ring_ref, sem_ref, *, layer, blocks, tiles):
+    step = pl.program_id(0) * tiles + pl.program_id(1)
+    weight = stream_tile(weight_ref, ring_ref, sem_ref, step, blocks * tiles, layer, tiles)
+    lifted = jnp.dot(x_ref[...], weight, preferred_element_type=jnp.float32) + bias_ref[...].astype(jnp.float32)
     out_ref[...] = jax.nn.gelu(lifted, approximate=True).astype(jnp.bfloat16)
 
 
-def expand_rows(acts, weight, bias, layer, rows=512, cols=256):
+def expand_rows(acts, weight, bias, layer, rows=512, cols=256, slots=4):
     chunk, model = acts.shape
     width = weight.shape[2]
-    return pl.pallas_call(
-        expand_kernel,
-        grid=(chunk // rows, width // cols),
-        in_specs=[pl.BlockSpec((rows, model), lambda i, j: (i, 0)), pl.BlockSpec((None, model, cols), lambda i, j: (layer, 0, j)), pl.BlockSpec((None, 1, cols), lambda i, j: (layer, 0, j))],
+    blocks, tiles = chunk // rows, width // cols
+    return pl.pallas_call(
+        functools.partial(expand_kernel, layer=layer, blocks=blocks, tiles=tiles),
+        grid=(blocks, tiles),
+        in_specs=[pl.BlockSpec((rows, model), lambda i, j: (i, 0)), pl.BlockSpec(memory_space=pl.ANY), pl.BlockSpec((None, 1, cols), lambda i, j: (layer, 0, j))],
         out_specs=pl.BlockSpec((rows, cols), lambda i, j: (i, j)),
+        scratch_shapes=[pltpu.VMEM((slots, model, cols), jnp.bfloat16), pltpu.SemaphoreType.DMA((slots,))],
         out_shape=jax.ShapeDtypeStruct((chunk, width), jnp.bfloat16),
         compiler_params=pltpu.CompilerParams(dimension_semantics=('arbitrary', 'arbitrary'), vmem_limit_bytes=VMEM_LIMIT),
-        cost_estimate=pl.CostEstimate(flops=2 * chunk * model * width, bytes_accessed=2 * (chunk * model + 2 * model * width + chunk * width), transcendentals=0),
+        cost_estimate=pl.CostEstimate(flops=2 * chunk * model * width, bytes_accessed=2 * (chunk * model + blocks * model * width + chunk * width), transcendentals=0),
         name='expand',
     )(acts, weight, bias)
 

time: 1360 us -> 1330 us (0.978)
  Pallas kernels: 808 us -> 777 us
    pallas_call x30, Pallas kernels: 433 us -> 412 us  [the longest x24 261 us: project_rows(): pl.pallas_call(functools.partial(project_kernel, shards=shards, joined=le...]
  transfers between devices with their start and end apart: 48 -> 48, of which waited for: 26 -> 26; matrix products, arithmetic and copies ran while one was open for 2% -> 2% of each run, Pallas kernels for 57% -> 56%
where the time goes in v3:
time: 1330 us; the launch traced here: 1320 us
  Pallas kernels  777 us (58%)
  waiting for transfers between devices  439 us (33%)
  starting transfers between devices  38.3 us (3%)
  other arithmetic  28.5 us (2%)
  local copies, waits for them, and re-layouts  25.2 us (2%)
  between operations  15.3 us (1%)
    ppermute x36, waiting for transfers between devices, send(): return lax.ppermute(value, 'tp', pairs)  396 us
    pallas_call x24, Pallas kernels, project_rows(): pl.pallas_call(functools.partial(project_kernel, shards=shards, joined=le...  261 us
    pallas_call x6, Pallas kernels, attend(): pl.pallas_call(functools.partial(attention_kernel, seq=seq, group=group,...  226 us
    pallas_call x6, Pallas kernels, expand_rows(): pl.pallas_call(functools.partial(expand_kernel, layer=layer, blocks=block...  151 us
    pallas_call x6, Pallas kernels, qkv_project(): pl.pallas_call(qkv_kernel, grid=(chunk // rows,), in_specs=[row_block(mod...  75.6 us
    pallas_call x12, Pallas kernels, normalize(): pl.pallas_call(functools.partial(norm_kernel, joined=terms is not None),...  47.4 us
    all_gather x12, waiting for transfers between devices, gather(): return lax.all_gather(value, 'tp', axis=0, tiled=True)  42.6 us
    ppermute x36, starting transfers between devices, send(): return lax.ppermute(value, 'tp', pairs)  37.8 us
  transfers between devices with their start and end apart: 48, of which 26 were waited for; matrix products, arithmetic and copies ran while one was open for 2% of the time, Pallas kernels for 56%

profile of v3, /device:TPU:0, one launch (start us, length us, event | category | flops | bytes accessed | tf_op | source)
XLA Modules:
  0.0 1323.4 jit_solution(4286894930150523217)
XLA Ops:
  21.0 42.4 %all-gather.13.cloned.1.call-done.x_ref = bf16[1024,4096]{1,0:T(8,128)(2,1)} async-done(((bf16[128,4096]{1,0:T(8,128)(2,1)}), bf16[1024,4096]{1,0:T(8,128)(2,1)}) %all-gather.13.cloned.1.call-update) | async-done | bytes 8388624 | tf_op jit(solution)/shard_map/all_gather | solution.py:377
  75.6 37.6 %attend.6.refs_0_.refs_1_.refs_2_.refs_3_ = bf16[1024,512]{1,0:T(8,128)(2,1)} custom-call(s32[3]{0:T(128)} %start_ref.13, bf16[1024,512]{1,0:T(8,128)(2,1)} %get-tuple-element.154.q_ref, bf16[1024,128]{1,0:T(8,128)(2,1)} %get-tuple-element.155.kn_ref, bf16[1024,128]{1,0:T(8,128)(2,1)} %get-tuple-element.156.vn_ref, bf16[2,3,4096,128]{3,2,1,0:T(8,128)(2,1)} %bitcast.47, ...), custom_call_target="tpu_custom_call" | custom-call | flops 21474836480 | bytes 4718592 | tf_op jit(solution)/shard_map/attend/pallas_call | solution.py:179
  149.0 37.8 %attend.7.refs_0_.refs_1_.refs_2_.refs_3_ = bf16[1024,512]{1,0:T(8,128)(2,1)} custom-call(s32[3]{0:T(128)} %start_ref.13, bf16[1024,512]{1,0:T(8,128)(2,1)} %get-tuple-element.161.q_ref, bf16[1024,128]{1,0:T(8,128)(2,1)} %get-tuple-element.162.kn_ref, bf16[1024,128]{1,0:T(8,128)(2,1)} %get-tuple-element.163.vn_ref, bf16[2,3,4096,128]{3,2,1,0:T(8,128)(2,1)} %bitcast.48, ...), custom_call_target="tpu_custom_call" | custom-call | flops 21474836480 | bytes 4718592 | tf_op jit(solution)/shard_map/attend/pallas_call | solution.py:179
  195.4 25.0 %collective-permute-done.1.refs_2_ = bf16[256,4096]{1,0:T(8,128)(2,1)S(1)} collective-permute-done((bf16[256,4096]{1,0:T(8,128)(2,1)}, bf16[256,4096]{1,0:T(8,128)(2,1)S(1)}, u32[]{:S(2)}, u32[]{:S(2)}) %collective-permute-start.1) | collective-permute-done | bytes 2097184 | tf_op jit(solution)/shard_map/ppermute | solution.py:374
  254.3 37.6 %attend.8.refs_0_.refs_1_.refs_2_.refs_3_ = bf16[1024,512]{1,0:T(8,128)(2,1)} custom-call(s32[3]{0:T(128)} %start_ref.13, bf16[1024,512]{1,0:T(8,128)(2,1)} %get-tuple-element.175.q_ref, bf16[1024,128]{1,0:T(8,128)(2,1)} %get-tuple-element.176.kn_ref, bf16[1024,128]{1,0:T(8,128)(2,1)} %get-tuple-element.177.vn_ref, bf16[2,3,4096,128]{3,2,1,0:T(8,128)(2,1)} %bitcast.49, ...), custom_call_target="tpu_custom_call" | custom-call | flops 21474836480 | bytes 4718592 | tf_op jit(solution)/shard_map/attend/pallas_call | solution.py:179
  300.4 25.1 %collective-permute-done.4.refs_2_ = bf16[256,4096]{1,0:T(8,128)(2,1)S(1)} collective-permute-done((bf16[256,4096]{1,0:T(8,128)(2,1)}, bf16[256,4096]{1,0:T(8,128)(2,1)S(1)}, u32[]{:S(2)}, u32[]{:S(2)}) %collective-permute-start.4) | collective-permute-done | bytes 2097184 | tf_op jit(solution)/shard_map/ppermute | solution.py:374
  348.8 25.6 %expand.6.refs_0_.refs_1_.refs_2_.refs_3_ = bf16[1024,1792]{1,0:T(8,128)(2,1)} custom-call(bf16[1024,4096]{1,0:T(8,128)(2,1)} %all-gather.17.cloned.1.call-done.x_ref, bf16[2,4096,1792]{2,1,0:T(8,128)(2,1)} %weight_ref.11, bf16[2,1,1792]{2,1,0:T(2,128)(2,1)} %copy.47.bias_ref), custom_call_target="tpu_custom_call" | custom-call | flops 15032385536 | bytes 41418752 | tf_op jit(solution)/shard_map/expand/pallas_call | solution.py:274
  374.4 14.5 %project_rows.30 = bf16[512,4096]{1,0:T(8,128)(2,1)} custom-call(s32[8]{0:T(128)} %stack.113.table_ref, bf16[1024,1792]{1,0:T(8,128)(2,1)} %expand.6.refs_0_.refs_1_.refs_2_.refs_3_, bf16[1024,1792]{1,0:T(8,128)(2,1)} %expand.6.refs_0_.refs_1_.refs_2_.refs_3_, bf16[1024,1792]{1,0:T(8,128)(2,1)} %expand.6.refs_0_.refs_1_.refs_2_.refs_3_, ...), custom_call_target="tpu_custom_call" | custom-call | flops 7516192768 | bytes 20709376 | tf_op jit(solution)/shard_map/project_rows/pallas_call | solution.py:247
  388.9 14.7 %collective-permute-done.8.refs_2_ = bf16[256,4096]{1,0:T(8,128)(2,1)} collective-permute-done((bf16[256,4096]{1,0:T(8,128)(2,1)}, bf16[256,4096]{1,0:T(8,128)(2,1)}, u32[]{:S(2)}, u32[]{:S(2)}) %collective-permute-start.8) | collective-permute-done | bytes 2097184 | tf_op jit(solution)/shard_map/ppermute | solution.py:374
  405.1 14.8 %collective-permute-done.9.refs_3_ = bf16[128,4096]{1,0:T(8,128)(2,1)S(1)} collective-permute-done((bf16[128,4096]{1,0:T(8,128)(2,1)S(1)}, bf16[128,4096]{1,0:T(8,128)(2,1)S(1)}, u32[]{:S(2)}, u32[]{:S(2)}) %collective-permute-start.9) | collective-permute-done | bytes 1048608 | tf_op jit(solution)/shard_map/ppermute | solution.py:374
  432.8 14.2 %project_rows.31 = (bf16[256,4096]{1,0:T(8,128)(2,1)}, bf16[256,4096]{1,0:T(8,128)(2,1)}) custom-call(s32[8]{0:T(128)} %stack.113.table_ref, bf16[1024,1792]{1,0:T(8,128)(2,1)} %expand.6.refs_0_.refs_1_.refs_2_.refs_3_, bf16[1024,1792]{1,0:T(8,128)(2,1)} %expand.6.refs_0_.refs_1_.refs_2_.refs_3_, bf16[1024,1792]{1,0:T(8,128)(2,1)} %expand.6.refs_0_.refs_1_.refs_2_.refs_3_, ...), custom_call_target="tpu_custom_call" | custom-call | flops 7516192768 | bytes 20709376 | tf_op jit(solution)/shard_map/project_rows/pallas_call | solution.py:247
  447.0 25.4 %expand.7.refs_0_.refs_1_.refs_2_.refs_3_ = bf16[1024,1792]{1,0:T(8,128)(2,1)} custom-call(bf16[1024,4096]{1,0:T(8,128)(2,1)} %all-gather.21.cloned.1.call-done.x_ref, bf16[2,4096,1792]{2,1,0:T(8,128)(2,1)} %weight_ref.11, bf16[2,1,1792]{2,1,0:T(2,128)(2,1)} %copy.47.bias_ref), custom_call_target="tpu_custom_call" | custom-call | flops 15032385536 | bytes 41418752 | tf_op jit(solution)/shard_map/expand/pallas_call | solution.py:274
  493.8 14.2 %project_rows.33 = (bf16[256,4096]{1,0:T(8,128)(2,1)}, bf16[256,4096]{1,0:T(8,128)(2,1)}) custom-call(s32[8]{0:T(128)} %stack.113.table_ref, bf16[1024,1792]{1,0:T(8,128)(2,1)} %expand.7.refs_0_.refs_1_.refs_2_.refs_3_, bf16[1024,1792]{1,0:T(8,128)(2,1)} %expand.7.refs_0_.refs_1_.refs_2_.refs_3_, bf16[1024,1792]{1,0:T(8,128)(2,1)} %expand.7.refs_0_.refs_1_.refs_2_.refs_3_, ...), custom_call_target="tpu_custom_call" | custom-call | flops 7516192768 | bytes 20709376 | tf_op jit(solution)/shard_map/project_rows/pallas_call | solution.py:247
  537.6 54.0 %collective-permute-done.13.refs_2_ = bf16[256,4096]{1,0:T(8,128)(2,1)S(1)} collective-permute-done((bf16[256,4096]{1,0:T(8,128)(2,1)}, bf16[256,4096]{1,0:T(8,128)(2,1)S(1)}, u32[]{:S(2)}, u32[]{:S(2)}) %collective-permute-start.13) | collective-permute-done | bytes 2097184 | tf_op jit(solution)/shard_map/ppermute | solution.py:374
  592.9 24.8 %expand.8.refs_0_.refs_1_.refs_2_.refs_3_ = bf16[1024,1792]{1,0:T(8,128)(2,1)} custom-call(bf16[1024,4096]{1,0:T(8,128)(2,1)} %all-gather.25.cloned.1.call-done.x_ref, bf16[2,4096,1792]{2,1,0:T(8,128)(2,1)} %weight_ref.11, bf16[2,1,1792]{2,1,0:T(2,128)(2,1)} %copy.47.bias_ref), custom_call_target="tpu_custom_call" | custom-call | flops 15032385536 | bytes 41418752 | tf_op jit(solution)/shard_map/expand/pallas_call | solution.py:274
  644.3 14.5 %project_rows.35 = (bf16[256,4096]{1,0:T(8,128)(2,1)}, bf16[256,4096]{1,0:T(8,128)(2,1)}) custom-call(s32[8]{0:T(128)} %stack.113.table_ref, bf16[1024,1792]{1,0:T(8,128)(2,1)} %expand.8.refs_0_.refs_1_.refs_2_.refs_3_, bf16[1024,1792]{1,0:T(8,128)(2,1)} %expand.8.refs_0_.refs_1_.refs_2_.refs_3_, bf16[1024,1792]{1,0:T(8,128)(2,1)} %expand.8.refs_0_.refs_1_.refs_2_.refs_3_, ...), custom_call_target="tpu_custom_call" | custom-call | flops 7516192768 | bytes 20709376 | tf_op jit(solution)/shard_map/project_rows/pallas_call | solution.py:247
  671.9 37.6 %attend.9.refs_0_.refs_1_.refs_2_.refs_3_ = bf16[1024,512]{1,0:T(8,128)(2,1)} custom-call(s32[3]{0:T(128)} %start_ref.13, bf16[1024,512]{1,0:T(8,128)(2,1)} %get-tuple-element.219.q_ref, bf16[1024,128]{1,0:T(8,128)(2,1)} %get-tuple-element.220.kn_ref, bf16[1024,128]{1,0:T(8,128)(2,1)} %get-tuple-element.221.vn_ref, bf16[2,3,4096,128]{3,2,1,0:T(8,128)(2,1)} %bitcast.50, ...), custom_call_target="tpu_custom_call" | custom-call | flops 21474836480 | bytes 4718592 | tf_op jit(solution)/shard_map/attend/pallas_call | solution.py:179
  719.4 24.2 %collective-permute-done.17.refs_2_ = bf16[256,4096]{1,0:T(8,128)(2,1)S(1)} collective-permute-done((bf16[256,4096]{1,0:T(8,128)(2,1)}, bf16[256,4096]{1,0:T(8,128)(2,1)S(1)}, u32[]{:S(2)}, u32[]{:S(2)}) %collective-permute-start.17) | collective-permute-done | bytes 2097184 | tf_op jit(solution)/shard_map/ppermute | solution.py:374
  777.6 37.6 %attend.10.refs_0_.refs_1_.refs_2_.refs_3_ = bf16[1024,512]{1,0:T(8,128)(2,1)} custom-call(s32[3]{0:T(128)} %start_ref.13, bf16[1024,512]{1,0:T(8,128)(2,1)} %get-tuple-element.234.q_ref, bf16[1024,128]{1,0:T(8,128)(2,1)} %get-tuple-element.235.kn_ref, bf16[1024,128]{1,0:T(8,128)(2,1)} %get-tuple-element.236.vn_ref, bf16[2,3,4096,128]{3,2,1,0:T(8,128)(2,1)} %bitcast.51, ...), custom_call_target="tpu_custom_call" | custom-call | flops 21474836480 | bytes 4718592 | tf_op jit(solution)/shard_map/attend/pallas_call | solution.py:179
  824.7 24.2 %collective-permute-done.18.refs_2_ = bf16[256,4096]{1,0:T(8,128)(2,1)S(1)} collective-permute-done((bf16[256,4096]{1,0:T(8,128)(2,1)}, bf16[256,4096]{1,0:T(8,128)(2,1)S(1)}, u32[]{:S(2)}, u32[]{:S(2)}) %collective-permute-start.18) | collective-permute-done | bytes 2097184 | tf_op jit(solution)/shard_map/ppermute | solution.py:374
  883.0 37.6 %attend.11.refs_0_.refs_1_.refs_2_.refs_3_ = bf16[1024,512]{1,0:T(8,128)(2,1)} custom-call(s32[3]{0:T(128)} %start_ref.13, bf16[1024,512]{1,0:T(8,128)(2,1)} %get-tuple-element.247.q_ref, bf16[1024,128]{1,0:T(8,128)(2,1)} %get-tuple-element.248.kn_ref, bf16[1024,128]{1,0:T(8,128)(2,1)} %get-tuple-element.249.vn_ref, bf16[2,3,4096,128]{3,2,1,0:T(8,128)(2,1)} %bitcast.52, ...), custom_call_target="tpu_custom_call" | custom-call | flops 21474836480 | bytes 4718592 | tf_op jit(solution)/shard_map/attend/pallas_call | solution.py:179
  930.0 24.2 %collective-permute-done.23.refs_2_ = bf16[256,4096]{1,0:T(8,128)(2,1)S(1)} collective-permute-done((bf16[256,4096]{1,0:T(8,128)(2,1)}, bf16[256,4096]{1,0:T(8,128)(2,1)S(1)}, u32[]{:S(2)}, u32[]{:S(2)}) %collective-permute-start.23) | collective-permute-done | bytes 2097184 | tf_op jit(solution)/shard_map/ppermute | solution.py:374
  978.3 50.5 %collective-permute-done.24.refs_2_ = bf16[256,4096]{1,0:T(8,128)(2,1)S(1)} collective-permute-done((bf16[256,4096]{1,0:T(8,128)(2,1)}, bf16[256,4096]{1,0:T(8,128)(2,1)S(1)}, u32[]{:S(2)}, u32[]{:S(2)}) %collective-permute-start.24) | collective-permute-done | bytes 2097184 | tf_op jit(solution)/shard_map/ppermute | solution.py:374
  1032.1 24.9 %expand.9.refs_0_.refs_1_.refs_2_.refs_3_ = bf16[1024,1792]{1,0:T(8,128)(2,1)} custom-call(bf16[1024,4096]{1,0:T(8,128)(2,1)} %all-gather.29.cloned.1.call-done.x_ref, bf16[2,4096,1792]{2,1,0:T(8,128)(2,1)} %weight_ref.11, bf16[2,1,1792]{2,1,0:T(2,128)(2,1)} %copy.47.bias_ref), custom_call_target="tpu_custom_call" | custom-call | flops 15032385536 | bytes 41418752 | tf_op jit(solution)/shard_map/expand/pallas_call | solution.py:274
  1083.5 14.2 %project_rows.43 = (bf16[256,4096]{1,0:T(8,128)(2,1)}, bf16[256,4096]{1,0:T(8,128)(2,1)}) custom-call(s32[8]{0:T(128)} %stack.113.table_ref, bf16[1024,1792]{1,0:T(8,128)(2,1)} %expand.9.refs_0_.refs_1_.refs_2_.refs_3_, bf16[1024,1792]{1,0:T(8,128)(2,1)} %expand.9.refs_0_.refs_1_.refs_2_.refs_3_, bf16[1024,1792]{1,0:T(8,128)(2,1)} %expand.9.refs_0_.refs_1_.refs_2_.refs_3_, ...), custom_call_target="tpu_custom_call" | custom-call | flops 7516192768 | bytes 20709376 | tf_op jit(solution)/shard_map/project_rows/pallas_call | solution.py:247
  1097.7 25.3 %expand.10.refs_0_.refs_1_.refs_2_.refs_3_ = bf16[1024,1792]{1,0:T(8,128)(2,1)} custom-call(bf16[1024,4096]{1,0:T(8,128)(2,1)} %all-gather.33.cloned.1.call-done.x_ref, bf16[2,4096,1792]{2,1,0:T(8,128)(2,1)} %weight_ref.11, bf16[2,1,1792]{2,1,0:T(2,128)(2,1)} %copy.47.bias_ref), custom_call_target="tpu_custom_call" | custom-call | flops 15032385536 | bytes 41418752 | tf_op jit(solution)/shard_map/expand/pallas_call | solution.py:274
  1144.4 14.2 %project_rows.45 = (bf16[256,4096]{1,0:T(8,128)(2,1)}, bf16[256,4096]{1,0:T(8,128)(2,1)}) custom-call(s32[8]{0:T(128)} %stack.113.table_ref, bf16[1024,1792]{1,0:T(8,128)(2,1)} %expand.10.refs_0_.refs_1_.refs_2_.refs_3_, bf16[1024,1792]{1,0:T(8,128)(2,1)} %expand.10.refs_0_.refs_1_.refs_2_.refs_3_, ...), custom_call_target="tpu_custom_call" | custom-call | flops 7516192768 | bytes 20709376 | tf_op jit(solution)/shard_map/project_rows/pallas_call | solution.py:247
  1166.9 24.7 %expand.11.refs_0_.refs_1_.refs_2_.refs_3_ = bf16[1024,1792]{1,0:T(8,128)(2,1)} custom-call(bf16[1024,4096]{1,0:T(8,128)(2,1)} %all-gather.35.cloned.1.call-done.x_ref, bf16[2,4096,1792]{2,1,0:T(8,128)(2,1)} %weight_ref.11, bf16[2,1,1792]{2,1,0:T(2,128)(2,1)} %copy.47.bias_ref), custom_call_target="tpu_custom_call" | custom-call | flops 15032385536 | bytes 41418752 | tf_op jit(solution)/shard_map/expand/pallas_call | solution.py:274
  1208.3 23.4 %collective-permute-done.32 = bf16[256,4096]{1,0:T(8,128)(2,1)S(1)} collective-permute-done((bf16[256,4096]{1,0:T(8,128)(2,1)}, bf16[256,4096]{1,0:T(8,128)(2,1)S(1)}, u32[]{:S(2)}, u32[]{:S(2)}) %collective-permute-start.32) | collective-permute-done | bytes 2097184 | tf_op jit(solution)/shard_map/ppermute | solution.py:374
  1235.8 14.3 %project_rows.47 = (bf16[256,4096]{1,0:T(8,128)(2,1)}, bf16[256,4096]{1,0:T(8,128)(2,1)}) custom-call(s32[8]{0:T(128)} %stack.113.table_ref, bf16[1024,1792]{1,0:T(8,128)(2,1)} %expand.11.refs_0_.refs_1_.refs_2_.refs_3_, bf16[1024,1792]{1,0:T(8,128)(2,1)} %expand.11.refs_0_.refs_1_.refs_2_.refs_3_, ...), custom_call_target="tpu_custom_call" | custom-call | flops 7516192768 | bytes 20709376 | tf_op jit(solution)/shard_map/project_rows/pallas_call | solution.py:247
  1261.8 25.8 %collective-permute-done.33 = bf16[256,4096]{1,0:T(8,128)(2,1)S(1)} collective-permute-done((bf16[256,4096]{1,0:T(8,128)(2,1)}, bf16[256,4096]{1,0:T(8,128)(2,1)S(1)}, u32[]{:S(2)}, u32[]{:S(2)}) %collective-permute-start.33) | collective-permute-done | bytes 2097184 | tf_op jit(solution)/shard_map/ppermute | solution.py:374
  1293.0 16.0 %write_caches.1 = (bf16[2,3,4096,128]{3,2,1,0:T(8,128)(2,1)}, bf16[2,3,4096,128]{3,2,1,0:T(8,128)(2,1)}) custom-call(s32[3]{0:T(128)} %start_ref.13, bf16[2,3,4096,128]{3,2,1,0:T(8,128)(2,1)} %bitcast.53, bf16[2,3,4096,128]{3,2,1,0:T(8,128)(2,1)} %bitcast.60, bf16[2,3,1024,128]{3,2,1,0:T(8,128)(2,1)} %get-tuple-element.310.kn_ref, ...), custom_call_target="tpu_custom_call" | custom-call | flops 16777216 | bytes 25165824 | tf_op jit(solution)/shard_map/write_caches/pallas_call | solution.py:315
  (270 shorter events, 466.9 us)
Async XLA Ops:
  7.2 56.2 %all-gather.13.cloned.1.call-start = ((), (), s32[]{:S(2)}) async-start(), calls=%async_computation | async-start | bytes 9437184 | tf_op jit(solution)/shard_map/all_gather | solution.py:377
  11.8 124.3 %all-gather.15.cloned.1.call-start = ((), (), s32[]{:S(2)}) async-start(), calls=%async_computation.1 | async-start | bytes 9437184 | tf_op jit(solution)/shard_map/all_gather | solution.py:377
  14.8 227.0 %all-gather.19.cloned.1.call-start = ((), (), s32[]{:S(2)}) async-start(), calls=%async_computation.3 | async-start | bytes 9437184 | tf_op jit(solution)/shard_map/all_gather | solution.py:377
  17.9 330.9 %all-gather.17.cloned.1.call-start = ((), (), s32[]{:S(2)}) async-start(), calls=%async_computation.2 | async-start | bytes 9437184 | tf_op jit(solution)/shard_map/all_gather | solution.py:377
  194.1 28.7 %collective-permute-start.3 = (bf16[512,4096]{1,0:T(8,128)(2,1)}, bf16[512,4096]{1,0:T(8,128)(2,1)}, u32[]{:S(2)}, u32[]{:S(2)}) collective-permute-start(bf16[512,4096]{1,0:T(8,128)(2,1)} %project_rows.26), channel_id=1, source_target_pairs={{0,1},{1,0},{2,3},{3,2},{4,5},{5,4},{6,7},{7,6}} | collective-permute-start | bytes 12582920 | tf_op jit(solution)/shard_map/ppermute | solution.py:374
  241.8 205.2 %all-gather.21.cloned.1.call-start = ((), (), s32[]{:S(2)}) async-start(), calls=%async_computation.4 | async-start | bytes 9437184 | tf_op jit(solution)/shard_map/all_gather | solution.py:377
  299.2 28.0 %collective-permute-start.6 = (bf16[512,4096]{1,0:T(8,128)(2,1)}, bf16[512,4096]{1,0:T(8,128)(2,1)}, u32[]{:S(2)}, u32[]{:S(2)}) collective-permute-start(bf16[512,4096]{1,0:T(8,128)(2,1)} %project_rows.28), channel_id=1, source_target_pairs={{0,1},{1,0},{2,3},{3,2},{4,5},{5,4},{6,7},{7,6}} | collective-permute-start | bytes 12582920 | tf_op jit(solution)/shard_map/ppermute | solution.py:374
  299.3 26.3 %collective-permute-start.4 = (bf16[256,4096]{1,0:T(8,128)(2,1)}, bf16[256,4096]{1,0:T(8,128)(2,1)S(1)}, u32[]{:S(2)}, u32[]{:S(2)}) collective-permute-start(bf16[256,4096]{1,0:T(8,128)(2,1)} %get-tuple-element.173), channel_id=1, source_target_pairs={{0,2},{1,5},{2,0},{3,7},{4,6},{5,1},{6,4},{7,3}} | collective-permute-start | bytes 6291464 | tf_op jit(solution)/shard_map/ppermute | solution.py:374
  347.0 245.9 %all-gather.25.cloned.1.call-start = ((), (), s32[]{:S(2)}) async-start(), calls=%async_computation.6 | async-start | bytes 9437184 | tf_op jit(solution)/shard_map/all_gather | solution.py:377
  347.6 56.0 %collective-permute-start.8 = (bf16[256,4096]{1,0:T(8,128)(2,1)}, bf16[256,4096]{1,0:T(8,128)(2,1)}, u32[]{:S(2)}, u32[]{:S(2)}) collective-permute-start(bf16[256,4096]{1,0:T(8,128)(2,1)} %get-tuple-element.187), channel_id=1, source_target_pairs={{0,2},{1,5},{2,0},{3,7},{4,6},{5,1},{6,4},{7,3}} | collective-permute-start | bytes 6291464 | tf_op jit(solution)/shard_map/ppermute | solution.py:374
  425.2 233.6 %all-gather.23.cloned.1.call-start = ((), (), s32[]{:S(2)}) async-start(), calls=%async_computation.5 | async-start | bytes 9437184 | tf_op jit(solution)/shard_map/all_gather | solution.py:377
  486.3 27.5 %collective-permute-start.10 = (bf16[256,4096]{1,0:T(8,128)(2,1)}, bf16[256,4096]{1,0:T(8,128)(2,1)}, u32[]{:S(2)}, u32[]{:S(2)}) collective-permute-start(bf16[256,4096]{1,0:T(8,128)(2,1)} %get-tuple-element.196), channel_id=1, source_target_pairs={{0,2},{1,5},{2,0},{3,7},{4,6},{5,1},{6,4},{7,3}} | collective-permute-start | bytes 6291464 | tf_op jit(solution)/shard_map/ppermute | solution.py:374
  535.5 229.7 %all-gather.27.cloned.1.call-start = ((), (), s32[]{:S(2)}) async-start(), calls=%async_computation.7 | async-start | bytes 9437184 | tf_op jit(solution)/shard_map/all_gather | solution.py:377
  535.5 56.0 %collective-permute-start.13 = (bf16[256,4096]{1,0:T(8,128)(2,1)}, bf16[256,4096]{1,0:T(8,128)(2,1)S(1)}, u32[]{:S(2)}, u32[]{:S(2)}) collective-permute-start(bf16[256,4096]{1,0:T(8,128)(2,1)} %get-tuple-element.207), channel_id=1, source_target_pairs={{0,2},{1,5},{2,0},{3,7},{4,6},{5,1},{6,4},{7,3}} | collective-permute-start | bytes 6291464 | tf_op jit(solution)/shard_map/ppermute | solution.py:374
  592.9 38.5 %collective-permute-start.15 = (bf16[128,4096]{1,0:T(8,128)(2,1)S(1)}, bf16[128,4096]{1,0:T(8,128)(2,1)S(1)}, u32[]{:S(2)}, u32[]{:S(2)}) collective-permute-start(bf16[128,4096]{1,0:T(8,128)(2,1)S(1)} %add_convert_fusion.10), channel_id=1, source_target_pairs={{0,4},{1,3},{2,6},{3,1},{4,0},{5,7},{6,2},{7,5}} | collective-permute-start | bytes 3145736 | tf_op jit(solution)/shard_map/ppermute | solution.py:374
  636.7 233.7 %all-gather.31.cloned.1.call-start = ((), (), s32[]{:S(2)}) async-start(), calls=%async_computation.9 | async-start | bytes 9437184 | tf_op jit(solution)/shard_map/all_gather | solution.py:377
  716.9 30.2 %collective-permute-start.16 = (bf16[512,4096]{1,0:T(8,128)(2,1)}, bf16[512,4096]{1,0:T(8,128)(2,1)}, u32[]{:S(2)}, u32[]{:S(2)}) collective-permute-start(bf16[512,4096]{1,0:T(8,128)(2,1)} %project_rows.36), channel_id=1, source_target_pairs={{0,1},{1,0},{2,3},{3,2},{4,5},{5,4},{6,7},{7,6}} | collective-permute-start | bytes 12582920 | tf_op jit(solution)/shard_map/ppermute | solution.py:374
  717.0 26.7 %collective-permute-start.17 = (bf16[256,4096]{1,0:T(8,128)(2,1)}, bf16[256,4096]{1,0:T(8,128)(2,1)S(1)}, u32[]{:S(2)}, u32[]{:S(2)}) collective-permute-start(bf16[256,4096]{1,0:T(8,128)(2,1)} %get-tuple-element.222), channel_id=1, source_target_pairs={{0,2},{1,5},{2,0},{3,7},{4,6},{5,1},{6,4},{7,3}} | collective-permute-start | bytes 6291464 | tf_op jit(solution)/shard_map/ppermute | solution.py:374
  765.2 266.9 %all-gather.29.cloned.1.call-start = ((), (), s32[]{:S(2)}) async-start(), calls=%async_computation.8 | async-start | bytes 9437184 | tf_op jit(solution)/shard_map/all_gather | solution.py:377
  822.6 29.7 %collective-permute-start.21 = (bf16[512,4096]{1,0:T(8,128)(2,1)}, bf16[512,4096]{1,0:T(8,128)(2,1)}, u32[]{:S(2)}, u32[]{:S(2)}) collective-permute-start(bf16[512,4096]{1,0:T(8,128)(2,1)} %project_rows.38), channel_id=1, source_target_pairs={{0,1},{1,0},{2,3},{3,2},{4,5},{5,4},{6,7},{7,6}} | collective-permute-start | bytes 12582920 | tf_op jit(solution)/shard_map/ppermute | solution.py:374
  822.6 26.3 %collective-permute-start.18 = (bf16[256,4096]{1,0:T(8,128)(2,1)}, bf16[256,4096]{1,0:T(8,128)(2,1)S(1)}, u32[]{:S(2)}, u32[]{:S(2)}) collective-permute-start(bf16[256,4096]{1,0:T(8,128)(2,1)} %get-tuple-element.227), channel_id=1, source_target_pairs={{0,2},{1,5},{2,0},{3,7},{4,6},{5,1},{6,4},{7,3}} | collective-permute-start | bytes 6291464 | tf_op jit(solution)/shard_map/ppermute | solution.py:374
  870.3 227.4 %all-gather.33.cloned.1.call-start = ((), (), s32[]{:S(2)}) async-start(), calls=%async_computation.10 | async-start | bytes 9437184 | tf_op jit(solution)/shard_map/all_gather | solution.py:377
  927.9 30.0 %collective-permute-start.22 = (bf16[512,4096]{1,0:T(8,128)(2,1)}, bf16[512,4096]{1,0:T(8,128)(2,1)}, u32[]{:S(2)}, u32[]{:S(2)}) collective-permute-start(bf16[512,4096]{1,0:T(8,128)(2,1)} %project_rows.40), channel_id=1, source_target_pairs={{0,1},{1,0},{2,3},{3,2},{4,5},{5,4},{6,7},{7,6}} | collective-permute-start | bytes 12582920 | tf_op jit(solution)/shard_map/ppermute | solution.py:374
  927.9 26.3 %collective-permute-start.23 = (bf16[256,4096]{1,0:T(8,128)(2,1)}, bf16[256,4096]{1,0:T(8,128)(2,1)S(1)}, u32[]{:S(2)}, u32[]{:S(2)}) collective-permute-start(bf16[256,4096]{1,0:T(8,128)(2,1)} %get-tuple-element.250), channel_id=1, source_target_pairs={{0,2},{1,5},{2,0},{3,7},{4,6},{5,1},{6,4},{7,3}} | collective-permute-start | bytes 6291464 | tf_op jit(solution)/shard_map/ppermute | solution.py:374
  976.3 190.6 %all-gather.35.cloned.1.call-start = ((), (), s32[]{:S(2)}) async-start(), calls=%async_computation.11 | async-start | bytes 9437184 | tf_op jit(solution)/shard_map/all_gather | solution.py:377
  976.3 52.5 %collective-permute-start.24 = (bf16[256,4096]{1,0:T(8,128)(2,1)}, bf16[256,4096]{1,0:T(8,128)(2,1)S(1)}, u32[]{:S(2)}, u32[]{:S(2)}) collective-permute-start(bf16[256,4096]{1,0:T(8,128)(2,1)} %get-tuple-element.255), channel_id=1, source_target_pairs={{0,2},{1,5},{2,0},{3,7},{4,6},{5,1},{6,4},{7,3}} | collective-permute-start | bytes 6291464 | tf_op jit(solution)/shard_map/ppermute | solution.py:374
  1030.2 40.5 %collective-permute-start.27 = (bf16[128,4096]{1,0:T(8,128)(2,1)S(1)}, bf16[128,4096]{1,0:T(8,128)(2,1)S(1)}, u32[]{:S(2)}, u32[]{:S(2)}) collective-permute-start(bf16[128,4096]{1,0:T(8,128)(2,1)S(1)} %add_convert_fusion.6), channel_id=1, source_target_pairs={{0,4},{1,3},{2,6},{3,1},{4,0},{5,7},{6,2},{7,5}} | collective-permute-start | bytes 3145736 | tf_op jit(solution)/shard_map/ppermute | solution.py:374
  1136.9 27.5 %collective-permute-start.28 = (bf16[256,4096]{1,0:T(8,128)(2,1)}, bf16[256,4096]{1,0:T(8,128)(2,1)}, u32[]{:S(2)}, u32[]{:S(2)}) collective-permute-start(bf16[256,4096]{1,0:T(8,128)(2,1)} %get-tuple-element.271), channel_id=1, source_target_pairs={{0,2},{1,5},{2,0},{3,7},{4,6},{5,1},{6,4},{7,3}} | collective-permute-start | bytes 6291464 | tf_op jit(solution)/shard_map/ppermute | solution.py:374
  1205.5 30.3 %collective-permute-start.31 = (bf16[512,4096]{1,0:T(8,128)(2,1)}, bf16[512,4096]{1,0:T(8,128)(2,1)}, u32[]{:S(2)}, u32[]{:S(2)}) collective-permute-start(bf16[512,4096]{1,0:T(8,128)(2,1)} %project_rows.46), channel_id=1, source_target_pairs={{0,1},{1,0},{2,3},{3,2},{4,5},{5,4},{6,7},{7,6}} | collective-permute-start | bytes 12582920 | tf_op jit(solution)/shard_map/ppermute | solution.py:374
  1205.5 26.3 %collective-permute-start.32 = (bf16[256,4096]{1,0:T(8,128)(2,1)}, bf16[256,4096]{1,0:T(8,128)(2,1)S(1)}, u32[]{:S(2)}, u32[]{:S(2)}) collective-permute-start(bf16[256,4096]{1,0:T(8,128)(2,1)} %get-tuple-element.278), channel_id=1, source_target_pairs={{0,2},{1,5},{2,0},{3,7},{4,6},{5,1},{6,4},{7,3}} | collective-permute-start | bytes 6291464 | tf_op jit(solution)/shard_map/ppermute | solution.py:374
  1250.1 37.5 %collective-permute-start.33 = (bf16[256,4096]{1,0:T(8,128)(2,1)}, bf16[256,4096]{1,0:T(8,128)(2,1)S(1)}, u32[]{:S(2)}, u32[]{:S(2)}) collective-permute-start(bf16[256,4096]{1,0:T(8,128)(2,1)} %get-tuple-element.283), channel_id=1, source_target_pairs={{0,2},{1,5},{2,0},{3,7},{4,6},{5,1},{6,4},{7,3}} | collective-permute-start | bytes 6291464 | tf_op jit(solution)/shard_map/ppermute | solution.py:374
  1256.9 52.0 %collective-permute-start.30 = (bf16[128,4096]{1,0:T(8,128)(2,1)}, bf16[128,4096]{1,0:T(8,128)(2,1)}, u32[]{:S(2)}, u32[]{:S(2)}) collective-permute-start(bf16[128,4096]{1,0:T(8,128)(2,1)} %add_convert_fusion.5), channel_id=1, source_target_pairs={{0,4},{1,3},{2,6},{3,1},{4,0},{5,7},{6,2},{7,5}} | collective-permute-start | bytes 3145736 | tf_op jit(solution)/shard_map/ppermute | solution.py:374
  (69 other events, 847.6 us)
Sparse Core Ops, SparseCore 0:
  11.9 51.4 all-gather.12
  65.8 48.7 all-gather.14
  116.4 48.6 all-gather.18
  241.9 48.4 all-gather.16
  347.1 65.8 all-gather.20
  425.3 49.6 all-gather.24
  535.6 66.6 all-gather.22
  636.8 50.9 all-gather.26
  765.3 50.7 all-gather.30
  870.4 50.6 all-gather.28
  976.4 66.7 all-gather.32
  1076.1 49.6 all-gather.34

commit v4 on v3

--- a/solution.py
+++ b/solution.py
@@ -12,23 +12,23 @@
 LOG2E = 1.4426950408889634
 HIDE = -(1 << 30)
 VMEM_LIMIT = 60 << 20
-TURNS = [int(c) for c in '012001010212102201100121202021010212120201102121202']
-
-
-def norm_kernel(*refs, joined):
+TURNS = [int(c) for c in '210221212010120201212010120201212010120012102101020']
+
+
+def norm_kernel(*refs, joined, which):
     if joined:
-        base_ref, pair_ref, came_ref, last_ref, bias_ref, gain_ref, shift_ref, sum_ref, norm_ref = refs
+        base_ref, pair_ref, came_ref, last_ref, bias_ref, scale_ref, sum_ref, norm_ref = refs
         summed = pair_ref[...].astype(jnp.float32) + came_ref[...].astype(jnp.float32) + last_ref[...].astype(jnp.float32)
         kept = (base_ref[...].astype(jnp.float32) + summed + bias_ref[...].astype(jnp.float32)).astype(jnp.bfloat16)
         sum_ref[...] = kept
     else:
-        base_ref, gain_ref, shift_ref, norm_ref = refs
+        base_ref, scale_ref, norm_ref = refs
         kept = base_ref[...]
     values = kept.astype(jnp.float32)
     centered = values - jnp.mean(values, axis=-1, keepdims=True)
     variance = jnp.mean(centered * centered, axis=-1, keepdims=True)
     scaled = centered * lax.rsqrt(variance + NORM_EPS)
-    norm_ref[...] = (scaled * gain_ref[...].astype(jnp.float32) + shift_ref[...].astype(jnp.float32)).astype(jnp.bfloat16)
+    norm_ref[...] = (scaled * scale_ref[which:which + 1, :].astype(jnp.float32) + scale_ref[which + 1:which + 2, :].astype(jnp.float32)).astype(jnp.bfloat16)
 
 
 def normalize(base, seq, terms, bias, norms, layer, which, rows=64):
@@ -36,8 +36,8 @@
     line = pl.BlockSpec((rows, model), lambda i: (i, 0))
     first = line if base.ndim == 2 else pl.BlockSpec((None, rows, model), lambda i: (seq, i, 0))
     vector = lambda at: pl.BlockSpec((None, 1, model), lambda i: (at, 0, 0))
-    scale_specs = [vector(4 * layer + which), vector(4 * layer + which + 1)]
-    scales = [norms, norms]
+    scale_specs = [pl.BlockSpec((None, norms.shape[1], model), lambda i: (layer, 0, 0))]
+    scales = [norms]
     whole = jax.ShapeDtypeStruct((part, model), jnp.bfloat16)
     if terms is None:
         specs, args, outs = [first], [base], [whole]
@@ -45,7 +45,7 @@
         bias, bias_at = bias
         specs, args, outs = [first, line, line, line, vector(bias_at)], [base, *terms, bias], [whole, whole]
     return pl.pallas_call(
-        functools.partial(norm_kernel, joined=terms is not None),
+        functools.partial(norm_kernel, joined=terms is not None, which=which),
         grid=(part // rows,),
         in_specs=specs + scale_specs,
         out_specs=[line] * len(outs),
@@ -226,7 +226,7 @@
         sent_ref[...] = total[total.shape[0] // 2:]
 
 
-def project_rows(table, acts, weight, layer, lead, cols, slots=4):
+def project_rows(table, acts, weight, layer, lead, cols, slots=3):
     chunk, depth = acts.shape
     model = weight.shape[2]
     half = chunk // 2
@@ -267,7 +267,7 @@
     out_ref[...] = jax.nn.gelu(lifted, approximate=True).astype(jnp.bfloat16)
 
 
-def expand_rows(acts, weight, bias, layer, rows=512, cols=256, slots=4):
+def expand_rows(acts, weight, bias, layer, rows=512, cols=896, slots=2):
     chunk, model = acts.shape
     width = weight.shape[2]
     blocks, tiles = chunk // rows, width // cols
@@ -342,7 +342,7 @@
     pairs_second = [(d, ((d // 2) ^ (3 - first_axis(d % 2))) * 2 + d % 2) for d in range(count)]
 
     def device_step(tokens, start_pos, cos_tab, sin_tab, key_cache, value_cache, slot_pos, norm_params, w_q, b_q, w_k, b_k, w_v, b_v, w_o, b_o, w_up, b_up, w_down, b_down):
-        num_seqs, part, model = tokens.shape
+        num_seqs, part, _ = tokens.shape
         chunk = cos_tab.shape[1]
         head_dim = cos_tab.shape[2]
         layers = key_cache.shape[0]
@@ -357,7 +357,7 @@
         theirs = [chip ^ flip for flip in (0, near, far, 3)]
         order = [c * 2 + core for c in mine] + [c * 2 + 1 - core for c in theirs]
         table = jnp.stack(order).astype(jnp.int32)
-        norms = norm_params.reshape(-1, 1, model)
+        norms = norm_params
         out_bias = b_o[:, None, :]
         down_bias = b_down[:, None, :]
         latest = [None]
@@ -397,12 +397,12 @@
             fresh_keys[layer][seq] = key_new
             fresh_values[layer][seq] = value_new
             mixed = attend(query, key_new, value_new, keys_in, values_in, held, start_pos, layer, seq)
-            lead, = project_rows(table, mixed, w_o, layer, None, 1024)
+            lead, = project_rows(table, mixed, w_o, layer, None, 2048)
             return lead, mixed
 
         def expand(gathered, layer):
             active = expand_rows(gathered, w_up, up_bias, layer)
-            lead, = project_rows(table, active, w_down, layer, None, 512)
+            lead, = project_rows(table, active, w_down, layer, None, 1024)
             return lead, active
 
         def finish(middle, kept, came, last):
@@ -425,13 +425,13 @@
                 gathered = gather(normed)
                 yield
                 lead, own = item(functools.partial(attention, layer=layer, seq=seq), gathered)
-                terms = yield from scatter_sum(lead, own, w_o, layer, 1024)
+                terms = yield from scatter_sum(lead, own, w_o, layer, 2048)
                 seq_of[0] = seq
                 normed, middle = item(lambda *terms: join(base, *terms, bias=out_bias, layer=layer, which=2), *terms)
                 gathered = gather(normed)
                 yield
                 lead, own = item(functools.partial(expand, layer=layer), gathered)
-                terms = yield from scatter_sum(lead, own, w_down, layer, 512)
+                terms = yield from scatter_sum(lead, own, w_down, layer, 1024)
                 if layer + 1 < layers:
                     seq_of[0] = seq
                     normed, base = item(lambda *terms: join(middle, *terms, bias=down_bias, layer=layer, which=4), *terms)

time: 1330 us -> 1270 us (0.955)
  waiting for transfers between devices: 439 us -> 396 us
  starting transfers between devices: 38.3 us -> 16.7 us
    ppermute x36, waiting for transfers between devices: 396 us -> 353 us  [send(): return lax.ppermute(value, 'tp', pairs)]
    ppermute x36, starting transfers between devices: 37.8 us -> 16.2 us  [send(): return lax.ppermute(value, 'tp', pairs)]
  transfers between devices with their start and end apart: 48 -> 48, of which waited for: 26 -> 20; matrix products, arithmetic and copies ran while one was open for 2% -> 2% of each run, Pallas kernels for 56% -> 59%
where the time goes in v4:
time: 1270 us; the launch traced here: 1260 us
  Pallas kernels  784 us (62%)
  waiting for transfers between devices  396 us (31%)
  local copies, waits for them, and re-layouts  24.1 us (2%)
  other arithmetic  23.9 us (2%)
  starting transfers between devices  16.7 us (1%)
  between operations  15.6 us (1%)
    ppermute x36, waiting for transfers between devices, send(): return lax.ppermute(value, 'tp', pairs)  353 us
    pallas_call x24, Pallas kernels, project_rows(): pl.pallas_call(functools.partial(project_kernel, shards=shards, joined=le...  259 us
    pallas_call x6, Pallas kernels, attend(): pl.pallas_call(functools.partial(attention_kernel, seq=seq, group=group,...  226 us
    pallas_call x6, Pallas kernels, expand_rows(): pl.pallas_call(functools.partial(expand_kernel, layer=layer, blocks=block...  159 us
    pallas_call x6, Pallas kernels, qkv_project(): pl.pallas_call(qkv_kernel, grid=(chunk // rows,), in_specs=[row_block(mod...  76.5 us
    pallas_call x12, Pallas kernels, normalize(): pl.pallas_call(functools.partial(norm_kernel, joined=terms is not None, w...  47.7 us
    all_gather x12, waiting for transfers between devices, gather(): return lax.all_gather(value, 'tp', axis=0, tiled=True)  42.7 us
  transfers between devices with their start and end apart: 48, of which 20 were waited for; matrix products, arithmetic and copies ran while one was open for 2% of the time, Pallas kernels for 59%

profile of v4, /device:TPU:0, one launch (start us, length us, event | category | flops | bytes accessed | tf_op | source)
XLA Modules:
  0.0 1259.9 jit_solution(7252304511259314055)
XLA Ops:
  19.4 42.5 %all-gather.15.cloned.1.call-done.x_ref = bf16[1024,4096]{1,0:T(8,128)(2,1)} async-done(((bf16[128,4096]{1,0:T(8,128)(2,1)}), bf16[1024,4096]{1,0:T(8,128)(2,1)}) %all-gather.15.cloned.1.call-update) | async-done | bytes 8388624 | tf_op jit(solution)/shard_map/all_gather | solution.py:377
  74.1 37.6 %attend.6.refs_0_.refs_1_.refs_2_.refs_3_ = bf16[1024,512]{1,0:T(8,128)(2,1)} custom-call(s32[3]{0:T(128)} %start_ref.13, bf16[1024,512]{1,0:T(8,128)(2,1)} %get-tuple-element.154.q_ref, bf16[1024,128]{1,0:T(8,128)(2,1)} %get-tuple-element.155.kn_ref, bf16[1024,128]{1,0:T(8,128)(2,1)} %get-tuple-element.156.vn_ref, bf16[2,3,4096,128]{3,2,1,0:T(8,128)(2,1)} %bitcast.47, ...), custom_call_target="tpu_custom_call" | custom-call | flops 21474836480 | bytes 4718592 | tf_op jit(solution)/shard_map/attend/pallas_call | solution.py:179
  147.9 38.1 %attend.7.refs_0_.refs_1_.refs_2_.refs_3_ = bf16[1024,512]{1,0:T(8,128)(2,1)} custom-call(s32[3]{0:T(128)} %start_ref.13, bf16[1024,512]{1,0:T(8,128)(2,1)} %get-tuple-element.161.q_ref, bf16[1024,128]{1,0:T(8,128)(2,1)} %get-tuple-element.162.kn_ref, bf16[1024,128]{1,0:T(8,128)(2,1)} %get-tuple-element.163.vn_ref, bf16[2,3,4096,128]{3,2,1,0:T(8,128)(2,1)} %bitcast.48, ...), custom_call_target="tpu_custom_call" | custom-call | flops 21474836480 | bytes 4718592 | tf_op jit(solution)/shard_map/attend/pallas_call | solution.py:179
  194.8 25.2 %collective-permute-done.1.refs_2_ = bf16[256,4096]{1,0:T(8,128)(2,1)S(1)} collective-permute-done((bf16[256,4096]{1,0:T(8,128)(2,1)}, bf16[256,4096]{1,0:T(8,128)(2,1)S(1)}, u32[]{:S(2)}, u32[]{:S(2)}) %collective-permute-start.1) | collective-permute-done | bytes 2097184 | tf_op jit(solution)/shard_map/ppermute | solution.py:374
  253.9 37.6 %attend.8.refs_0_.refs_1_.refs_2_.refs_3_ = bf16[1024,512]{1,0:T(8,128)(2,1)} custom-call(s32[3]{0:T(128)} %start_ref.13, bf16[1024,512]{1,0:T(8,128)(2,1)} %get-tuple-element.173.q_ref, bf16[1024,128]{1,0:T(8,128)(2,1)} %get-tuple-element.174.kn_ref, bf16[1024,128]{1,0:T(8,128)(2,1)} %get-tuple-element.175.vn_ref, bf16[2,3,4096,128]{3,2,1,0:T(8,128)(2,1)} %bitcast.49, ...), custom_call_target="tpu_custom_call" | custom-call | flops 21474836480 | bytes 4718592 | tf_op jit(solution)/shard_map/attend/pallas_call | solution.py:179
  300.0 25.3 %collective-permute-done.5.refs_2_ = bf16[256,4096]{1,0:T(8,128)(2,1)S(1)} collective-permute-done((bf16[256,4096]{1,0:T(8,128)(2,1)}, bf16[256,4096]{1,0:T(8,128)(2,1)S(1)}, u32[]{:S(2)}, u32[]{:S(2)}) %collective-permute-start.5) | collective-permute-done | bytes 2097184 | tf_op jit(solution)/shard_map/ppermute | solution.py:374
  347.4 26.5 %expand.6.refs_0_.refs_1_.refs_2_.refs_3_ = bf16[1024,1792]{1,0:T(8,128)(2,1)} custom-call(bf16[1024,4096]{1,0:T(8,128)(2,1)} %all-gather.19.cloned.1.call-done.x_ref, bf16[2,4096,1792]{2,1,0:T(8,128)(2,1)} %weight_ref.11, bf16[2,1,1792]{2,1,0:T(2,128)(2,1)} %copy.37.bias_ref), custom_call_target="tpu_custom_call" | custom-call | flops 15032385536 | bytes 41418752 | tf_op jit(solution)/shard_map/expand/pallas_call | solution.py:274
  388.7 26.9 %collective-permute-done.6.refs_2_ = bf16[256,4096]{1,0:T(8,128)(2,1)S(1)} collective-permute-done((bf16[256,4096]{1,0:T(8,128)(2,1)}, bf16[256,4096]{1,0:T(8,128)(2,1)S(1)}, u32[]{:S(2)}, u32[]{:S(2)}) %collective-permute-start.6) | collective-permute-done | bytes 2097184 | tf_op jit(solution)/shard_map/ppermute | solution.py:374
  437.8 26.5 %expand.7.refs_0_.refs_1_.refs_2_.refs_3_ = bf16[1024,1792]{1,0:T(8,128)(2,1)} custom-call(bf16[1024,4096]{1,0:T(8,128)(2,1)} %all-gather.23.cloned.1.call-done.x_ref, bf16[2,4096,1792]{2,1,0:T(8,128)(2,1)} %weight_ref.11, bf16[2,1,1792]{2,1,0:T(2,128)(2,1)} %copy.37.bias_ref), custom_call_target="tpu_custom_call" | custom-call | flops 15032385536 | bytes 41418752 | tf_op jit(solution)/shard_map/expand/pallas_call | solution.py:274
  478.5 28.0 %collective-permute-done.10.refs_2_ = bf16[256,4096]{1,0:T(8,128)(2,1)S(1)} collective-permute-done((bf16[256,4096]{1,0:T(8,128)(2,1)}, bf16[256,4096]{1,0:T(8,128)(2,1)S(1)}, u32[]{:S(2)}, u32[]{:S(2)}) %collective-permute-start.10) | collective-permute-done | bytes 2097184 | tf_op jit(solution)/shard_map/ppermute | solution.py:374
  509.8 14.0 %project_rows.33 = (bf16[256,4096]{1,0:T(8,128)(2,1)}, bf16[256,4096]{1,0:T(8,128)(2,1)}) custom-call(s32[8]{0:T(128)} %stack.113.table_ref, bf16[1024,1792]{1,0:T(8,128)(2,1)} %expand.7.refs_0_.refs_1_.refs_2_.refs_3_, bf16[1024,1792]{1,0:T(8,128)(2,1)} %expand.7.refs_0_.refs_1_.refs_2_.refs_3_, bf16[1024,1792]{1,0:T(8,128)(2,1)} %expand.7.refs_0_.refs_1_.refs_2_.refs_3_, ...), custom_call_target="tpu_custom_call" | custom-call | flops 7516192768 | bytes 20709376 | tf_op jit(solution)/shard_map/project_rows/pallas_call | solution.py:247
  529.2 26.9 %expand.8.refs_0_.refs_1_.refs_2_.refs_3_ = bf16[1024,1792]{1,0:T(8,128)(2,1)} custom-call(bf16[1024,4096]{1,0:T(8,128)(2,1)} %all-gather.21.cloned.1.call-done.x_ref, bf16[2,4096,1792]{2,1,0:T(8,128)(2,1)} %weight_ref.11, bf16[2,1,1792]{2,1,0:T(2,128)(2,1)} %copy.37.bias_ref), custom_call_target="tpu_custom_call" | custom-call | flops 15032385536 | bytes 41418752 | tf_op jit(solution)/shard_map/expand/pallas_call | solution.py:274
  570.3 27.3 %collective-permute-done.14.refs_2_ = bf16[256,4096]{1,0:T(8,128)(2,1)S(1)} collective-permute-done((bf16[256,4096]{1,0:T(8,128)(2,1)}, bf16[256,4096]{1,0:T(8,128)(2,1)S(1)}, u32[]{:S(2)}, u32[]{:S(2)}) %collective-permute-start.14) | collective-permute-done | bytes 2097184 | tf_op jit(solution)/shard_map/ppermute | solution.py:374
  600.4 14.0 %project_rows.35 = (bf16[256,4096]{1,0:T(8,128)(2,1)}, bf16[256,4096]{1,0:T(8,128)(2,1)}) custom-call(s32[8]{0:T(128)} %stack.113.table_ref, bf16[1024,1792]{1,0:T(8,128)(2,1)} %expand.8.refs_0_.refs_1_.refs_2_.refs_3_, bf16[1024,1792]{1,0:T(8,128)(2,1)} %expand.8.refs_0_.refs_1_.refs_2_.refs_3_, bf16[1024,1792]{1,0:T(8,128)(2,1)} %expand.8.refs_0_.refs_1_.refs_2_.refs_3_, ...), custom_call_target="tpu_custom_call" | custom-call | flops 7516192768 | bytes 20709376 | tf_op jit(solution)/shard_map/project_rows/pallas_call | solution.py:247
  632.4 37.6 %attend.9.refs_0_.refs_1_.refs_2_.refs_3_ = bf16[1024,512]{1,0:T(8,128)(2,1)} custom-call(s32[3]{0:T(128)} %start_ref.13, bf16[1024,512]{1,0:T(8,128)(2,1)} %get-tuple-element.220.q_ref, bf16[1024,128]{1,0:T(8,128)(2,1)} %get-tuple-element.221.kn_ref, bf16[1024,128]{1,0:T(8,128)(2,1)} %get-tuple-element.222.vn_ref, bf16[2,3,4096,128]{3,2,1,0:T(8,128)(2,1)} %bitcast.50, ...), custom_call_target="tpu_custom_call" | custom-call | flops 21474836480 | bytes 4718592 | tf_op jit(solution)/shard_map/attend/pallas_call | solution.py:179
  677.8 26.0 %collective-permute-done.15.refs_2_ = bf16[256,4096]{1,0:T(8,128)(2,1)S(1)} collective-permute-done((bf16[256,4096]{1,0:T(8,128)(2,1)}, bf16[256,4096]{1,0:T(8,128)(2,1)S(1)}, u32[]{:S(2)}, u32[]{:S(2)}) %collective-permute-start.15) | collective-permute-done | bytes 2097184 | tf_op jit(solution)/shard_map/ppermute | solution.py:374
  738.0 37.6 %attend.10.refs_0_.refs_1_.refs_2_.refs_3_ = bf16[1024,512]{1,0:T(8,128)(2,1)} custom-call(s32[3]{0:T(128)} %start_ref.13, bf16[1024,512]{1,0:T(8,128)(2,1)} %get-tuple-element.235.q_ref, bf16[1024,128]{1,0:T(8,128)(2,1)} %get-tuple-element.236.kn_ref, bf16[1024,128]{1,0:T(8,128)(2,1)} %get-tuple-element.237.vn_ref, bf16[2,3,4096,128]{3,2,1,0:T(8,128)(2,1)} %bitcast.51, ...), custom_call_target="tpu_custom_call" | custom-call | flops 21474836480 | bytes 4718592 | tf_op jit(solution)/shard_map/attend/pallas_call | solution.py:179
  783.1 26.2 %collective-permute-done.19.refs_2_ = bf16[256,4096]{1,0:T(8,128)(2,1)S(1)} collective-permute-done((bf16[256,4096]{1,0:T(8,128)(2,1)}, bf16[256,4096]{1,0:T(8,128)(2,1)S(1)}, u32[]{:S(2)}, u32[]{:S(2)}) %collective-permute-start.19) | collective-permute-done | bytes 2097184 | tf_op jit(solution)/shard_map/ppermute | solution.py:374
  844.0 37.6 %attend.11.refs_0_.refs_1_.refs_2_.refs_3_ = bf16[1024,512]{1,0:T(8,128)(2,1)} custom-call(s32[3]{0:T(128)} %start_ref.13, bf16[1024,512]{1,0:T(8,128)(2,1)} %get-tuple-element.247.q_ref, bf16[1024,128]{1,0:T(8,128)(2,1)} %get-tuple-element.248.kn_ref, bf16[1024,128]{1,0:T(8,128)(2,1)} %get-tuple-element.249.vn_ref, bf16[2,3,4096,128]{3,2,1,0:T(8,128)(2,1)} %bitcast.52, ...), custom_call_target="tpu_custom_call" | custom-call | flops 21474836480 | bytes 4718592 | tf_op jit(solution)/shard_map/attend/pallas_call | solution.py:179
  889.1 26.2 %collective-permute-done.23.refs_2_ = bf16[256,4096]{1,0:T(8,128)(2,1)S(1)} collective-permute-done((bf16[256,4096]{1,0:T(8,128)(2,1)}, bf16[256,4096]{1,0:T(8,128)(2,1)S(1)}, u32[]{:S(2)}, u32[]{:S(2)}) %collective-permute-start.23) | collective-permute-done | bytes 2097184 | tf_op jit(solution)/shard_map/ppermute | solution.py:374
  936.9 26.6 %expand.9.refs_0_.refs_1_.refs_2_.refs_3_ = bf16[1024,1792]{1,0:T(8,128)(2,1)} custom-call(bf16[1024,4096]{1,0:T(8,128)(2,1)} %all-gather.31.cloned.1.call-done.x_ref, bf16[2,4096,1792]{2,1,0:T(8,128)(2,1)} %weight_ref.11, bf16[2,1,1792]{2,1,0:T(2,128)(2,1)} %copy.37.bias_ref), custom_call_target="tpu_custom_call" | custom-call | flops 15032385536 | bytes 41418752 | tf_op jit(solution)/shard_map/expand/pallas_call | solution.py:274
  963.5 14.1 %project_rows.42 = bf16[512,4096]{1,0:T(8,128)(2,1)} custom-call(s32[8]{0:T(128)} %stack.113.table_ref, bf16[1024,1792]{1,0:T(8,128)(2,1)} %expand.9.refs_0_.refs_1_.refs_2_.refs_3_, bf16[1024,1792]{1,0:T(8,128)(2,1)} %expand.9.refs_0_.refs_1_.refs_2_.refs_3_, bf16[1024,1792]{1,0:T(8,128)(2,1)} %expand.9.refs_0_.refs_1_.refs_2_.refs_3_, ...), custom_call_target="tpu_custom_call" | custom-call | flops 7516192768 | bytes 20709376 | tf_op jit(solution)/shard_map/project_rows/pallas_call | solution.py:247
  977.7 14.9 %collective-permute-done.24.refs_2_ = bf16[256,4096]{1,0:T(8,128)(2,1)} collective-permute-done((bf16[256,4096]{1,0:T(8,128)(2,1)}, bf16[256,4096]{1,0:T(8,128)(2,1)}, u32[]{:S(2)}, u32[]{:S(2)}) %collective-permute-start.24) | collective-permute-done | bytes 2097184 | tf_op jit(solution)/shard_map/ppermute | solution.py:374
  994.1 14.8 %collective-permute-done.26.refs_3_ = bf16[128,4096]{1,0:T(8,128)(2,1)S(1)} collective-permute-done((bf16[128,4096]{1,0:T(8,128)(2,1)S(1)}, bf16[128,4096]{1,0:T(8,128)(2,1)S(1)}, u32[]{:S(2)}, u32[]{:S(2)}) %collective-permute-start.26) | collective-permute-done | bytes 1048608 | tf_op jit(solution)/shard_map/ppermute | solution.py:374
  1014.2 26.4 %expand.10.refs_0_.refs_1_.refs_2_.refs_3_ = bf16[1024,1792]{1,0:T(8,128)(2,1)} custom-call(bf16[1024,4096]{1,0:T(8,128)(2,1)} %all-gather.35.cloned.1.call-done.x_ref, bf16[2,4096,1792]{2,1,0:T(8,128)(2,1)} %weight_ref.11, bf16[2,1,1792]{2,1,0:T(2,128)(2,1)} %copy.37.bias_ref), custom_call_target="tpu_custom_call" | custom-call | flops 15032385536 | bytes 41418752 | tf_op jit(solution)/shard_map/expand/pallas_call | solution.py:274
  1068.7 14.2 %project_rows.45 = (bf16[256,4096]{1,0:T(8,128)(2,1)}, bf16[256,4096]{1,0:T(8,128)(2,1)}) custom-call(s32[8]{0:T(128)} %stack.113.table_ref, bf16[1024,1792]{1,0:T(8,128)(2,1)} %expand.10.refs_0_.refs_1_.refs_2_.refs_3_, bf16[1024,1792]{1,0:T(8,128)(2,1)} %expand.10.refs_0_.refs_1_.refs_2_.refs_3_, ...), custom_call_target="tpu_custom_call" | custom-call | flops 7516192768 | bytes 20709376 | tf_op jit(solution)/shard_map/project_rows/pallas_call | solution.py:247
  1082.9 25.6 %expand.11.refs_0_.refs_1_.refs_2_.refs_3_ = bf16[1024,1792]{1,0:T(8,128)(2,1)} custom-call(bf16[1024,4096]{1,0:T(8,128)(2,1)} %all-gather.33.cloned.1.call-done.x_ref, bf16[2,4096,1792]{2,1,0:T(8,128)(2,1)} %weight_ref.11, bf16[2,1,1792]{2,1,0:T(2,128)(2,1)} %copy.37.bias_ref), custom_call_target="tpu_custom_call" | custom-call | flops 15032385536 | bytes 41418752 | tf_op jit(solution)/shard_map/expand/pallas_call | solution.py:274
  1125.2 23.4 %collective-permute-done.31 = bf16[256,4096]{1,0:T(8,128)(2,1)S(1)} collective-permute-done((bf16[256,4096]{1,0:T(8,128)(2,1)}, bf16[256,4096]{1,0:T(8,128)(2,1)S(1)}, u32[]{:S(2)}, u32[]{:S(2)}) %collective-permute-start.31) | collective-permute-done | bytes 2097184 | tf_op jit(solution)/shard_map/ppermute | solution.py:374
  1150.1 21.0 %collective-permute-done.30 = bf16[256,4096]{1,0:T(8,128)(2,1)S(1)} collective-permute-done((bf16[256,4096]{1,0:T(8,128)(2,1)}, bf16[256,4096]{1,0:T(8,128)(2,1)S(1)}, u32[]{:S(2)}, u32[]{:S(2)}) %collective-permute-start.30) | collective-permute-done | bytes 2097184 | tf_op jit(solution)/shard_map/ppermute | solution.py:374
  1172.8 14.0 %project_rows.47 = (bf16[256,4096]{1,0:T(8,128)(2,1)}, bf16[256,4096]{1,0:T(8,128)(2,1)}) custom-call(s32[8]{0:T(128)} %stack.113.table_ref, bf16[1024,1792]{1,0:T(8,128)(2,1)} %expand.11.refs_0_.refs_1_.refs_2_.refs_3_, bf16[1024,1792]{1,0:T(8,128)(2,1)} %expand.11.refs_0_.refs_1_.refs_2_.refs_3_, ...), custom_call_target="tpu_custom_call" | custom-call | flops 7516192768 | bytes 20709376 | tf_op jit(solution)/shard_map/project_rows/pallas_call | solution.py:247
  1196.4 27.9 %collective-permute-done.32 = bf16[256,4096]{1,0:T(8,128)(2,1)S(1)} collective-permute-done((bf16[256,4096]{1,0:T(8,128)(2,1)}, bf16[256,4096]{1,0:T(8,128)(2,1)S(1)}, u32[]{:S(2)}, u32[]{:S(2)}) %collective-permute-start.32) | collective-permute-done | bytes 2097184 | tf_op jit(solution)/shard_map/ppermute | solution.py:374
  1229.5 15.7 %write_caches.1 = (bf16[2,3,4096,128]{3,2,1,0:T(8,128)(2,1)}, bf16[2,3,4096,128]{3,2,1,0:T(8,128)(2,1)}) custom-call(s32[3]{0:T(128)} %start_ref.13, bf16[2,3,4096,128]{3,2,1,0:T(8,128)(2,1)} %bitcast.53, bf16[2,3,4096,128]{3,2,1,0:T(8,128)(2,1)} %bitcast.60, bf16[2,3,1024,128]{3,2,1,0:T(8,128)(2,1)} %get-tuple-element.310.kn_ref, ...), custom_call_target="tpu_custom_call" | custom-call | flops 16777216 | bytes 25165824 | tf_op jit(solution)/shard_map/write_caches/pallas_call | solution.py:315
  (275 shorter events, 417.9 us)
Async XLA Ops:
  7.2 54.7 %all-gather.15.cloned.1.call-start = ((), (), s32[]{:S(2)}) async-start(), calls=%async_computation.1 | async-start | bytes 9437184 | tf_op jit(solution)/shard_map/all_gather | solution.py:377
  10.2 124.3 %all-gather.17.cloned.1.call-start = ((), (), s32[]{:S(2)}) async-start(), calls=%async_computation.2 | async-start | bytes 9437184 | tf_op jit(solution)/shard_map/all_gather | solution.py:377
  13.3 228.1 %all-gather.13.cloned.1.call-start = ((), (), s32[]{:S(2)}) async-start(), calls=%async_computation | async-start | bytes 9437184 | tf_op jit(solution)/shard_map/all_gather | solution.py:377
  16.3 331.1 %all-gather.19.cloned.1.call-start = ((), (), s32[]{:S(2)}) async-start(), calls=%async_computation.3 | async-start | bytes 9437184 | tf_op jit(solution)/shard_map/all_gather | solution.py:377
  193.4 28.8 %collective-permute-start.3 = (bf16[512,4096]{1,0:T(8,128)(2,1)}, bf16[512,4096]{1,0:T(8,128)(2,1)}, u32[]{:S(2)}, u32[]{:S(2)}) collective-permute-start(bf16[512,4096]{1,0:T(8,128)(2,1)} %project_rows.26), channel_id=1, source_target_pairs={{0,1},{1,0},{2,3},{3,2},{4,5},{5,4},{6,7},{7,6}} | collective-permute-start | bytes 12582920 | tf_op jit(solution)/shard_map/ppermute | solution.py:374
  241.3 196.4 %all-gather.23.cloned.1.call-start = ((), (), s32[]{:S(2)}) async-start(), calls=%async_computation.5 | async-start | bytes 9437184 | tf_op jit(solution)/shard_map/all_gather | solution.py:377
  299.0 27.7 %collective-permute-start.4 = (bf16[512,4096]{1,0:T(8,128)(2,1)}, bf16[512,4096]{1,0:T(8,128)(2,1)}, u32[]{:S(2)}, u32[]{:S(2)}) collective-permute-start(bf16[512,4096]{1,0:T(8,128)(2,1)} %project_rows.28), channel_id=1, source_target_pairs={{0,1},{1,0},{2,3},{3,2},{4,5},{5,4},{6,7},{7,6}} | collective-permute-start | bytes 12582920 | tf_op jit(solution)/shard_map/ppermute | solution.py:374
  299.0 26.3 %collective-permute-start.5 = (bf16[256,4096]{1,0:T(8,128)(2,1)}, bf16[256,4096]{1,0:T(8,128)(2,1)S(1)}, u32[]{:S(2)}, u32[]{:S(2)}) collective-permute-start(bf16[256,4096]{1,0:T(8,128)(2,1)} %get-tuple-element.176), channel_id=1, source_target_pairs={{0,2},{1,5},{2,0},{3,7},{4,6},{5,1},{6,4},{7,3}} | collective-permute-start | bytes 6291464 | tf_op jit(solution)/shard_map/ppermute | solution.py:374
  346.8 182.5 %all-gather.21.cloned.1.call-start = ((), (), s32[]{:S(2)}) async-start(), calls=%async_computation.4 | async-start | bytes 9437184 | tf_op jit(solution)/shard_map/all_gather | solution.py:377
  387.8 30.6 %collective-permute-start.9 = (bf16[512,4096]{1,0:T(8,128)(2,1)}, bf16[512,4096]{1,0:T(8,128)(2,1)}, u32[]{:S(2)}, u32[]{:S(2)}) collective-permute-start(bf16[512,4096]{1,0:T(8,128)(2,1)} %project_rows.30), channel_id=1, source_target_pairs={{0,1},{1,0},{2,3},{3,2},{4,5},{5,4},{6,7},{7,6}} | collective-permute-start | bytes 12582920 | tf_op jit(solution)/shard_map/ppermute | solution.py:374
  387.8 27.8 %collective-permute-start.6 = (bf16[256,4096]{1,0:T(8,128)(2,1)}, bf16[256,4096]{1,0:T(8,128)(2,1)S(1)}, u32[]{:S(2)}, u32[]{:S(2)}) collective-permute-start(bf16[256,4096]{1,0:T(8,128)(2,1)} %get-tuple-element.181), channel_id=1, source_target_pairs={{0,2},{1,5},{2,0},{3,7},{4,6},{5,1},{6,4},{7,3}} | collective-permute-start | bytes 6291464 | tf_op jit(solution)/shard_map/ppermute | solution.py:374
  437.7 182.1 %all-gather.25.cloned.1.call-start = ((), (), s32[]{:S(2)}) async-start(), calls=%async_computation.6 | async-start | bytes 9437184 | tf_op jit(solution)/shard_map/all_gather | solution.py:377
  478.1 31.8 %collective-permute-start.12 = (bf16[512,4096]{1,0:T(8,128)(2,1)}, bf16[512,4096]{1,0:T(8,128)(2,1)}, u32[]{:S(2)}, u32[]{:S(2)}) collective-permute-start(bf16[512,4096]{1,0:T(8,128)(2,1)} %project_rows.32), channel_id=1, source_target_pairs={{0,1},{1,0},{2,3},{3,2},{4,5},{5,4},{6,7},{7,6}} | collective-permute-start | bytes 12582920 | tf_op jit(solution)/shard_map/ppermute | solution.py:374
  478.1 28.3 %collective-permute-start.10 = (bf16[256,4096]{1,0:T(8,128)(2,1)}, bf16[256,4096]{1,0:T(8,128)(2,1)S(1)}, u32[]{:S(2)}, u32[]{:S(2)}) collective-permute-start(bf16[256,4096]{1,0:T(8,128)(2,1)} %get-tuple-element.197), channel_id=1, source_target_pairs={{0,2},{1,5},{2,0},{3,7},{4,6},{5,1},{6,4},{7,3}} | collective-permute-start | bytes 6291464 | tf_op jit(solution)/shard_map/ppermute | solution.py:374
  529.2 196.1 %all-gather.29.cloned.1.call-start = ((), (), s32[]{:S(2)}) async-start(), calls=%async_computation.8 | async-start | bytes 9437184 | tf_op jit(solution)/shard_map/all_gather | solution.py:377
  569.9 30.5 %collective-permute-start.13 = (bf16[512,4096]{1,0:T(8,128)(2,1)}, bf16[512,4096]{1,0:T(8,128)(2,1)}, u32[]{:S(2)}, u32[]{:S(2)}) collective-permute-start(bf16[512,4096]{1,0:T(8,128)(2,1)} %project_rows.34), channel_id=1, source_target_pairs={{0,1},{1,0},{2,3},{3,2},{4,5},{5,4},{6,7},{7,6}} | collective-permute-start | bytes 12582920 | tf_op jit(solution)/shard_map/ppermute | solution.py:374
  570.0 27.6 %collective-permute-start.14 = (bf16[256,4096]{1,0:T(8,128)(2,1)}, bf16[256,4096]{1,0:T(8,128)(2,1)S(1)}, u32[]{:S(2)}, u32[]{:S(2)}) collective-permute-start(bf16[256,4096]{1,0:T(8,128)(2,1)} %get-tuple-element.208), channel_id=1, source_target_pairs={{0,2},{1,5},{2,0},{3,7},{4,6},{5,1},{6,4},{7,3}} | collective-permute-start | bytes 6291464 | tf_op jit(solution)/shard_map/ppermute | solution.py:374
  619.8 211.0 %all-gather.27.cloned.1.call-start = ((), (), s32[]{:S(2)}) async-start(), calls=%async_computation.7 | async-start | bytes 9437184 | tf_op jit(solution)/shard_map/all_gather | solution.py:377
  677.5 28.2 %collective-permute-start.18 = (bf16[512,4096]{1,0:T(8,128)(2,1)}, bf16[512,4096]{1,0:T(8,128)(2,1)}, u32[]{:S(2)}, u32[]{:S(2)}) collective-permute-start(bf16[512,4096]{1,0:T(8,128)(2,1)} %project_rows.36), channel_id=1, source_target_pairs={{0,1},{1,0},{2,3},{3,2},{4,5},{5,4},{6,7},{7,6}} | collective-permute-start | bytes 12582920 | tf_op jit(solution)/shard_map/ppermute | solution.py:374
  677.5 26.3 %collective-permute-start.15 = (bf16[256,4096]{1,0:T(8,128)(2,1)}, bf16[256,4096]{1,0:T(8,128)(2,1)S(1)}, u32[]{:S(2)}, u32[]{:S(2)}) collective-permute-start(bf16[256,4096]{1,0:T(8,128)(2,1)} %get-tuple-element.213), channel_id=1, source_target_pairs={{0,2},{1,5},{2,0},{3,7},{4,6},{5,1},{6,4},{7,3}} | collective-permute-start | bytes 6291464 | tf_op jit(solution)/shard_map/ppermute | solution.py:374
  725.2 211.6 %all-gather.31.cloned.1.call-start = ((), (), s32[]{:S(2)}) async-start(), calls=%async_computation.9 | async-start | bytes 9437184 | tf_op jit(solution)/shard_map/all_gather | solution.py:377
  783.0 27.8 %collective-permute-start.21 = (bf16[512,4096]{1,0:T(8,128)(2,1)}, bf16[512,4096]{1,0:T(8,128)(2,1)}, u32[]{:S(2)}, u32[]{:S(2)}) collective-permute-start(bf16[512,4096]{1,0:T(8,128)(2,1)} %project_rows.38), channel_id=1, source_target_pairs={{0,1},{1,0},{2,3},{3,2},{4,5},{5,4},{6,7},{7,6}} | collective-permute-start | bytes 12582920 | tf_op jit(solution)/shard_map/ppermute | solution.py:374
  830.7 183.5 %all-gather.35.cloned.1.call-start = ((), (), s32[]{:S(2)}) async-start(), calls=%async_computation.11 | async-start | bytes 9437184 | tf_op jit(solution)/shard_map/all_gather | solution.py:377
  889.0 27.6 %collective-permute-start.22 = (bf16[512,4096]{1,0:T(8,128)(2,1)}, bf16[512,4096]{1,0:T(8,128)(2,1)}, u32[]{:S(2)}, u32[]{:S(2)}) collective-permute-start(bf16[512,4096]{1,0:T(8,128)(2,1)} %project_rows.40), channel_id=1, source_target_pairs={{0,1},{1,0},{2,3},{3,2},{4,5},{5,4},{6,7},{7,6}} | collective-permute-start | bytes 12582920 | tf_op jit(solution)/shard_map/ppermute | solution.py:374
  889.1 26.3 %collective-permute-start.23 = (bf16[256,4096]{1,0:T(8,128)(2,1)}, bf16[256,4096]{1,0:T(8,128)(2,1)S(1)}, u32[]{:S(2)}, u32[]{:S(2)}) collective-permute-start(bf16[256,4096]{1,0:T(8,128)(2,1)} %get-tuple-element.250), channel_id=1, source_target_pairs={{0,2},{1,5},{2,0},{3,7},{4,6},{5,1},{6,4},{7,3}} | collective-permute-start | bytes 6291464 | tf_op jit(solution)/shard_map/ppermute | solution.py:374
  936.7 146.1 %all-gather.33.cloned.1.call-start = ((), (), s32[]{:S(2)}) async-start(), calls=%async_computation.10 | async-start | bytes 9437184 | tf_op jit(solution)/shard_map/all_gather | solution.py:377
  936.8 55.7 %collective-permute-start.24 = (bf16[256,4096]{1,0:T(8,128)(2,1)}, bf16[256,4096]{1,0:T(8,128)(2,1)}, u32[]{:S(2)}, u32[]{:S(2)}) collective-permute-start(bf16[256,4096]{1,0:T(8,128)(2,1)} %get-tuple-element.255), channel_id=1, source_target_pairs={{0,2},{1,5},{2,0},{3,7},{4,6},{5,1},{6,4},{7,3}} | collective-permute-start | bytes 6291464 | tf_op jit(solution)/shard_map/ppermute | solution.py:374
  1014.1 40.6 %collective-permute-start.28 = (bf16[512,4096]{1,0:T(8,128)(2,1)}, bf16[512,4096]{1,0:T(8,128)(2,1)}, u32[]{:S(2)}, u32[]{:S(2)}) collective-permute-start(bf16[512,4096]{1,0:T(8,128)(2,1)} %project_rows.42), channel_id=1, source_target_pairs={{0,1},{1,0},{2,3},{3,2},{4,5},{5,4},{6,7},{7,6}} | collective-permute-start | bytes 12582920 | tf_op jit(solution)/shard_map/ppermute | solution.py:374
  1122.2 50.5 %collective-permute-start.29 = (bf16[512,4096]{1,0:T(8,128)(2,1)}, bf16[512,4096]{1,0:T(8,128)(2,1)}, u32[]{:S(2)}, u32[]{:S(2)}) collective-permute-start(bf16[512,4096]{1,0:T(8,128)(2,1)} %project_rows.46), channel_id=1, source_target_pairs={{0,1},{1,0},{2,3},{3,2},{4,5},{5,4},{6,7},{7,6}} | collective-permute-start | bytes 12582920 | tf_op jit(solution)/shard_map/ppermute | solution.py:374
  1122.4 48.7 %collective-permute-start.30 = (bf16[256,4096]{1,0:T(8,128)(2,1)}, bf16[256,4096]{1,0:T(8,128)(2,1)S(1)}, u32[]{:S(2)}, u32[]{:S(2)}) collective-permute-start(bf16[256,4096]{1,0:T(8,128)(2,1)} %get-tuple-element.275), channel_id=1, source_target_pairs={{0,2},{1,5},{2,0},{3,7},{4,6},{5,1},{6,4},{7,3}} | collective-permute-start | bytes 6291464 | tf_op jit(solution)/shard_map/ppermute | solution.py:374
  1186.8 37.5 %collective-permute-start.32 = (bf16[256,4096]{1,0:T(8,128)(2,1)}, bf16[256,4096]{1,0:T(8,128)(2,1)S(1)}, u32[]{:S(2)}, u32[]{:S(2)}) collective-permute-start(bf16[256,4096]{1,0:T(8,128)(2,1)} %get-tuple-element.283), channel_id=1, source_target_pairs={{0,2},{1,5},{2,0},{3,7},{4,6},{5,1},{6,4},{7,3}} | collective-permute-start | bytes 6291464 | tf_op jit(solution)/shard_map/ppermute | solution.py:374
  1191.6 53.6 %collective-permute-start.35 = (bf16[128,4096]{1,0:T(8,128)(2,1)}, bf16[128,4096]{1,0:T(8,128)(2,1)}, u32[]{:S(2)}, u32[]{:S(2)}) collective-permute-start(bf16[128,4096]{1,0:T(8,128)(2,1)} %add_convert_fusion.5), channel_id=1, source_target_pairs={{0,4},{1,3},{2,6},{3,1},{4,0},{5,7},{6,2},{7,5}} | collective-permute-start | bytes 3145736 | tf_op jit(solution)/shard_map/ppermute | solution.py:374
  (72 other events, 985.9 us)
Sparse Core Ops, SparseCore 0:
  10.4 51.4 all-gather.14
  63.7 48.6 all-gather.16
  114.3 48.6 all-gather.12
  241.5 48.2 all-gather.18
  346.9 49.4 all-gather.22
  437.8 49.3 all-gather.20
  529.3 49.1 all-gather.24
  619.9 48.0 all-gather.28
  725.3 47.7 all-gather.26
  830.9 47.3 all-gather.30
  936.9 64.8 all-gather.34
  1014.3 47.8 all-gather.32

commit v5 on v4

--- a/solution.py
+++ b/solution.py
@@ -12,7 +12,7 @@
 LOG2E = 1.4426950408889634
 HIDE = -(1 << 30)
 VMEM_LIMIT = 60 << 20
-TURNS = [int(c) for c in '210221212010120201212010120201212010120012102101020']
+TURNS = [int(c) for c in '212021212010120201212010120201212010120201102100120']
 
 
 def norm_kernel(*refs, joined, which):
@@ -97,7 +97,7 @@
     )(acts, cos_tab, sin_tab, w_q, w_k, w_v, b_q[:, None, :], b_k[:, None, :], b_v[:, None, :])
 
 
-def attention_kernel(start_ref, q_ref, kn_ref, vn_ref, ko_ref, vo_ref, held_ref, o_ref, score_ref, *, seq, group, key_block, new_block):
+def attention_kernel(start_ref, q_ref, kn_ref, vn_ref, ko_ref, vo_ref, held_ref, o_ref, score_ref, peak_ref, top_ref, total_ref, mixed_ref, *, seq, group, key_block, new_block):
     rows = q_ref.shape[0]
     head_dim = kn_ref.shape[1]
     window = ko_ref.shape[0]
@@ -108,7 +108,8 @@
     token = block * rows + lax.broadcasted_iota(jnp.int32, (rows, 1), 0)
     token = jnp.concatenate([token] * group, axis=0)
     oldest = start + token - window
-    top_shape = (rows * group, 128)
+    half = rows * group // 2
+    spans = [slice(i * half, (i + 1) * half) for i in range(2)]
 
     def lane_max(values, top):
         for i in range(values.shape[1] // 128):
@@ -124,34 +125,43 @@
 
     def score_old(step, top):
         at = pl.multiple_of(step * key_block, key_block)
-        values = lax.dot_general(query, ko_ref[pl.ds(at, key_block), :], contract, preferred_element_type=jnp.float32)
         held = held_ref[:, pl.ds(at, key_block)]
         held = jnp.where((held >= 0) & (held < start), held, HIDE)
-        values = jnp.where(held > oldest, values, -jnp.inf)
-        score_ref[:, pl.ds(at, key_block)] = values
-        return lane_max(values, top)
+        keys = ko_ref[pl.ds(at, key_block), :]
+        for span in spans:
+            values = lax.dot_general(query[span], keys, contract, preferred_element_type=jnp.float32)
+            values = jnp.where(held > oldest[span], values * scale, -jnp.inf)
+            score_ref[span, pl.ds(at, key_block)] = values
+            peak_ref[span, :] = lane_max(values, peak_ref[span, :])
+        return top
 
     def score_new(step, top):
         at = pl.multiple_of(step * new_block, new_block)
-        values = lax.dot_general(query, kn_ref[pl.ds(at, new_block), :], contract, preferred_element_type=jnp.float32)
         fresh = at + lax.broadcasted_iota(jnp.int32, (1, new_block), 1)
-        values = jnp.where(fresh <= token, values, -jnp.inf)
-        score_ref[:, pl.ds(pl.multiple_of(window + at, new_block), new_block)] = values
-        return lane_max(values, top)
+        keys = kn_ref[pl.ds(at, new_block), :]
+        for span in spans:
+            values = lax.dot_general(query[span], keys, contract, preferred_element_type=jnp.float32)
+            values = jnp.where(fresh <= token[span], values * scale, -jnp.inf)
+            score_ref[span, pl.ds(pl.multiple_of(window + at, new_block), new_block)] = values
+            peak_ref[span, :] = lane_max(values, peak_ref[span, :])
+        return top
 
     old_steps = (jnp.minimum(start, window) + key_block - 1) // key_block
     new_steps = (block * rows + rows + new_block - 1) // new_block
-    top = jnp.full(top_shape, -jnp.inf, jnp.float32)
-    top = lax.fori_loop(0, old_steps, score_old, top)
-    top = lax.fori_loop(0, new_steps, score_new, top)
-    top = jnp.max(top, axis=1, keepdims=True)
+    peak_ref[...] = jnp.full_like(peak_ref, -jnp.inf)
+    lax.fori_loop(0, old_steps, score_old, 0)
+    lax.fori_loop(0, new_steps, score_new, 0)
+    top_ref[...] = jnp.max(peak_ref[...], axis=1, keepdims=True)
+    total_ref[...] = jnp.zeros_like(total_ref)
+    mixed_ref[...] = jnp.zeros_like(mixed_ref)
 
     def weigh(at, size, value_ref, value_at, carry):
-        total, mixed = carry
-        weights = jnp.exp2((score_ref[:, pl.ds(at, size)] - top) * scale)
-        total = lane_sum(weights, total)
-        mixed = mixed + jnp.dot(weights.astype(jnp.bfloat16), value_ref[pl.ds(value_at, size), :], preferred_element_type=jnp.float32)
-        return total, mixed
+        value = value_ref[pl.ds(value_at, size), :]
+        for span in spans:
+            weights = jnp.exp2(score_ref[span, pl.ds(at, size)] - top_ref[span, :])
+            total_ref[span, :] = lane_sum(weights, total_ref[span, :])
+            mixed_ref[span, :] += jnp.dot(weights.astype(jnp.bfloat16), value, preferred_element_type=jnp.float32)
+        return carry
 
     def mix_old(step, carry):
         at = pl.multiple_of(step * key_block, key_block)
@@ -161,10 +171,9 @@
         at = pl.multiple_of(step * new_block, new_block)
         return weigh(pl.multiple_of(window + at, new_block), new_block, vn_ref, at, carry)
 
-    carry = (jnp.zeros(top_shape, jnp.float32), jnp.zeros((rows * group, head_dim), jnp.float32))
-    carry = lax.fori_loop(0, old_steps, mix_old, carry)
-    total, mixed = lax.fori_loop(0, new_steps, mix_new, carry)
-    mixed = (mixed / jnp.sum(total, axis=1, keepdims=True)).astype(jnp.bfloat16)
+    lax.fori_loop(0, old_steps, mix_old, 0)
+    lax.fori_loop(0, new_steps, mix_new, 0)
+    mixed = (mixed_ref[...] / jnp.sum(total_ref[...], axis=1, keepdims=True)).astype(jnp.bfloat16)
     for g in range(group):
         o_ref[:, g * head_dim:(g + 1) * head_dim] = mixed[g * rows:(g + 1) * rows]
 
@@ -183,7 +192,7 @@
             grid=(chunk // rows,),
             in_specs=[pl.BlockSpec((rows, q_cols), lambda i, *_: (i, 0)), whole, whole, cache, cache, pl.BlockSpec((None, 1, window), lambda i, *_: (seq, 0, 0))],
             out_specs=pl.BlockSpec((rows, q_cols), lambda i, *_: (i, 0)),
-            scratch_shapes=[pltpu.VMEM((rows * group, keys), jnp.float32)],
+            scratch_shapes=[pltpu.VMEM((rows * group, keys), jnp.float32), pltpu.VMEM((rows * group, 128), jnp.float32), pltpu.VMEM((rows * group, 1), jnp.float32), pltpu.VMEM((rows * group, 128), jnp.float32), pltpu.VMEM((rows * group, head_dim), jnp.float32)],
         ),
         out_shape=jax.ShapeDtypeStruct((chunk, q_cols), jnp.bfloat16),
         compiler_params=pltpu.CompilerParams(dimension_semantics=('arbitrary',), vmem_limit_bytes=VMEM_LIMIT),
@@ -226,16 +235,15 @@
         sent_ref[...] = total[total.shape[0] // 2:]
 
 
-def project_rows(table, acts, weight, layer, lead, cols, slots=3):
-    chunk, depth = acts.shape
-    model = weight.shape[2]
-    half = chunk // 2
+def project_rows(table, acts, part, weight, layer, lead, cols, slots=4):
+    depth, model = weight.shape[1:]
     shards = table.shape[0] // 2
-    part = half // shards
-    first = shards if lead is None else 0
+    picked = acts.shape[0] // part == shards
+    half = part * shards
+    first = 0 if picked or lead is not None else shards
     out = lambda rows: pl.BlockSpec((rows, cols), lambda i, *_: (0, i))
     shape = lambda rows: jax.ShapeDtypeStruct((rows, model), jnp.bfloat16)
-    shard = lambda at: pl.BlockSpec((part, depth), lambda i, places: (places[at], 0))
+    shard = lambda at: pl.BlockSpec((part, depth), lambda i, places: (at if picked else places[at], 0))
     in_specs = [shard(first + k) for k in range(shards)] + [pl.BlockSpec(memory_space=pl.ANY)]
     args = [table] + [acts] * shards + [weight]
     if lead is None:
@@ -260,28 +268,36 @@
     )(*args)
 
 
-def expand_kernel(x_ref, weight_ref, bias_ref, out_ref, ring_ref, sem_ref, *, layer, blocks, tiles):
-    step = pl.program_id(0) * tiles + pl.program_id(1)
-    weight = stream_tile(weight_ref, ring_ref, sem_ref, step, blocks * tiles, layer, tiles)
-    lifted = jnp.dot(x_ref[...], weight, preferred_element_type=jnp.float32) + bias_ref[...].astype(jnp.float32)
+def expand_kernel(table_ref, *refs, shards, layer, tiles):
+    x_refs, (weight_ref, bias_ref, out_ref, ring_ref, sem_ref) = refs[:shards], refs[shards:]
+    weight = stream_tile(weight_ref, ring_ref, sem_ref, pl.program_id(0), tiles, layer, tiles)
+    acts = jnp.concatenate([ref[...] for ref in x_refs], axis=0)
+    lifted = jnp.dot(acts, weight, preferred_element_type=jnp.float32) + bias_ref[...].astype(jnp.float32)
     out_ref[...] = jax.nn.gelu(lifted, approximate=True).astype(jnp.bfloat16)
 
 
-def expand_rows(acts, weight, bias, layer, rows=512, cols=896, slots=2):
+def expand_rows(table, acts, weight, bias, layer, first, cols=256, slots=4):
     chunk, model = acts.shape
     width = weight.shape[2]
-    blocks, tiles = chunk // rows, width // cols
-    return pl.pallas_call(
-        functools.partial(expand_kernel, layer=layer, blocks=blocks, tiles=tiles),
-        grid=(blocks, tiles),
-        in_specs=[pl.BlockSpec((rows, model), lambda i, j: (i, 0)), pl.BlockSpec(memory_space=pl.ANY), pl.BlockSpec((None, 1, cols), lambda i, j: (layer, 0, j))],
-        out_specs=pl.BlockSpec((rows, cols), lambda i, j: (i, j)),
-        scratch_shapes=[pltpu.VMEM((slots, model, cols), jnp.bfloat16), pltpu.SemaphoreType.DMA((slots,))],
-        out_shape=jax.ShapeDtypeStruct((chunk, width), jnp.bfloat16),
-        compiler_params=pltpu.CompilerParams(dimension_semantics=('arbitrary', 'arbitrary'), vmem_limit_bytes=VMEM_LIMIT),
-        cost_estimate=pl.CostEstimate(flops=2 * chunk * model * width, bytes_accessed=2 * (chunk * model + blocks * model * width + chunk * width), transcendentals=0),
+    tiles = width // cols
+    shards = table.shape[0] // 2
+    part = chunk // table.shape[0]
+    rows = part * shards
+    shard = lambda at: pl.BlockSpec((part, model), lambda i, places: (places[at], 0))
+    return pl.pallas_call(
+        functools.partial(expand_kernel, shards=shards, layer=layer, tiles=tiles),
+        grid_spec=pltpu.PrefetchScalarGridSpec(
+            num_scalar_prefetch=1,
+            grid=(tiles,),
+            in_specs=[shard(first + k) for k in range(shards)] + [pl.BlockSpec(memory_space=pl.ANY), pl.BlockSpec((None, 1, cols), lambda i, *_: (layer, 0, i))],
+            out_specs=pl.BlockSpec((rows, cols), lambda i, *_: (0, i)),
+            scratch_shapes=[pltpu.VMEM((slots, model, cols), jnp.bfloat16), pltpu.SemaphoreType.DMA((slots,))],
+        ),
+        out_shape=jax.ShapeDtypeStruct((rows, width), jnp.bfloat16),
+        compiler_params=pltpu.CompilerParams(dimension_semantics=('arbitrary',), vmem_limit_bytes=VMEM_LIMIT),
+        cost_estimate=pl.CostEstimate(flops=2 * rows * model * width, bytes_accessed=2 * (rows * model + model * width + rows * width), transcendentals=0),
         name='expand',
-    )(acts, weight, bias)
+    )(table, *[acts] * shards, weight, bias)
 
 
 def cache_kernel(start_ref, ko_ref, vo_ref, kn_ref, vn_ref, kout_ref, vout_ref, ring_ref):
@@ -381,10 +397,10 @@
         def add_came(kept, came):
             return ((kept[part:].astype(jnp.float32) + came[part:].astype(jnp.float32)).astype(jnp.bfloat16),)
 
-        def scatter_sum(lead, acts, weight, layer, cols):
+        def scatter_sum(lead, acts, make_acts, weight, layer, cols):
             lead = send(lead, pairs_core)
             yield
-            kept, sent = item(lambda lead: project_rows(table, acts, weight, layer, lead, cols), lead)
+            kept, sent = item(lambda acts: project_rows(table, make_acts(acts), part, weight, layer, lead, cols), acts)
             came = send(sent, pairs_first)
             yield
             onward, = item(add_came, kept, came)
@@ -397,13 +413,13 @@
             fresh_keys[layer][seq] = key_new
             fresh_values[layer][seq] = value_new
             mixed = attend(query, key_new, value_new, keys_in, values_in, held, start_pos, layer, seq)
-            lead, = project_rows(table, mixed, w_o, layer, None, 2048)
+            lead, = project_rows(table, mixed, part, w_o, layer, None, 1024)
             return lead, mixed
 
         def expand(gathered, layer):
-            active = expand_rows(gathered, w_up, up_bias, layer)
-            lead, = project_rows(table, active, w_down, layer, None, 1024)
-            return lead, active
+            active = expand_rows(table, gathered, w_up, up_bias, layer, count // 2)
+            lead, = project_rows(table, active, part, w_down, layer, None, 512)
+            return lead, gathered
 
         def finish(middle, kept, came, last):
             summed = kept[:part].astype(jnp.float32) + came[:part].astype(jnp.float32) + last.astype(jnp.float32)
@@ -425,13 +441,13 @@
                 gathered = gather(normed)
                 yield
                 lead, own = item(functools.partial(attention, layer=layer, seq=seq), gathered)
-                terms = yield from scatter_sum(lead, own, w_o, layer, 2048)
+                terms = yield from scatter_sum(lead, own, lambda mixed: mixed, w_o, layer, 1024)
                 seq_of[0] = seq
                 normed, middle = item(lambda *terms: join(base, *terms, bias=out_bias, layer=layer, which=2), *terms)
                 gathered = gather(normed)
                 yield
                 lead, own = item(functools.partial(expand, layer=layer), gathered)
-                terms = yield from scatter_sum(lead, own, w_down, layer, 1024)
+                terms = yield from scatter_sum(lead, own, lambda acts: expand_rows(table, acts, w_up, up_bias, layer, 0), w_down, layer, 512)
                 if layer + 1 < layers:
                     seq_of[0] = seq
                     normed, base = item(lambda *terms: join(middle, *terms, bias=down_bias, layer=layer, which=4), *terms)

time: 1270 us -> 1290 us (1.016)
  waiting for transfers between devices: 396 us -> 417 us
    pallas_call x6, Pallas kernels: 226 us -> 198 us  [attend(): pl.pallas_call(functools.partial(attention_kernel, seq=seq, group=group,...]
    pallas_call x6 -> x12, Pallas kernels: 159 us -> 181 us  [expand_rows(): pl.pallas_call(functools.partial(expand_kernel, shards=shards, layer=laye...]
    ppermute x36, waiting for transfers between devices: 353 us -> 374 us  [send(): return lax.ppermute(value, 'tp', pairs)]
  transfers between devices with their start and end apart: 48 -> 48, of which waited for: 20 -> 19; matrix products, arithmetic and copies ran while one was open for 2% -> 2% of each run, Pallas kernels for 59% -> 60%
where the time goes in v5:
time: 1290 us; the launch traced here: 1280 us
  Pallas kernels  778 us (60%)
  waiting for transfers between devices  417 us (32%)
  local copies, waits for them, and re-layouts  24.8 us (2%)
  starting transfers between devices  21.3 us (2%)
  other arithmetic  20.3 us (2%)
  between operations  15.8 us (1%)
    ppermute x36, waiting for transfers between devices, send(): return lax.ppermute(value, 'tp', pairs)  374 us
    pallas_call x24, Pallas kernels, project_rows(): pl.pallas_call(functools.partial(project_kernel, shards=shards, joined=le...  261 us
    pallas_call x6, Pallas kernels, attend(): pl.pallas_call(functools.partial(attention_kernel, seq=seq, group=group,...  198 us
    pallas_call x12, Pallas kernels, expand_rows(): pl.pallas_call(functools.partial(expand_kernel, shards=shards, layer=laye...  181 us
    pallas_call x6, Pallas kernels, qkv_project(): pl.pallas_call(qkv_kernel, grid=(chunk // rows,), in_specs=[row_block(mod...  75.1 us
    pallas_call x12, Pallas kernels, normalize(): pl.pallas_call(functools.partial(norm_kernel, joined=terms is not None, w...  47.6 us
    all_gather x12, waiting for transfers between devices, gather(): return lax.all_gather(value, 'tp', axis=0, tiled=True)  42.6 us
  transfers between devices with their start and end apart: 48, of which 19 were waited for; matrix products, arithmetic and copies ran while one was open for 2% of the time, Pallas kernels for 60%

profile of v5, /device:TPU:0, one launch (start us, length us, event | category | flops | bytes accessed | tf_op | source)
XLA Modules:
  0.0 1277.0 jit_solution(14919388786876416837)
XLA Ops:
  19.4 42.5 %all-gather.15.cloned.1.call-done.x_ref = bf16[1024,4096]{1,0:T(8,128)(2,1)} async-done(((bf16[128,4096]{1,0:T(8,128)(2,1)}), bf16[1024,4096]{1,0:T(8,128)(2,1)}) %all-gather.15.cloned.1.call-update) | async-done | bytes 8388624 | tf_op jit(solution)/shard_map/all_gather | solution.py:393
  74.1 32.9 %attend.6.refs_0_.refs_1_.refs_2_.refs_3_ = bf16[1024,512]{1,0:T(8,128)(2,1)} custom-call(s32[3]{0:T(128)} %start_ref.13, bf16[1024,512]{1,0:T(8,128)(2,1)} %get-tuple-element.154.q_ref, bf16[1024,128]{1,0:T(8,128)(2,1)} %get-tuple-element.155.kn_ref, bf16[1024,128]{1,0:T(8,128)(2,1)} %get-tuple-element.156.vn_ref, bf16[2,3,4096,128]{3,2,1,0:T(8,128)(2,1)} %bitcast.47, ...), custom_call_target="tpu_custom_call" | custom-call | flops 21474836480 | bytes 4718592 | tf_op jit(solution)/shard_map/attend/pallas_call | solution.py:188
  142.1 33.5 %attend.7.refs_0_.refs_1_.refs_2_.refs_3_ = bf16[1024,512]{1,0:T(8,128)(2,1)} custom-call(s32[3]{0:T(128)} %start_ref.13, bf16[1024,512]{1,0:T(8,128)(2,1)} %get-tuple-element.161.q_ref, bf16[1024,128]{1,0:T(8,128)(2,1)} %get-tuple-element.162.kn_ref, bf16[1024,128]{1,0:T(8,128)(2,1)} %get-tuple-element.163.vn_ref, bf16[2,3,4096,128]{3,2,1,0:T(8,128)(2,1)} %bitcast.48, ...), custom_call_target="tpu_custom_call" | custom-call | flops 21474836480 | bytes 4718592 | tf_op jit(solution)/shard_map/attend/pallas_call | solution.py:188
  184.4 25.0 %collective-permute-done.1.refs_2_ = bf16[256,4096]{1,0:T(8,128)(2,1)S(1)} collective-permute-done((bf16[256,4096]{1,0:T(8,128)(2,1)}, bf16[256,4096]{1,0:T(8,128)(2,1)S(1)}, u32[]{:S(2)}, u32[]{:S(2)}) %collective-permute-start.1) | collective-permute-done | bytes 2097184 | tf_op jit(solution)/shard_map/ppermute | solution.py:390
  243.3 32.9 %attend.8.refs_0_.refs_1_.refs_2_.refs_3_ = bf16[1024,512]{1,0:T(8,128)(2,1)} custom-call(s32[3]{0:T(128)} %start_ref.13, bf16[1024,512]{1,0:T(8,128)(2,1)} %get-tuple-element.173.q_ref, bf16[1024,128]{1,0:T(8,128)(2,1)} %get-tuple-element.174.kn_ref, bf16[1024,128]{1,0:T(8,128)(2,1)} %get-tuple-element.175.vn_ref, bf16[2,3,4096,128]{3,2,1,0:T(8,128)(2,1)} %bitcast.49, ...), custom_call_target="tpu_custom_call" | custom-call | flops 21474836480 | bytes 4718592 | tf_op jit(solution)/shard_map/attend/pallas_call | solution.py:188
  284.7 25.3 %collective-permute-done.4.refs_2_ = bf16[256,4096]{1,0:T(8,128)(2,1)S(1)} collective-permute-done((bf16[256,4096]{1,0:T(8,128)(2,1)}, bf16[256,4096]{1,0:T(8,128)(2,1)S(1)}, u32[]{:S(2)}, u32[]{:S(2)}) %collective-permute-start.4) | collective-permute-done | bytes 2097184 | tf_op jit(solution)/shard_map/ppermute | solution.py:390
  332.1 15.3 %expand.12.refs_0_.refs_1_.refs_2_.refs_3_ = bf16[512,1792]{1,0:T(8,128)(2,1)} custom-call(s32[8]{0:T(128)} %stack.113.table_ref, bf16[1024,4096]{1,0:T(8,128)(2,1)} %all-gather.19.cloned.1.call-done.refs_0_.refs_1_.refs_2_.refs_3_, bf16[1024,4096]{1,0:T(8,128)(2,1)} %all-gather.19.cloned.1.call-done.refs_0_.refs_1_.refs_2_.refs_3_, ...), custom_call_target="tpu_custom_call" | custom-call | flops 7516192768 | bytes 20709376 | tf_op jit(solution)/shard_map/expand/pallas_call | solution.py:287
  362.1 38.8 %collective-permute-done.6.refs_2_ = bf16[256,4096]{1,0:T(8,128)(2,1)S(1)} collective-permute-done((bf16[256,4096]{1,0:T(8,128)(2,1)}, bf16[256,4096]{1,0:T(8,128)(2,1)S(1)}, u32[]{:S(2)}, u32[]{:S(2)}) %collective-permute-start.6) | collective-permute-done | bytes 2097184 | tf_op jit(solution)/shard_map/ppermute | solution.py:390
  403.8 14.8 %expand.13.refs_0_.refs_1_.refs_2_.refs_3_ = bf16[512,1792]{1,0:T(8,128)(2,1)} custom-call(s32[8]{0:T(128)} %stack.113.table_ref, bf16[1024,4096]{1,0:T(8,128)(2,1)} %all-gather.19.cloned.1.call-done.refs_0_.refs_1_.refs_2_.refs_3_, bf16[1024,4096]{1,0:T(8,128)(2,1)} %all-gather.19.cloned.1.call-done.refs_0_.refs_1_.refs_2_.refs_3_, ...), custom_call_target="tpu_custom_call" | custom-call | flops 7516192768 | bytes 20709376 | tf_op jit(solution)/shard_map/expand/pallas_call | solution.py:287
  438.2 15.2 %expand.14.refs_0_.refs_1_.refs_2_.refs_3_ = bf16[512,1792]{1,0:T(8,128)(2,1)} custom-call(s32[8]{0:T(128)} %stack.113.table_ref, bf16[1024,4096]{1,0:T(8,128)(2,1)} %all-gather.23.cloned.1.call-done.refs_0_.refs_1_.refs_2_.refs_3_, bf16[1024,4096]{1,0:T(8,128)(2,1)} %all-gather.23.cloned.1.call-done.refs_0_.refs_1_.refs_2_.refs_3_, ...), custom_call_target="tpu_custom_call" | custom-call | flops 7516192768 | bytes 20709376 | tf_op jit(solution)/shard_map/expand/pallas_call | solution.py:287
  468.2 38.4 %collective-permute-done.10.refs_2_ = bf16[256,4096]{1,0:T(8,128)(2,1)S(1)} collective-permute-done((bf16[256,4096]{1,0:T(8,128)(2,1)}, bf16[256,4096]{1,0:T(8,128)(2,1)S(1)}, u32[]{:S(2)}, u32[]{:S(2)}) %collective-permute-start.10) | collective-permute-done | bytes 2097184 | tf_op jit(solution)/shard_map/ppermute | solution.py:390
  509.3 14.9 %expand.15.refs_0_.refs_1_.refs_2_.refs_3_ = bf16[512,1792]{1,0:T(8,128)(2,1)} custom-call(s32[8]{0:T(128)} %stack.113.table_ref, bf16[1024,4096]{1,0:T(8,128)(2,1)} %all-gather.23.cloned.1.call-done.refs_0_.refs_1_.refs_2_.refs_3_, bf16[1024,4096]{1,0:T(8,128)(2,1)} %all-gather.23.cloned.1.call-done.refs_0_.refs_1_.refs_2_.refs_3_, ...), custom_call_target="tpu_custom_call" | custom-call | flops 7516192768 | bytes 20709376 | tf_op jit(solution)/shard_map/expand/pallas_call | solution.py:287
  543.8 15.7 %expand.16.refs_0_.refs_1_.refs_2_.refs_3_ = bf16[512,1792]{1,0:T(8,128)(2,1)} custom-call(s32[8]{0:T(128)} %stack.113.table_ref, bf16[1024,4096]{1,0:T(8,128)(2,1)} %all-gather.21.cloned.1.call-done.refs_0_.refs_1_.refs_2_.refs_3_, bf16[1024,4096]{1,0:T(8,128)(2,1)} %all-gather.21.cloned.1.call-done.refs_0_.refs_1_.refs_2_.refs_3_, ...), custom_call_target="tpu_custom_call" | custom-call | flops 7516192768 | bytes 20709376 | tf_op jit(solution)/shard_map/expand/pallas_call | solution.py:287
  573.6 38.6 %collective-permute-done.13.refs_2_ = bf16[256,4096]{1,0:T(8,128)(2,1)S(1)} collective-permute-done((bf16[256,4096]{1,0:T(8,128)(2,1)}, bf16[256,4096]{1,0:T(8,128)(2,1)S(1)}, u32[]{:S(2)}, u32[]{:S(2)}) %collective-permute-start.13) | collective-permute-done | bytes 2097184 | tf_op jit(solution)/shard_map/ppermute | solution.py:390
  615.0 14.8 %expand.17.refs_0_.refs_1_.refs_2_.refs_3_ = bf16[512,1792]{1,0:T(8,128)(2,1)} custom-call(s32[8]{0:T(128)} %stack.113.table_ref, bf16[1024,4096]{1,0:T(8,128)(2,1)} %all-gather.21.cloned.1.call-done.refs_0_.refs_1_.refs_2_.refs_3_, bf16[1024,4096]{1,0:T(8,128)(2,1)} %all-gather.21.cloned.1.call-done.refs_0_.refs_1_.refs_2_.refs_3_, ...), custom_call_target="tpu_custom_call" | custom-call | flops 7516192768 | bytes 20709376 | tf_op jit(solution)/shard_map/expand/pallas_call | solution.py:287
  661.9 32.9 %attend.9.refs_0_.refs_1_.refs_2_.refs_3_ = bf16[1024,512]{1,0:T(8,128)(2,1)} custom-call(s32[3]{0:T(128)} %start_ref.13, bf16[1024,512]{1,0:T(8,128)(2,1)} %get-tuple-element.220.q_ref, bf16[1024,128]{1,0:T(8,128)(2,1)} %get-tuple-element.221.kn_ref, bf16[1024,128]{1,0:T(8,128)(2,1)} %get-tuple-element.222.vn_ref, bf16[2,3,4096,128]{3,2,1,0:T(8,128)(2,1)} %bitcast.50, ...), custom_call_target="tpu_custom_call" | custom-call | flops 21474836480 | bytes 4718592 | tf_op jit(solution)/shard_map/attend/pallas_call | solution.py:188
  702.4 26.1 %collective-permute-done.15.refs_2_ = bf16[256,4096]{1,0:T(8,128)(2,1)S(1)} collective-permute-done((bf16[256,4096]{1,0:T(8,128)(2,1)}, bf16[256,4096]{1,0:T(8,128)(2,1)S(1)}, u32[]{:S(2)}, u32[]{:S(2)}) %collective-permute-start.15) | collective-permute-done | bytes 2097184 | tf_op jit(solution)/shard_map/ppermute | solution.py:390
  762.9 32.9 %attend.10.refs_0_.refs_1_.refs_2_.refs_3_ = bf16[1024,512]{1,0:T(8,128)(2,1)} custom-call(s32[3]{0:T(128)} %start_ref.13, bf16[1024,512]{1,0:T(8,128)(2,1)} %get-tuple-element.235.q_ref, bf16[1024,128]{1,0:T(8,128)(2,1)} %get-tuple-element.236.kn_ref, bf16[1024,128]{1,0:T(8,128)(2,1)} %get-tuple-element.237.vn_ref, bf16[2,3,4096,128]{3,2,1,0:T(8,128)(2,1)} %bitcast.51, ...), custom_call_target="tpu_custom_call" | custom-call | flops 21474836480 | bytes 4718592 | tf_op jit(solution)/shard_map/attend/pallas_call | solution.py:188
  803.1 26.2 %collective-permute-done.19.refs_2_ = bf16[256,4096]{1,0:T(8,128)(2,1)S(1)} collective-permute-done((bf16[256,4096]{1,0:T(8,128)(2,1)}, bf16[256,4096]{1,0:T(8,128)(2,1)S(1)}, u32[]{:S(2)}, u32[]{:S(2)}) %collective-permute-start.19) | collective-permute-done | bytes 2097184 | tf_op jit(solution)/shard_map/ppermute | solution.py:390
  863.7 32.9 %attend.11.refs_0_.refs_1_.refs_2_.refs_3_ = bf16[1024,512]{1,0:T(8,128)(2,1)} custom-call(s32[3]{0:T(128)} %start_ref.13, bf16[1024,512]{1,0:T(8,128)(2,1)} %get-tuple-element.247.q_ref, bf16[1024,128]{1,0:T(8,128)(2,1)} %get-tuple-element.248.kn_ref, bf16[1024,128]{1,0:T(8,128)(2,1)} %get-tuple-element.249.vn_ref, bf16[2,3,4096,128]{3,2,1,0:T(8,128)(2,1)} %bitcast.52, ...), custom_call_target="tpu_custom_call" | custom-call | flops 21474836480 | bytes 4718592 | tf_op jit(solution)/shard_map/attend/pallas_call | solution.py:188
  904.1 26.2 %collective-permute-done.22.refs_2_ = bf16[256,4096]{1,0:T(8,128)(2,1)S(1)} collective-permute-done((bf16[256,4096]{1,0:T(8,128)(2,1)}, bf16[256,4096]{1,0:T(8,128)(2,1)S(1)}, u32[]{:S(2)}, u32[]{:S(2)}) %collective-permute-start.22) | collective-permute-done | bytes 2097184 | tf_op jit(solution)/shard_map/ppermute | solution.py:390
  951.8 15.6 %expand.18.refs_0_.refs_1_.refs_2_.refs_3_ = bf16[512,1792]{1,0:T(8,128)(2,1)} custom-call(s32[8]{0:T(128)} %stack.113.table_ref, bf16[1024,4096]{1,0:T(8,128)(2,1)} %all-gather.31.cloned.1.call-done.refs_0_.refs_1_.refs_2_.refs_3_, bf16[1024,4096]{1,0:T(8,128)(2,1)} %all-gather.31.cloned.1.call-done.refs_0_.refs_1_.refs_2_.refs_3_, ...), custom_call_target="tpu_custom_call" | custom-call | flops 7516192768 | bytes 20709376 | tf_op jit(solution)/shard_map/expand/pallas_call | solution.py:287
  981.2 38.5 %collective-permute-done.24.refs_2_ = bf16[256,4096]{1,0:T(8,128)(2,1)S(1)} collective-permute-done((bf16[256,4096]{1,0:T(8,128)(2,1)}, bf16[256,4096]{1,0:T(8,128)(2,1)S(1)}, u32[]{:S(2)}, u32[]{:S(2)}) %collective-permute-start.24) | collective-permute-done | bytes 2097184 | tf_op jit(solution)/shard_map/ppermute | solution.py:390
  1022.6 14.8 %expand.19.refs_0_.refs_1_.refs_2_.refs_3_ = bf16[512,1792]{1,0:T(8,128)(2,1)} custom-call(s32[8]{0:T(128)} %stack.113.table_ref, bf16[1024,4096]{1,0:T(8,128)(2,1)} %all-gather.31.cloned.1.call-done.refs_0_.refs_1_.refs_2_.refs_3_, bf16[1024,4096]{1,0:T(8,128)(2,1)} %all-gather.31.cloned.1.call-done.refs_0_.refs_1_.refs_2_.refs_3_, ...), custom_call_target="tpu_custom_call" | custom-call | flops 7516192768 | bytes 20709376 | tf_op jit(solution)/shard_map/expand/pallas_call | solution.py:287
  1056.9 15.2 %expand.20.refs_0_.refs_1_.refs_2_.refs_3_ = bf16[512,1792]{1,0:T(8,128)(2,1)} custom-call(s32[8]{0:T(128)} %stack.113.table_ref, bf16[1024,4096]{1,0:T(8,128)(2,1)} %all-gather.35.cloned.1.call-done.refs_0_.refs_1_.refs_2_.refs_3_, bf16[1024,4096]{1,0:T(8,128)(2,1)} %all-gather.35.cloned.1.call-done.refs_0_.refs_1_.refs_2_.refs_3_, ...), custom_call_target="tpu_custom_call" | custom-call | flops 7516192768 | bytes 20709376 | tf_op jit(solution)/shard_map/expand/pallas_call | solution.py:287
  1086.1 15.0 %expand.21.refs_0_.refs_1_.refs_2_.refs_3_ = bf16[512,1792]{1,0:T(8,128)(2,1)} custom-call(s32[8]{0:T(128)} %stack.113.table_ref, bf16[1024,4096]{1,0:T(8,128)(2,1)} %all-gather.35.cloned.1.call-done.refs_0_.refs_1_.refs_2_.refs_3_, bf16[1024,4096]{1,0:T(8,128)(2,1)} %all-gather.35.cloned.1.call-done.refs_0_.refs_1_.refs_2_.refs_3_, ...), custom_call_target="tpu_custom_call" | custom-call | flops 7516192768 | bytes 20709376 | tf_op jit(solution)/shard_map/expand/pallas_call | solution.py:287
  1115.6 14.8 %expand.22.refs_0_.refs_1_.refs_2_.refs_3_ = bf16[512,1792]{1,0:T(8,128)(2,1)} custom-call(s32[8]{0:T(128)} %stack.113.table_ref, bf16[1024,4096]{1,0:T(8,128)(2,1)} %all-gather.33.cloned.1.call-done.refs_0_.refs_1_.refs_2_.refs_3_, bf16[1024,4096]{1,0:T(8,128)(2,1)} %all-gather.33.cloned.1.call-done.refs_0_.refs_1_.refs_2_.refs_3_, ...), custom_call_target="tpu_custom_call" | custom-call | flops 7516192768 | bytes 20709376 | tf_op jit(solution)/shard_map/expand/pallas_call | solution.py:287
  1147.2 23.3 %collective-permute-done.29 = bf16[256,4096]{1,0:T(8,128)(2,1)S(1)} collective-permute-done((bf16[256,4096]{1,0:T(8,128)(2,1)}, bf16[256,4096]{1,0:T(8,128)(2,1)S(1)}, u32[]{:S(2)}, u32[]{:S(2)}) %collective-permute-start.29) | collective-permute-done | bytes 2097184 | tf_op jit(solution)/shard_map/ppermute | solution.py:390
  1173.2 14.8 %expand.23.refs_0_.refs_1_.refs_2_.refs_3_ = bf16[512,1792]{1,0:T(8,128)(2,1)} custom-call(s32[8]{0:T(128)} %stack.113.table_ref, bf16[1024,4096]{1,0:T(8,128)(2,1)} %all-gather.33.cloned.1.call-done.refs_0_.refs_1_.refs_2_.refs_3_, bf16[1024,4096]{1,0:T(8,128)(2,1)} %all-gather.33.cloned.1.call-done.refs_0_.refs_1_.refs_2_.refs_3_, ...), custom_call_target="tpu_custom_call" | custom-call | flops 7516192768 | bytes 20709376 | tf_op jit(solution)/shard_map/expand/pallas_call | solution.py:287
  1188.1 14.6 %project_rows.47 = (bf16[256,4096]{1,0:T(8,128)(2,1)}, bf16[256,4096]{1,0:T(8,128)(2,1)}) custom-call(s32[8]{0:T(128)} %stack.113.table_ref, bf16[512,1792]{1,0:T(8,128)(2,1)} %expand.23.refs_0_.refs_1_.refs_2_.refs_3_, bf16[512,1792]{1,0:T(8,128)(2,1)} %expand.23.refs_0_.refs_1_.refs_2_.refs_3_, bf16[512,1792]{1,0:T(8,128)(2,1)} %expand.23.refs_0_.refs_1_.refs_2_.refs_3_, ...), custom_call_target="tpu_custom_call" | custom-call | flops 7516192768 | bytes 20709376 | tf_op jit(solution)/shard_map/project_rows/pallas_call | solution.py:255
  1210.2 15.7 %write_caches.1 = (bf16[2,3,4096,128]{3,2,1,0:T(8,128)(2,1)}, bf16[2,3,4096,128]{3,2,1,0:T(8,128)(2,1)}) custom-call(s32[3]{0:T(128)} %start_ref.13, bf16[2,3,4096,128]{3,2,1,0:T(8,128)(2,1)} %bitcast.53, bf16[2,3,4096,128]{3,2,1,0:T(8,128)(2,1)} %bitcast.60, bf16[2,3,1024,128]{3,2,1,0:T(8,128)(2,1)} %get-tuple-element.310.kn_ref, ...), custom_call_target="tpu_custom_call" | custom-call | flops 16777216 | bytes 25165824 | tf_op jit(solution)/shard_map/write_caches/pallas_call | solution.py:331
  1227.3 21.3 %collective-permute-done.32 = bf16[256,4096]{1,0:T(8,128)(2,1)} collective-permute-done((bf16[256,4096]{1,0:T(8,128)(2,1)}, bf16[256,4096]{1,0:T(8,128)(2,1)}, u32[]{:S(2)}, u32[]{:S(2)}) %collective-permute-start.32) | collective-permute-done | bytes 2097184 | tf_op jit(solution)/shard_map/ppermute | solution.py:390
  (277 shorter events, 481.6 us)
Async XLA Ops:
  7.2 54.7 %all-gather.15.cloned.1.call-start = ((), (), s32[]{:S(2)}) async-start(), calls=%async_computation.1 | async-start | bytes 9437184 | tf_op jit(solution)/shard_map/all_gather | solution.py:393
  10.2 119.6 %all-gather.17.cloned.1.call-start = ((), (), s32[]{:S(2)}) async-start(), calls=%async_computation.2 | async-start | bytes 9437184 | tf_op jit(solution)/shard_map/all_gather | solution.py:393
  13.3 217.6 %all-gather.13.cloned.1.call-start = ((), (), s32[]{:S(2)}) async-start(), calls=%async_computation | async-start | bytes 9437184 | tf_op jit(solution)/shard_map/all_gather | solution.py:393
  16.3 315.8 %all-gather.19.cloned.1.call-start = ((), (), s32[]{:S(2)}) async-start(), calls=%async_computation.3 | async-start | bytes 9437184 | tf_op jit(solution)/shard_map/all_gather | solution.py:393
  182.9 29.6 %collective-permute-start.3 = (bf16[512,4096]{1,0:T(8,128)(2,1)}, bf16[512,4096]{1,0:T(8,128)(2,1)}, u32[]{:S(2)}, u32[]{:S(2)}) collective-permute-start(bf16[512,4096]{1,0:T(8,128)(2,1)} %project_rows.26), channel_id=1, source_target_pairs={{0,1},{1,0},{2,3},{3,2},{4,5},{5,4},{6,7},{7,6}} | collective-permute-start | bytes 12582920 | tf_op jit(solution)/shard_map/ppermute | solution.py:390
  230.8 207.4 %all-gather.23.cloned.1.call-start = ((), (), s32[]{:S(2)}) async-start(), calls=%async_computation.5 | async-start | bytes 9437184 | tf_op jit(solution)/shard_map/all_gather | solution.py:393
  283.7 28.6 %collective-permute-start.5 = (bf16[512,4096]{1,0:T(8,128)(2,1)}, bf16[512,4096]{1,0:T(8,128)(2,1)}, u32[]{:S(2)}, u32[]{:S(2)}) collective-permute-start(bf16[512,4096]{1,0:T(8,128)(2,1)} %project_rows.28), channel_id=1, source_target_pairs={{0,1},{1,0},{2,3},{3,2},{4,5},{5,4},{6,7},{7,6}} | collective-permute-start | bytes 12582920 | tf_op jit(solution)/shard_map/ppermute | solution.py:390
  331.4 212.4 %all-gather.21.cloned.1.call-start = ((), (), s32[]{:S(2)}) async-start(), calls=%async_computation.4 | async-start | bytes 9437184 | tf_op jit(solution)/shard_map/all_gather | solution.py:393
  361.2 57.5 %collective-permute-start.9 = (bf16[512,4096]{1,0:T(8,128)(2,1)}, bf16[512,4096]{1,0:T(8,128)(2,1)}, u32[]{:S(2)}, u32[]{:S(2)}) collective-permute-start(bf16[512,4096]{1,0:T(8,128)(2,1)} %project_rows.30), channel_id=1, source_target_pairs={{0,1},{1,0},{2,3},{3,2},{4,5},{5,4},{6,7},{7,6}} | collective-permute-start | bytes 12582920 | tf_op jit(solution)/shard_map/ppermute | solution.py:390
  361.2 39.7 %collective-permute-start.6 = (bf16[256,4096]{1,0:T(8,128)(2,1)}, bf16[256,4096]{1,0:T(8,128)(2,1)S(1)}, u32[]{:S(2)}, u32[]{:S(2)}) collective-permute-start(bf16[256,4096]{1,0:T(8,128)(2,1)} %get-tuple-element.181), channel_id=1, source_target_pairs={{0,2},{1,5},{2,0},{3,7},{4,6},{5,1},{6,4},{7,3}} | collective-permute-start | bytes 6291464 | tf_op jit(solution)/shard_map/ppermute | solution.py:390
  402.3 30.5 %collective-permute-start.8 = (bf16[128,4096]{1,0:T(8,128)(2,1)S(1)}, bf16[128,4096]{1,0:T(8,128)(2,1)S(1)}, u32[]{:S(2)}, u32[]{:S(2)}) collective-permute-start(bf16[128,4096]{1,0:T(8,128)(2,1)S(1)} %add_convert_fusion.12), channel_id=1, source_target_pairs={{0,4},{1,3},{2,6},{3,1},{4,0},{5,7},{6,2},{7,5}} | collective-permute-start | bytes 3145736 | tf_op jit(solution)/shard_map/ppermute | solution.py:390
  438.1 211.4 %all-gather.25.cloned.1.call-start = ((), (), s32[]{:S(2)}) async-start(), calls=%async_computation.6 | async-start | bytes 9437184 | tf_op jit(solution)/shard_map/all_gather | solution.py:393
  467.1 57.1 %collective-permute-start.12 = (bf16[512,4096]{1,0:T(8,128)(2,1)}, bf16[512,4096]{1,0:T(8,128)(2,1)}, u32[]{:S(2)}, u32[]{:S(2)}) collective-permute-start(bf16[512,4096]{1,0:T(8,128)(2,1)} %project_rows.32), channel_id=1, source_target_pairs={{0,1},{1,0},{2,3},{3,2},{4,5},{5,4},{6,7},{7,6}} | collective-permute-start | bytes 12582920 | tf_op jit(solution)/shard_map/ppermute | solution.py:390
  467.2 39.4 %collective-permute-start.10 = (bf16[256,4096]{1,0:T(8,128)(2,1)}, bf16[256,4096]{1,0:T(8,128)(2,1)S(1)}, u32[]{:S(2)}, u32[]{:S(2)}) collective-permute-start(bf16[256,4096]{1,0:T(8,128)(2,1)} %get-tuple-element.197), channel_id=1, source_target_pairs={{0,2},{1,5},{2,0},{3,7},{4,6},{5,1},{6,4},{7,3}} | collective-permute-start | bytes 6291464 | tf_op jit(solution)/shard_map/ppermute | solution.py:390
  507.9 30.6 %collective-permute-start.11 = (bf16[128,4096]{1,0:T(8,128)(2,1)S(1)}, bf16[128,4096]{1,0:T(8,128)(2,1)S(1)}, u32[]{:S(2)}, u32[]{:S(2)}) collective-permute-start(bf16[128,4096]{1,0:T(8,128)(2,1)S(1)} %add_convert_fusion.11), channel_id=1, source_target_pairs={{0,4},{1,3},{2,6},{3,1},{4,0},{5,7},{6,2},{7,5}} | collective-permute-start | bytes 3145736 | tf_op jit(solution)/shard_map/ppermute | solution.py:390
  543.8 206.3 %all-gather.29.cloned.1.call-start = ((), (), s32[]{:S(2)}) async-start(), calls=%async_computation.8 | async-start | bytes 9437184 | tf_op jit(solution)/shard_map/all_gather | solution.py:393
  573.2 56.6 %collective-permute-start.14 = (bf16[512,4096]{1,0:T(8,128)(2,1)}, bf16[512,4096]{1,0:T(8,128)(2,1)}, u32[]{:S(2)}, u32[]{:S(2)}) collective-permute-start(bf16[512,4096]{1,0:T(8,128)(2,1)} %project_rows.34), channel_id=1, source_target_pairs={{0,1},{1,0},{2,3},{3,2},{4,5},{5,4},{6,7},{7,6}} | collective-permute-start | bytes 12582920 | tf_op jit(solution)/shard_map/ppermute | solution.py:390
  573.3 38.9 %collective-permute-start.13 = (bf16[256,4096]{1,0:T(8,128)(2,1)}, bf16[256,4096]{1,0:T(8,128)(2,1)S(1)}, u32[]{:S(2)}, u32[]{:S(2)}) collective-permute-start(bf16[256,4096]{1,0:T(8,128)(2,1)} %get-tuple-element.208), channel_id=1, source_target_pairs={{0,2},{1,5},{2,0},{3,7},{4,6},{5,1},{6,4},{7,3}} | collective-permute-start | bytes 6291464 | tf_op jit(solution)/shard_map/ppermute | solution.py:390
  613.5 30.5 %collective-permute-start.16 = (bf16[128,4096]{1,0:T(8,128)(2,1)S(1)}, bf16[128,4096]{1,0:T(8,128)(2,1)S(1)}, u32[]{:S(2)}, u32[]{:S(2)}) collective-permute-start(bf16[128,4096]{1,0:T(8,128)(2,1)S(1)} %add_convert_fusion.10), channel_id=1, source_target_pairs={{0,4},{1,3},{2,6},{3,1},{4,0},{5,7},{6,2},{7,5}} | collective-permute-start | bytes 3145736 | tf_op jit(solution)/shard_map/ppermute | solution.py:390
  649.4 201.4 %all-gather.27.cloned.1.call-start = ((), (), s32[]{:S(2)}) async-start(), calls=%async_computation.7 | async-start | bytes 9437184 | tf_op jit(solution)/shard_map/all_gather | solution.py:393
  702.2 27.7 %collective-permute-start.18 = (bf16[512,4096]{1,0:T(8,128)(2,1)}, bf16[512,4096]{1,0:T(8,128)(2,1)}, u32[]{:S(2)}, u32[]{:S(2)}) collective-permute-start(bf16[512,4096]{1,0:T(8,128)(2,1)} %project_rows.36), channel_id=1, source_target_pairs={{0,1},{1,0},{2,3},{3,2},{4,5},{5,4},{6,7},{7,6}} | collective-permute-start | bytes 12582920 | tf_op jit(solution)/shard_map/ppermute | solution.py:390
  749.9 201.8 %all-gather.31.cloned.1.call-start = ((), (), s32[]{:S(2)}) async-start(), calls=%async_computation.9 | async-start | bytes 9437184 | tf_op jit(solution)/shard_map/all_gather | solution.py:393
  850.8 206.2 %all-gather.35.cloned.1.call-start = ((), (), s32[]{:S(2)}) async-start(), calls=%async_computation.11 | async-start | bytes 9437184 | tf_op jit(solution)/shard_map/all_gather | solution.py:393
  951.7 163.9 %all-gather.33.cloned.1.call-start = ((), (), s32[]{:S(2)}) async-start(), calls=%async_computation.10 | async-start | bytes 9437184 | tf_op jit(solution)/shard_map/all_gather | solution.py:393
  981.1 56.3 %collective-permute-start.27 = (bf16[512,4096]{1,0:T(8,128)(2,1)}, bf16[512,4096]{1,0:T(8,128)(2,1)}, u32[]{:S(2)}, u32[]{:S(2)}) collective-permute-start(bf16[512,4096]{1,0:T(8,128)(2,1)} %project_rows.42), channel_id=1, source_target_pairs={{0,1},{1,0},{2,3},{3,2},{4,5},{5,4},{6,7},{7,6}} | collective-permute-start | bytes 12582920 | tf_op jit(solution)/shard_map/ppermute | solution.py:390
  981.1 38.6 %collective-permute-start.24 = (bf16[256,4096]{1,0:T(8,128)(2,1)}, bf16[256,4096]{1,0:T(8,128)(2,1)S(1)}, u32[]{:S(2)}, u32[]{:S(2)}) collective-permute-start(bf16[256,4096]{1,0:T(8,128)(2,1)} %get-tuple-element.255), channel_id=1, source_target_pairs={{0,2},{1,5},{2,0},{3,7},{4,6},{5,1},{6,4},{7,3}} | collective-permute-start | bytes 6291464 | tf_op jit(solution)/shard_map/ppermute | solution.py:390
  1021.1 30.5 %collective-permute-start.26 = (bf16[128,4096]{1,0:T(8,128)(2,1)S(1)}, bf16[128,4096]{1,0:T(8,128)(2,1)S(1)}, u32[]{:S(2)}, u32[]{:S(2)}) collective-permute-start(bf16[128,4096]{1,0:T(8,128)(2,1)S(1)} %add_convert_fusion.6), channel_id=1, source_target_pairs={{0,4},{1,3},{2,6},{3,1},{4,0},{5,7},{6,2},{7,5}} | collective-permute-start | bytes 3145736 | tf_op jit(solution)/shard_map/ppermute | solution.py:390
  1085.8 59.9 %collective-permute-start.30 = (bf16[256,4096]{1,0:T(8,128)(2,1)}, bf16[256,4096]{1,0:T(8,128)(2,1)}, u32[]{:S(2)}, u32[]{:S(2)}) collective-permute-start(bf16[256,4096]{1,0:T(8,128)(2,1)} %get-tuple-element.276), channel_id=1, source_target_pairs={{0,2},{1,5},{2,0},{3,7},{4,6},{5,1},{6,4},{7,3}} | collective-permute-start | bytes 6291464 | tf_op jit(solution)/shard_map/ppermute | solution.py:390
  1144.2 43.8 %collective-permute-start.31 = (bf16[512,4096]{1,0:T(8,128)(2,1)}, bf16[512,4096]{1,0:T(8,128)(2,1)}, u32[]{:S(2)}, u32[]{:S(2)}) collective-permute-start(bf16[512,4096]{1,0:T(8,128)(2,1)} %project_rows.46), channel_id=1, source_target_pairs={{0,1},{1,0},{2,3},{3,2},{4,5},{5,4},{6,7},{7,6}} | collective-permute-start | bytes 12582920 | tf_op jit(solution)/shard_map/ppermute | solution.py:390
  1202.7 45.9 %collective-permute-start.32 = (bf16[256,4096]{1,0:T(8,128)(2,1)}, bf16[256,4096]{1,0:T(8,128)(2,1)}, u32[]{:S(2)}, u32[]{:S(2)}) collective-permute-start(bf16[256,4096]{1,0:T(8,128)(2,1)} %get-tuple-element.283), channel_id=1, source_target_pairs={{0,2},{1,5},{2,0},{3,7},{4,6},{5,1},{6,4},{7,3}} | collective-permute-start | bytes 6291464 | tf_op jit(solution)/shard_map/ppermute | solution.py:390
  1207.5 45.4 %collective-permute-start.35 = (bf16[128,4096]{1,0:T(8,128)(2,1)}, bf16[128,4096]{1,0:T(8,128)(2,1)}, u32[]{:S(2)}, u32[]{:S(2)}) collective-permute-start(bf16[128,4096]{1,0:T(8,128)(2,1)} %add_convert_fusion.4), channel_id=1, source_target_pairs={{0,4},{1,3},{2,6},{3,1},{4,0},{5,7},{6,2},{7,5}} | collective-permute-start | bytes 3145736 | tf_op jit(solution)/shard_map/ppermute | solution.py:390
  1225.9 29.4 %collective-permute-start.34 = (bf16[128,4096]{1,0:T(8,128)(2,1)S(1)}, bf16[128,4096]{1,0:T(8,128)(2,1)S(1)}, u32[]{:S(2)}, u32[]{:S(2)}) collective-permute-start(bf16[128,4096]{1,0:T(8,128)(2,1)S(1)} %add_convert_fusion.5), channel_id=1, source_target_pairs={{0,4},{1,3},{2,6},{3,1},{4,0},{5,7},{6,2},{7,5}} | collective-permute-start | bytes 3145736 | tf_op jit(solution)/shard_map/ppermute | solution.py:390
  (70 other events, 1034.3 us)
Sparse Core Ops, SparseCore 0:
  10.4 51.4 all-gather.14
  63.7 48.6 all-gather.16
  114.3 48.6 all-gather.12
  230.9 48.9 all-gather.18
  331.5 55.8 all-gather.22
  438.2 54.6 all-gather.20
  543.9 54.4 all-gather.24
  649.6 47.7 all-gather.28
  750.1 47.3 all-gather.26
  850.9 47.3 all-gather.30
  951.8 53.8 all-gather.34
  1057.0 54.7 all-gather.32

commit v6 on v5

--- a/solution.py
+++ b/solution.py
@@ -97,7 +97,7 @@
     )(acts, cos_tab, sin_tab, w_q, w_k, w_v, b_q[:, None, :], b_k[:, None, :], b_v[:, None, :])
 
 
-def attention_kernel(start_ref, q_ref, kn_ref, vn_ref, ko_ref, vo_ref, held_ref, o_ref, score_ref, peak_ref, top_ref, total_ref, mixed_ref, *, seq, group, key_block, new_block):
+def attention_kernel(start_ref, table_ref, q_ref, kn_ref, vn_ref, ko_ref, vo_ref, held_ref, weight_ref, o_ref, lead_ref, score_ref, peak_ref, top_ref, total_ref, mixed_ref, all_ref, tile_ref, stage_ref, tile_sem, stage_sem, *, layer, seq, group, key_block, new_block):
     rows = q_ref.shape[0]
     head_dim = kn_ref.shape[1]
     window = ko_ref.shape[0]
@@ -174,57 +174,92 @@
     lax.fori_loop(0, old_steps, mix_old, 0)
     lax.fori_loop(0, new_steps, mix_new, 0)
     mixed = (mixed_ref[...] / jnp.sum(total_ref[...], axis=1, keepdims=True)).astype(jnp.bfloat16)
+    here = pl.ds(pl.multiple_of(block * rows, rows), rows)
     for g in range(group):
         o_ref[:, g * head_dim:(g + 1) * head_dim] = mixed[g * rows:(g + 1) * rows]
-
-
-def attend(query, key_new, value_new, key_cache, value_cache, held, start_pos, layer, seq, rows=256, key_block=2048, new_block=512):
+        all_ref[here, g * head_dim:(g + 1) * head_dim] = mixed[g * rows:(g + 1) * rows]
+
+    tiles, _, cols = tile_ref.shape
+
+    def tile_copy(i):
+        return pltpu.make_async_copy(weight_ref.at[layer, :, i * cols:(i + 1) * cols], tile_ref.at[i], tile_sem.at[i])
+
+    def stage_copy(i):
+        return pltpu.make_async_copy(stage_ref.at[:, i * cols:(i + 1) * cols], lead_ref.at[:, i * cols:(i + 1) * cols], stage_sem.at[i])
+
+    @pl.when(block == 0)
+    def _():
+        for i in range(tiles):
+            tile_copy(i).start()
+
+    @pl.when(block == pl.num_programs(0) - 1)
+    def _():
+        shards = table_ref.shape[0] // 2
+        part = all_ref.shape[0] // table_ref.shape[0]
+        picked = [all_ref[pl.ds(pl.multiple_of(table_ref[shards + i] * part, part), part), :] for i in range(shards)]
+        picked = jnp.concatenate(picked, axis=0)
+        for i in range(tiles):
+            tile_copy(i).wait()
+            stage_ref[:, i * cols:(i + 1) * cols] = jnp.dot(picked, tile_ref[i], preferred_element_type=jnp.float32).astype(jnp.bfloat16)
+            stage_copy(i).start()
+        for i in range(tiles):
+            stage_copy(i).wait()
+
+
+def attend(query, key_new, value_new, key_cache, value_cache, held, start_pos, table, w_o, layer, seq, rows=256, key_block=2048, new_block=512):
     chunk, q_cols = query.shape
     window, head_dim = key_cache.shape[2:]
     group = q_cols // head_dim
     keys = window + chunk
+    model = w_o.shape[2]
+    cols = 1024
     whole = pl.BlockSpec((chunk, head_dim), lambda i, *_: (0, 0))
     cache = pl.BlockSpec((None, None, window, head_dim), lambda i, *_: (layer, seq, 0, 0))
     return pl.pallas_call(
-        functools.partial(attention_kernel, seq=seq, group=group, key_block=key_block, new_block=new_block),
+        functools.partial(attention_kernel, layer=layer, seq=seq, group=group, key_block=key_block, new_block=new_block),
         grid_spec=pltpu.PrefetchScalarGridSpec(
-            num_scalar_prefetch=1,
+            num_scalar_prefetch=2,
             grid=(chunk // rows,),
-            in_specs=[pl.BlockSpec((rows, q_cols), lambda i, *_: (i, 0)), whole, whole, cache, cache, pl.BlockSpec((None, 1, window), lambda i, *_: (seq, 0, 0))],
-            out_specs=pl.BlockSpec((rows, q_cols), lambda i, *_: (i, 0)),
-            scratch_shapes=[pltpu.VMEM((rows * group, keys), jnp.float32), pltpu.VMEM((rows * group, 128), jnp.float32), pltpu.VMEM((rows * group, 1), jnp.float32), pltpu.VMEM((rows * group, 128), jnp.float32), pltpu.VMEM((rows * group, head_dim), jnp.float32)],
+            in_specs=[pl.BlockSpec((rows, q_cols), lambda i, *_: (i, 0)), whole, whole, cache, cache, pl.BlockSpec((None, 1, window), lambda i, *_: (seq, 0, 0)), pl.BlockSpec(memory_space=pl.ANY)],
+            out_specs=[pl.BlockSpec((rows, q_cols), lambda i, *_: (i, 0)), pl.BlockSpec(memory_space=pl.ANY)],
+            scratch_shapes=[pltpu.VMEM((rows * group, keys), jnp.float32), pltpu.VMEM((rows * group, 128), jnp.float32), pltpu.VMEM((rows * group, 1), jnp.float32), pltpu.VMEM((rows * group, 128), jnp.float32), pltpu.VMEM((rows * group, head_dim), jnp.float32),
+                pltpu.VMEM((chunk, q_cols), jnp.bfloat16), pltpu.VMEM((model // cols, q_cols, cols), jnp.bfloat16), pltpu.VMEM((chunk // 2, model), jnp.bfloat16),
+                pltpu.SemaphoreType.DMA((model // cols,)), pltpu.SemaphoreType.DMA((model // cols,))],
         ),
-        out_shape=jax.ShapeDtypeStruct((chunk, q_cols), jnp.bfloat16),
+        out_shape=[jax.ShapeDtypeStruct((chunk, q_cols), jnp.bfloat16), jax.ShapeDtypeStruct((chunk // 2, model), jnp.bfloat16)],
         compiler_params=pltpu.CompilerParams(dimension_semantics=('arbitrary',), vmem_limit_bytes=VMEM_LIMIT),
         cost_estimate=pl.CostEstimate(flops=8 * chunk * q_cols * keys, bytes_accessed=4 * (window + chunk) * head_dim + 4 * chunk * q_cols, transcendentals=0),
         name='attend',
-    )(start_pos, query, key_new, value_new, key_cache, value_cache, held)
-
-
-def stream_tile(weight_ref, ring_ref, sem_ref, step, steps, layer, tiles):
+    )(start_pos, table, query, key_new, value_new, key_cache, value_cache, held, w_o)
+
+
+def stream_tile(weight_ref, ring_ref, sem_ref, step, steps, layer, first, ahead=0):
     slots, _, cols = ring_ref.shape
 
     def copy(at):
         slot = lax.rem(at, slots)
-        columns = pl.ds(pl.multiple_of(lax.rem(at, tiles) * cols, cols), cols)
+        columns = pl.ds(pl.multiple_of((first + at) * cols, cols), cols)
         return pltpu.make_async_copy(weight_ref.at[layer, :, columns], ring_ref.at[slot], sem_ref.at[slot])
 
-    @pl.when(step == 0)
+    @pl.when(step == -ahead)
     def _():
         for i in range(min(slots - 1, steps)):
             copy(jnp.int32(i)).start()
 
-    @pl.when(step + slots - 1 < steps)
-    def _():
-        copy(step + slots - 1).start()
-
-    copy(step).wait()
-    return ring_ref[lax.rem(step, slots)]
-
-
-def project_kernel(table_ref, *refs, shards, joined, layer, steps):
+    def take():
+        @pl.when(step + slots - 1 < steps)
+        def _():
+            copy(step + slots - 1).start()
+
+        copy(step).wait()
+        return ring_ref[lax.rem(step, slots)]
+
+    return take
+
+
+def project_kernel(table_ref, *refs, shards, joined, layer, steps, first):
     acts_refs, (weight_ref, *refs), (ring_ref, sem_ref) = refs[:shards], refs[shards:-2], refs[-2:]
-    weight = stream_tile(weight_ref, ring_ref, sem_ref, pl.program_id(0), steps, layer, steps)
+    weight = stream_tile(weight_ref, ring_ref, sem_ref, pl.program_id(0), steps, layer, first)()
     total = jnp.dot(jnp.concatenate([ref[...] for ref in acts_refs], axis=0), weight, preferred_element_type=jnp.float32)
     if not joined:
         refs[0][...] = total.astype(jnp.bfloat16)
@@ -235,12 +270,14 @@
         sent_ref[...] = total[total.shape[0] // 2:]
 
 
-def project_rows(table, acts, part, weight, layer, lead, cols, slots=4):
+def project_rows(table, acts, part, weight, layer, lead, cols, slots=4, piece=0, pieces=1):
     depth, model = weight.shape[1:]
     shards = table.shape[0] // 2
     picked = acts.shape[0] // part == shards
     half = part * shards
     first = 0 if picked or lead is not None else shards
+    model = model // pieces
+    steps = model // cols
     out = lambda rows: pl.BlockSpec((rows, cols), lambda i, *_: (0, i))
     shape = lambda rows: jax.ShapeDtypeStruct((rows, model), jnp.bfloat16)
     shard = lambda at: pl.BlockSpec((part, depth), lambda i, places: (at if picked else places[at], 0))
@@ -249,11 +286,11 @@
     if lead is None:
         out_specs, out_shape = [out(half)], [shape(half)]
     else:
-        in_specs.append(out(half))
+        in_specs.append(pl.BlockSpec((half, cols), lambda i, *_: (0, piece * steps + i)))
         args.append(lead)
         out_specs, out_shape = [out(half // 2)] * 2, [shape(half // 2)] * 2
     return pl.pallas_call(
-        functools.partial(project_kernel, shards=shards, joined=lead is not None, layer=layer, steps=model // cols),
+        functools.partial(project_kernel, shards=shards, joined=lead is not None, layer=layer, steps=steps, first=piece * steps),
         grid_spec=pltpu.PrefetchScalarGridSpec(
             num_scalar_prefetch=1,
             grid=(model // cols,),
@@ -270,7 +307,7 @@
 
 def expand_kernel(table_ref, *refs, shards, layer, tiles):
     x_refs, (weight_ref, bias_ref, out_ref, ring_ref, sem_ref) = refs[:shards], refs[shards:]
-    weight = stream_tile(weight_ref, ring_ref, sem_ref, pl.program_id(0), tiles, layer, tiles)
+    weight = stream_tile(weight_ref, ring_ref, sem_ref, pl.program_id(0), tiles, layer, 0)()
     acts = jnp.concatenate([ref[...] for ref in x_refs], axis=0)
     lifted = jnp.dot(acts, weight, preferred_element_type=jnp.float32) + bias_ref[...].astype(jnp.float32)
     out_ref[...] = jax.nn.gelu(lifted, approximate=True).astype(jnp.bfloat16)
@@ -298,6 +335,53 @@
         cost_estimate=pl.CostEstimate(flops=2 * rows * model * width, bytes_accessed=2 * (rows * model + model * width + rows * width), transcendentals=0),
         name='expand',
     )(table, *[acts] * shards, weight, bias)
+
+
+def lead_kernel(table_ref, *refs, shards, layer, tiles, steps):
+    x_refs, (up_ref, bias_ref, down_ref, out_ref, act_ref, up_ring, up_sem, down_ring, down_sem) = refs[:shards], refs[shards:]
+    cols = up_ring.shape[2]
+    step = pl.program_id(0)
+    take_up = stream_tile(up_ref, up_ring, up_sem, step, tiles, layer, 0)
+    take_down = stream_tile(down_ref, down_ring, down_sem, step - tiles, steps, layer, 0, ahead=2)
+
+    @pl.when(step < tiles)
+    def _():
+        acts = jnp.concatenate([ref[...] for ref in x_refs], axis=0)
+        at = pl.ds(pl.multiple_of(step * cols, cols), cols)
+        lifted = jnp.dot(acts, take_up(), preferred_element_type=jnp.float32) + bias_ref[:, at].astype(jnp.float32)
+        act_ref[:, at] = jax.nn.gelu(lifted, approximate=True).astype(jnp.bfloat16)
+
+    @pl.when(step >= tiles)
+    def _():
+        out_ref[...] = jnp.dot(act_ref[...], take_down(), preferred_element_type=jnp.float32).astype(jnp.bfloat16)
+
+
+def lead_rows(table, acts, w_up, bias, w_down, layer, up_cols=256, down_cols=512, slots=4):
+    chunk, model = acts.shape
+    width = w_up.shape[2]
+    tiles, steps = width // up_cols, model // down_cols
+    shards = table.shape[0] // 2
+    part = chunk // table.shape[0]
+    rows = part * shards
+    shard = lambda at: pl.BlockSpec((part, model), lambda i, places: (places[at], 0))
+    return pl.pallas_call(
+        functools.partial(lead_kernel, shards=shards, layer=layer, tiles=tiles, steps=steps),
+        grid_spec=pltpu.PrefetchScalarGridSpec(
+            num_scalar_prefetch=1,
+            grid=(tiles + steps,),
+            in_specs=[shard(shards + k) for k in range(shards)] + [pl.BlockSpec(memory_space=pl.ANY), pl.BlockSpec((None, 1, width), lambda i, *_: (layer, 0, 0)), pl.BlockSpec(memory_space=pl.ANY)],
+            out_specs=pl.BlockSpec((rows, down_cols), lambda i, *_: (0, jnp.maximum(i - tiles, 0))),
+            scratch_shapes=[
+                pltpu.VMEM((rows, width), jnp.bfloat16),
+                pltpu.VMEM((slots, model, up_cols), jnp.bfloat16), pltpu.SemaphoreType.DMA((slots,)),
+                pltpu.VMEM((slots, width, down_cols), jnp.bfloat16), pltpu.SemaphoreType.DMA((slots,)),
+            ],
+        ),
+        out_shape=jax.ShapeDtypeStruct((rows, model), jnp.bfloat16),
+        compiler_params=pltpu.CompilerParams(dimension_semantics=('arbitrary',), vmem_limit_bytes=VMEM_LIMIT),
+        cost_estimate=pl.CostEstimate(flops=4 * rows * model * width, bytes_accessed=2 * (2 * rows * model + 2 * model * width), transcendentals=0),
+        name='lead_rows',
+    )(table, *[acts] * shards, w_up, bias, w_down)
 
 
 def cache_kernel(start_ref, ko_ref, vo_ref, kn_ref, vn_ref, kout_ref, vout_ref, ring_ref):
@@ -408,21 +492,41 @@
             yield
             return kept, came, last
 
+        def scatter_last(lead, acts, layer, pieces=2):
+            lead = send(lead, pairs_core)
+            yield
+            active = []
+            state = []
+
+            def make(acts, piece):
+                if not active:
+                    active.append(expand_rows(table, acts, w_up, up_bias, layer, 0))
+                return project_rows(table, active[0], part, w_down, layer, lead, 512, 4, piece, pieces)
+
+            for piece in range(pieces):
+                kept, sent = item(functools.partial(make, piece=piece), acts)
+                state.append((kept, send(sent, pairs_first)))
+            yield
+            lasts = []
+            for kept, came in state:
+                onward, = item(add_came, kept, came)
+                lasts.append(send(onward, pairs_second))
+            yield
+            return [(kept, came, last) for (kept, came), last in zip(state, lasts)]
+
         def attention(gathered, layer, seq):
             query, key_new, value_new = qkv_project(gathered, cos_tab, sin_tab, w_q, w_k, w_v, b_q, b_k, b_v, layer, seq)
             fresh_keys[layer][seq] = key_new
             fresh_values[layer][seq] = value_new
-            mixed = attend(query, key_new, value_new, keys_in, values_in, held, start_pos, layer, seq)
-            lead, = project_rows(table, mixed, part, w_o, layer, None, 1024)
+            mixed, lead = attend(query, key_new, value_new, keys_in, values_in, held, start_pos, table, w_o, layer, seq)
             return lead, mixed
 
         def expand(gathered, layer):
-            active = expand_rows(table, gathered, w_up, up_bias, layer, count // 2)
-            lead, = project_rows(table, active, part, w_down, layer, None, 512)
-            return lead, gathered
-
-        def finish(middle, kept, came, last):
-            summed = kept[:part].astype(jnp.float32) + came[:part].astype(jnp.float32) + last.astype(jnp.float32)
+            return lead_rows(table, gathered, w_up, up_bias, w_down, layer), gathered
+
+        def finish(middle, *terms):
+            sums = [kept[:part].astype(jnp.float32) + came[:part].astype(jnp.float32) + last.astype(jnp.float32) for kept, came, last in zip(*[iter(terms)] * 3)]
+            summed = jnp.concatenate(sums, axis=1)
             return ((middle.astype(jnp.float32) + summed + b_down[layers - 1].astype(jnp.float32)).astype(jnp.bfloat16),)
 
         def join(base, *terms, bias, layer, which):
@@ -447,6 +551,10 @@
                 gathered = gather(normed)
                 yield
                 lead, own = item(functools.partial(expand, layer=layer), gathered)
+                if layer + 1 == layers and seq == TURNS[-1]:
+                    pieces = yield from scatter_last(lead, own, layer)
+                    hidden_out[seq], = item(finish, middle, *[value for piece in pieces for value in piece])
+                    break
                 terms = yield from scatter_sum(lead, own, lambda acts: expand_rows(table, acts, w_up, up_bias, layer, 0), w_down, layer, 512)
                 if layer + 1 < layers:
                     seq_of[0] = seq

time: 1290 us -> 1260 us (0.977)
  Pallas kernels: 778 us -> 752 us
    pallas_call x6 -> x12, Pallas kernels: 198 us -> 386 us  [the longest x6 222 us: attend(): pl.pallas_call(functools.partial(attention_kernel, layer=layer, seq=seq,...]
    pallas_call x24 -> x13, Pallas kernels: 261 us -> 139 us  [project_rows(): pl.pallas_call(functools.partial(project_kernel, shards=shards, joined=le...]
    pallas_call x12 -> x6, Pallas kernels: 181 us -> 89.2 us  [expand_rows(): pl.pallas_call(functools.partial(expand_kernel, shards=shards, layer=laye...]
    ppermute x36 -> x38, waiting for transfers between devices: 374 us -> 363 us  [send(): return lax.ppermute(value, 'tp', pairs)]
  transfers between devices with their start and end apart: 48 -> 50, of which waited for: 19 -> 21; matrix products, arithmetic and copies ran while one was open for 2% -> 2% of each run, Pallas kernels for 60% -> 59%
where the time goes in v6:
time: 1260 us; the launch traced here: 1240 us
  Pallas kernels  752 us (60%)
  waiting for transfers between devices  406 us (32%)
  starting transfers between devices  24.8 us (2%)
  local copies, waits for them, and re-layouts  24.8 us (2%)
  other arithmetic  21.4 us (2%)
  between operations  15.7 us (1%)
    ppermute x38, waiting for transfers between devices, send(): return lax.ppermute(value, 'tp', pairs)  363 us
    pallas_call x6, Pallas kernels, attend(): pl.pallas_call(functools.partial(attention_kernel, layer=layer, seq=seq,...  222 us
    pallas_call x6, Pallas kernels, lead_rows(): pl.pallas_call(functools.partial(lead_kernel, shards=shards, layer=layer,...  164 us
    pallas_call x13, Pallas kernels, project_rows(): pl.pallas_call(functools.partial(project_kernel, shards=shards, joined=le...  139 us
    pallas_call x6, Pallas kernels, expand_rows(): pl.pallas_call(functools.partial(expand_kernel, shards=shards, layer=laye...  89.2 us
    pallas_call x6, Pallas kernels, qkv_project(): pl.pallas_call(qkv_kernel, grid=(chunk // rows,), in_specs=[row_block(mod...  75.3 us
    pallas_call x12, Pallas kernels, normalize(): pl.pallas_call(functools.partial(norm_kernel, joined=terms is not None, w...  47.4 us
    all_gather x12, waiting for transfers between devices, gather(): return lax.all_gather(value, 'tp', axis=0, tiled=True)  42.6 us
  transfers between devices with their start and end apart: 50, of which 21 were waited for; matrix products, arithmetic and copies ran while one was open for 2% of the time, Pallas kernels for 59%

profile of v6, /device:TPU:0, one launch (start us, length us, event | category | flops | bytes accessed | tf_op | source)
XLA Modules:
  0.0 1245.0 jit_solution(2505079257877462401)
XLA Ops:
  19.4 42.4 %all-gather.15.cloned.1.call-done.x_ref = bf16[1024,4096]{1,0:T(8,128)(2,1)} async-done(((bf16[128,4096]{1,0:T(8,128)(2,1)}), bf16[1024,4096]{1,0:T(8,128)(2,1)}) %all-gather.15.cloned.1.call-update) | async-done | bytes 8388624 | tf_op jit(solution)/shard_map/all_gather | solution.py:477
  74.1 36.8 %attend.6 = (bf16[1024,512]{1,0:T(8,128)(2,1)}, bf16[512,4096]{1,0:T(8,128)(2,1)}) custom-call(s32[3]{0:T(128)} %start_ref.13, s32[8]{0:T(128)} %stack.113.table_ref, bf16[1024,512]{1,0:T(8,128)(2,1)} %get-tuple-element.173.q_ref, bf16[1024,128]{1,0:T(8,128)(2,1)} %get-tuple-element.174.kn_ref, bf16[1024,128]{1,0:T(8,128)(2,1)} %get-tuple-element.175.vn_ref, ...), custom_call_target="tpu_custom_call" | custom-call | flops 21474836480 | bytes 4718592 | tf_op jit(solution)/shard_map/attend/pallas_call | solution.py:218
  138.8 37.2 %attend.7 = (bf16[1024,512]{1,0:T(8,128)(2,1)}, bf16[512,4096]{1,0:T(8,128)(2,1)}) custom-call(s32[3]{0:T(128)} %start_ref.13, s32[8]{0:T(128)} %stack.113.table_ref, bf16[1024,512]{1,0:T(8,128)(2,1)} %get-tuple-element.182.q_ref, bf16[1024,128]{1,0:T(8,128)(2,1)} %get-tuple-element.183.kn_ref, bf16[1024,128]{1,0:T(8,128)(2,1)} %get-tuple-element.184.vn_ref, ...), custom_call_target="tpu_custom_call" | custom-call | flops 21474836480 | bytes 4718592 | tf_op jit(solution)/shard_map/attend/pallas_call | solution.py:218
  178.0 24.7 %collective-permute-done.1.refs_2_ = bf16[256,4096]{1,0:T(8,128)(2,1)S(1)} collective-permute-done((bf16[256,4096]{1,0:T(8,128)(2,1)}, bf16[256,4096]{1,0:T(8,128)(2,1)S(1)}, u32[]{:S(2)}, u32[]{:S(2)}) %collective-permute-start.1) | collective-permute-done | bytes 2097184 | tf_op jit(solution)/shard_map/ppermute | solution.py:474
  236.8 36.9 %attend.8 = (bf16[1024,512]{1,0:T(8,128)(2,1)}, bf16[512,4096]{1,0:T(8,128)(2,1)}) custom-call(s32[3]{0:T(128)} %start_ref.13, s32[8]{0:T(128)} %stack.113.table_ref, bf16[1024,512]{1,0:T(8,128)(2,1)} %get-tuple-element.196.q_ref, bf16[1024,128]{1,0:T(8,128)(2,1)} %get-tuple-element.197.kn_ref, bf16[1024,128]{1,0:T(8,128)(2,1)} %get-tuple-element.198.vn_ref, ...), custom_call_target="tpu_custom_call" | custom-call | flops 21474836480 | bytes 4718592 | tf_op jit(solution)/shard_map/attend/pallas_call | solution.py:218
  275.4 24.7 %collective-permute-done.4.refs_2_ = bf16[256,4096]{1,0:T(8,128)(2,1)S(1)} collective-permute-done((bf16[256,4096]{1,0:T(8,128)(2,1)}, bf16[256,4096]{1,0:T(8,128)(2,1)S(1)}, u32[]{:S(2)}, u32[]{:S(2)}) %collective-permute-start.4) | collective-permute-done | bytes 2097184 | tf_op jit(solution)/shard_map/ppermute | solution.py:474
  322.2 27.4 %lead_rows.6 = bf16[512,4096]{1,0:T(8,128)(2,1)} custom-call(s32[8]{0:T(128)} %stack.113.table_ref, bf16[1024,4096]{1,0:T(8,128)(2,1)} %all-gather.19.cloned.1.call-done.refs_0_.refs_1_.refs_2_.refs_3_, bf16[1024,4096]{1,0:T(8,128)(2,1)} %all-gather.19.cloned.1.call-done.refs_0_.refs_1_.refs_2_.refs_3_, ...), custom_call_target="tpu_custom_call" | custom-call | flops 15032385536 | bytes 37748736 | tf_op jit(solution)/shard_map/lead_rows/pallas_call | solution.py:367
  351.2 39.8 %collective-permute-done.6.refs_2_ = bf16[256,4096]{1,0:T(8,128)(2,1)S(1)} collective-permute-done((bf16[256,4096]{1,0:T(8,128)(2,1)}, bf16[256,4096]{1,0:T(8,128)(2,1)S(1)}, u32[]{:S(2)}, u32[]{:S(2)}) %collective-permute-start.6) | collective-permute-done | bytes 2097184 | tf_op jit(solution)/shard_map/ppermute | solution.py:474
  393.9 14.8 %expand.6.refs_0_.refs_1_.refs_2_.refs_3_ = bf16[512,1792]{1,0:T(8,128)(2,1)} custom-call(s32[8]{0:T(128)} %stack.113.table_ref, bf16[1024,4096]{1,0:T(8,128)(2,1)} %all-gather.19.cloned.1.call-done.refs_0_.refs_1_.refs_2_.refs_3_, bf16[1024,4096]{1,0:T(8,128)(2,1)} %all-gather.19.cloned.1.call-done.refs_0_.refs_1_.refs_2_.refs_3_, ...), custom_call_target="tpu_custom_call" | custom-call | flops 7516192768 | bytes 20709376 | tf_op jit(solution)/shard_map/expand/pallas_call | solution.py:324
  428.3 27.3 %lead_rows.7 = bf16[512,4096]{1,0:T(8,128)(2,1)} custom-call(s32[8]{0:T(128)} %stack.113.table_ref, bf16[1024,4096]{1,0:T(8,128)(2,1)} %all-gather.23.cloned.1.call-done.refs_0_.refs_1_.refs_2_.refs_3_, bf16[1024,4096]{1,0:T(8,128)(2,1)} %all-gather.23.cloned.1.call-done.refs_0_.refs_1_.refs_2_.refs_3_, ...), custom_call_target="tpu_custom_call" | custom-call | flops 15032385536 | bytes 37748736 | tf_op jit(solution)/shard_map/lead_rows/pallas_call | solution.py:367
  456.6 40.0 %collective-permute-done.10.refs_2_ = bf16[256,4096]{1,0:T(8,128)(2,1)S(1)} collective-permute-done((bf16[256,4096]{1,0:T(8,128)(2,1)}, bf16[256,4096]{1,0:T(8,128)(2,1)S(1)}, u32[]{:S(2)}, u32[]{:S(2)}) %collective-permute-start.10) | collective-permute-done | bytes 2097184 | tf_op jit(solution)/shard_map/ppermute | solution.py:474
  499.4 14.8 %expand.7.refs_0_.refs_1_.refs_2_.refs_3_ = bf16[512,1792]{1,0:T(8,128)(2,1)} custom-call(s32[8]{0:T(128)} %stack.113.table_ref, bf16[1024,4096]{1,0:T(8,128)(2,1)} %all-gather.23.cloned.1.call-done.refs_0_.refs_1_.refs_2_.refs_3_, bf16[1024,4096]{1,0:T(8,128)(2,1)} %all-gather.23.cloned.1.call-done.refs_0_.refs_1_.refs_2_.refs_3_, ...), custom_call_target="tpu_custom_call" | custom-call | flops 7516192768 | bytes 20709376 | tf_op jit(solution)/shard_map/expand/pallas_call | solution.py:324
  514.3 14.2 %project_rows.17 = (bf16[256,4096]{1,0:T(8,128)(2,1)}, bf16[256,4096]{1,0:T(8,128)(2,1)}) custom-call(s32[8]{0:T(128)} %stack.113.table_ref, bf16[512,1792]{1,0:T(8,128)(2,1)} %expand.7.refs_0_.refs_1_.refs_2_.refs_3_, bf16[512,1792]{1,0:T(8,128)(2,1)} %expand.7.refs_0_.refs_1_.refs_2_.refs_3_, bf16[512,1792]{1,0:T(8,128)(2,1)} %expand.7.refs_0_.refs_1_.refs_2_.refs_3_, ...), custom_call_target="tpu_custom_call" | custom-call | flops 7516192768 | bytes 20709376 | tf_op jit(solution)/shard_map/project_rows/pallas_call | solution.py:292
  533.8 27.6 %lead_rows.8 = bf16[512,4096]{1,0:T(8,128)(2,1)} custom-call(s32[8]{0:T(128)} %stack.113.table_ref, bf16[1024,4096]{1,0:T(8,128)(2,1)} %all-gather.21.cloned.1.call-done.refs_0_.refs_1_.refs_2_.refs_3_, bf16[1024,4096]{1,0:T(8,128)(2,1)} %all-gather.21.cloned.1.call-done.refs_0_.refs_1_.refs_2_.refs_3_, ...), custom_call_target="tpu_custom_call" | custom-call | flops 15032385536 | bytes 37748736 | tf_op jit(solution)/shard_map/lead_rows/pallas_call | solution.py:367
  561.8 40.4 %collective-permute-done.13.refs_2_ = bf16[256,4096]{1,0:T(8,128)(2,1)S(1)} collective-permute-done((bf16[256,4096]{1,0:T(8,128)(2,1)}, bf16[256,4096]{1,0:T(8,128)(2,1)S(1)}, u32[]{:S(2)}, u32[]{:S(2)}) %collective-permute-start.13) | collective-permute-done | bytes 2097184 | tf_op jit(solution)/shard_map/ppermute | solution.py:474
  605.0 14.8 %expand.8.refs_0_.refs_1_.refs_2_.refs_3_ = bf16[512,1792]{1,0:T(8,128)(2,1)} custom-call(s32[8]{0:T(128)} %stack.113.table_ref, bf16[1024,4096]{1,0:T(8,128)(2,1)} %all-gather.21.cloned.1.call-done.refs_0_.refs_1_.refs_2_.refs_3_, bf16[1024,4096]{1,0:T(8,128)(2,1)} %all-gather.21.cloned.1.call-done.refs_0_.refs_1_.refs_2_.refs_3_, ...), custom_call_target="tpu_custom_call" | custom-call | flops 7516192768 | bytes 20709376 | tf_op jit(solution)/shard_map/expand/pallas_call | solution.py:324
  651.8 37.0 %attend.9 = (bf16[1024,512]{1,0:T(8,128)(2,1)}, bf16[512,4096]{1,0:T(8,128)(2,1)}) custom-call(s32[3]{0:T(128)} %start_ref.13, s32[8]{0:T(128)} %stack.113.table_ref, bf16[1024,512]{1,0:T(8,128)(2,1)} %get-tuple-element.245.q_ref, bf16[1024,128]{1,0:T(8,128)(2,1)} %get-tuple-element.246.kn_ref, bf16[1024,128]{1,0:T(8,128)(2,1)} %get-tuple-element.247.vn_ref, ...), custom_call_target="tpu_custom_call" | custom-call | flops 21474836480 | bytes 4718592 | tf_op jit(solution)/shard_map/attend/pallas_call | solution.py:218
  689.0 26.0 %collective-permute-done.15.refs_2_ = bf16[256,4096]{1,0:T(8,128)(2,1)S(1)} collective-permute-done((bf16[256,4096]{1,0:T(8,128)(2,1)}, bf16[256,4096]{1,0:T(8,128)(2,1)S(1)}, u32[]{:S(2)}, u32[]{:S(2)}) %collective-permute-start.15) | collective-permute-done | bytes 2097184 | tf_op jit(solution)/shard_map/ppermute | solution.py:474
  749.7 37.0 %attend.10 = (bf16[1024,512]{1,0:T(8,128)(2,1)}, bf16[512,4096]{1,0:T(8,128)(2,1)}) custom-call(s32[3]{0:T(128)} %start_ref.13, s32[8]{0:T(128)} %stack.113.table_ref, bf16[1024,512]{1,0:T(8,128)(2,1)} %get-tuple-element.262.q_ref, bf16[1024,128]{1,0:T(8,128)(2,1)} %get-tuple-element.263.kn_ref, bf16[1024,128]{1,0:T(8,128)(2,1)} %get-tuple-element.264.vn_ref, ...), custom_call_target="tpu_custom_call" | custom-call | flops 21474836480 | bytes 4718592 | tf_op jit(solution)/shard_map/attend/pallas_call | solution.py:218
  786.8 26.2 %collective-permute-done.19.refs_2_ = bf16[256,4096]{1,0:T(8,128)(2,1)S(1)} collective-permute-done((bf16[256,4096]{1,0:T(8,128)(2,1)}, bf16[256,4096]{1,0:T(8,128)(2,1)S(1)}, u32[]{:S(2)}, u32[]{:S(2)}) %collective-permute-start.19) | collective-permute-done | bytes 2097184 | tf_op jit(solution)/shard_map/ppermute | solution.py:474
  847.3 37.0 %attend.11 = (bf16[1024,512]{1,0:T(8,128)(2,1)}, bf16[512,4096]{1,0:T(8,128)(2,1)}) custom-call(s32[3]{0:T(128)} %start_ref.13, s32[8]{0:T(128)} %stack.113.table_ref, bf16[1024,512]{1,0:T(8,128)(2,1)} %get-tuple-element.276.q_ref, bf16[1024,128]{1,0:T(8,128)(2,1)} %get-tuple-element.277.kn_ref, bf16[1024,128]{1,0:T(8,128)(2,1)} %get-tuple-element.278.vn_ref, ...), custom_call_target="tpu_custom_call" | custom-call | flops 21474836480 | bytes 4718592 | tf_op jit(solution)/shard_map/attend/pallas_call | solution.py:218
  884.4 26.2 %collective-permute-done.22.refs_2_ = bf16[256,4096]{1,0:T(8,128)(2,1)S(1)} collective-permute-done((bf16[256,4096]{1,0:T(8,128)(2,1)}, bf16[256,4096]{1,0:T(8,128)(2,1)S(1)}, u32[]{:S(2)}, u32[]{:S(2)}) %collective-permute-start.22) | collective-permute-done | bytes 2097184 | tf_op jit(solution)/shard_map/ppermute | solution.py:474
  932.1 27.6 %lead_rows.9 = bf16[512,4096]{1,0:T(8,128)(2,1)} custom-call(s32[8]{0:T(128)} %stack.113.table_ref, bf16[1024,4096]{1,0:T(8,128)(2,1)} %all-gather.31.cloned.1.call-done.refs_0_.refs_1_.refs_2_.refs_3_, bf16[1024,4096]{1,0:T(8,128)(2,1)} %all-gather.31.cloned.1.call-done.refs_0_.refs_1_.refs_2_.refs_3_, ...), custom_call_target="tpu_custom_call" | custom-call | flops 15032385536 | bytes 37748736 | tf_op jit(solution)/shard_map/lead_rows/pallas_call | solution.py:367
  959.8 40.2 %collective-permute-done.24.refs_2_ = bf16[256,4096]{1,0:T(8,128)(2,1)S(1)} collective-permute-done((bf16[256,4096]{1,0:T(8,128)(2,1)}, bf16[256,4096]{1,0:T(8,128)(2,1)S(1)}, u32[]{:S(2)}, u32[]{:S(2)}) %collective-permute-start.24) | collective-permute-done | bytes 2097184 | tf_op jit(solution)/shard_map/ppermute | solution.py:474
  1002.9 14.8 %expand.9.refs_0_.refs_1_.refs_2_.refs_3_ = bf16[512,1792]{1,0:T(8,128)(2,1)} custom-call(s32[8]{0:T(128)} %stack.113.table_ref, bf16[1024,4096]{1,0:T(8,128)(2,1)} %all-gather.31.cloned.1.call-done.refs_0_.refs_1_.refs_2_.refs_3_, bf16[1024,4096]{1,0:T(8,128)(2,1)} %all-gather.31.cloned.1.call-done.refs_0_.refs_1_.refs_2_.refs_3_, ...), custom_call_target="tpu_custom_call" | custom-call | flops 7516192768 | bytes 20709376 | tf_op jit(solution)/shard_map/expand/pallas_call | solution.py:324
  1037.2 27.1 %lead_rows.10 = bf16[512,4096]{1,0:T(8,128)(2,1)} custom-call(s32[8]{0:T(128)} %stack.113.table_ref, bf16[1024,4096]{1,0:T(8,128)(2,1)} %all-gather.35.cloned.1.call-done.refs_0_.refs_1_.refs_2_.refs_3_, bf16[1024,4096]{1,0:T(8,128)(2,1)} %all-gather.35.cloned.1.call-done.refs_0_.refs_1_.refs_2_.refs_3_, ...), custom_call_target="tpu_custom_call" | custom-call | flops 15032385536 | bytes 37748736 | tf_op jit(solution)/shard_map/lead_rows/pallas_call | solution.py:367
  1064.7 14.8 %expand.10.refs_0_.refs_1_.refs_2_.refs_3_ = bf16[512,1792]{1,0:T(8,128)(2,1)} custom-call(s32[8]{0:T(128)} %stack.113.table_ref, bf16[1024,4096]{1,0:T(8,128)(2,1)} %all-gather.35.cloned.1.call-done.refs_0_.refs_1_.refs_2_.refs_3_, bf16[1024,4096]{1,0:T(8,128)(2,1)} %all-gather.35.cloned.1.call-done.refs_0_.refs_1_.refs_2_.refs_3_, ...), custom_call_target="tpu_custom_call" | custom-call | flops 7516192768 | bytes 20709376 | tf_op jit(solution)/shard_map/expand/pallas_call | solution.py:324
  1079.6 14.2 %project_rows.23 = (bf16[256,4096]{1,0:T(8,128)(2,1)}, bf16[256,4096]{1,0:T(8,128)(2,1)}) custom-call(s32[8]{0:T(128)} %stack.113.table_ref, bf16[512,1792]{1,0:T(8,128)(2,1)} %expand.10.refs_0_.refs_1_.refs_2_.refs_3_, bf16[512,1792]{1,0:T(8,128)(2,1)} %expand.10.refs_0_.refs_1_.refs_2_.refs_3_, bf16[512,1792]{1,0:T(8,128)(2,1)} %expand.10.refs_0_.refs_1_.refs_2_.refs_3_, ...), custom_call_target="tpu_custom_call" | custom-call | flops 7516192768 | bytes 20709376 | tf_op jit(solution)/shard_map/project_rows/pallas_call | solution.py:292
  1093.9 26.9 %lead_rows.11 = bf16[512,4096]{1,0:T(8,128)(2,1)} custom-call(s32[8]{0:T(128)} %stack.113.table_ref, bf16[1024,4096]{1,0:T(8,128)(2,1)} %all-gather.33.cloned.1.call-done.refs_0_.refs_1_.refs_2_.refs_3_, bf16[1024,4096]{1,0:T(8,128)(2,1)} %all-gather.33.cloned.1.call-done.refs_0_.refs_1_.refs_2_.refs_3_, ...), custom_call_target="tpu_custom_call" | custom-call | flops 15032385536 | bytes 37748736 | tf_op jit(solution)/shard_map/lead_rows/pallas_call | solution.py:367
  1125.9 21.7 %collective-permute-done.29 = bf16[256,4096]{1,0:T(8,128)(2,1)S(1)} collective-permute-done((bf16[256,4096]{1,0:T(8,128)(2,1)}, bf16[256,4096]{1,0:T(8,128)(2,1)S(1)}, u32[]{:S(2)}, u32[]{:S(2)}) %collective-permute-start.29) | collective-permute-done | bytes 2097184 | tf_op jit(solution)/shard_map/ppermute | solution.py:474
  1150.2 15.0 %expand.11.refs_0_.refs_1_.refs_2_.refs_3_ = bf16[512,1792]{1,0:T(8,128)(2,1)} custom-call(s32[8]{0:T(128)} %stack.113.table_ref, bf16[1024,4096]{1,0:T(8,128)(2,1)} %all-gather.33.cloned.1.call-done.refs_0_.refs_1_.refs_2_.refs_3_, bf16[1024,4096]{1,0:T(8,128)(2,1)} %all-gather.33.cloned.1.call-done.refs_0_.refs_1_.refs_2_.refs_3_, ...), custom_call_target="tpu_custom_call" | custom-call | flops 7516192768 | bytes 20709376 | tf_op jit(solution)/shard_map/expand/pallas_call | solution.py:324
  1191.4 15.9 %write_caches.1 = (bf16[2,3,4096,128]{3,2,1,0:T(8,128)(2,1)}, bf16[2,3,4096,128]{3,2,1,0:T(8,128)(2,1)}) custom-call(s32[3]{0:T(128)} %start_ref.13, bf16[2,3,4096,128]{3,2,1,0:T(8,128)(2,1)} %bitcast.53, bf16[2,3,4096,128]{3,2,1,0:T(8,128)(2,1)} %bitcast.60, bf16[2,3,1024,128]{3,2,1,0:T(8,128)(2,1)} %get-tuple-element.350.kn_ref, ...), custom_call_target="tpu_custom_call" | custom-call | flops 16777216 | bytes 25165824 | tf_op jit(solution)/shard_map/write_caches/pallas_call | solution.py:415
  (274 shorter events, 357.5 us)
Async XLA Ops:
  7.2 54.7 %all-gather.15.cloned.1.call-start = ((), (), s32[]{:S(2)}) async-start(), calls=%async_computation.1 | async-start | bytes 9437184 | tf_op jit(solution)/shard_map/all_gather | solution.py:477
  10.2 116.6 %all-gather.17.cloned.1.call-start = ((), (), s32[]{:S(2)}) async-start(), calls=%async_computation.2 | async-start | bytes 9437184 | tf_op jit(solution)/shard_map/all_gather | solution.py:477
  13.3 210.9 %all-gather.13.cloned.1.call-start = ((), (), s32[]{:S(2)}) async-start(), calls=%async_computation | async-start | bytes 9437184 | tf_op jit(solution)/shard_map/all_gather | solution.py:477
  16.3 305.9 %all-gather.19.cloned.1.call-start = ((), (), s32[]{:S(2)}) async-start(), calls=%async_computation.3 | async-start | bytes 9437184 | tf_op jit(solution)/shard_map/all_gather | solution.py:477
  176.0 29.8 %collective-permute-start.3 = (bf16[512,4096]{1,0:T(8,128)(2,1)}, bf16[512,4096]{1,0:T(8,128)(2,1)}, u32[]{:S(2)}, u32[]{:S(2)}) collective-permute-start(bf16[512,4096]{1,0:T(8,128)(2,1)} %get-tuple-element.185), channel_id=1, source_target_pairs={{0,1},{1,0},{2,3},{3,2},{4,5},{5,4},{6,7},{7,6}} | collective-permute-start | bytes 12582920 | tf_op jit(solution)/shard_map/ppermute | solution.py:474
  224.1 204.2 %all-gather.23.cloned.1.call-start = ((), (), s32[]{:S(2)}) async-start(), calls=%async_computation.5 | async-start | bytes 9437184 | tf_op jit(solution)/shard_map/all_gather | solution.py:477
  273.8 28.8 %collective-permute-start.5 = (bf16[512,4096]{1,0:T(8,128)(2,1)}, bf16[512,4096]{1,0:T(8,128)(2,1)}, u32[]{:S(2)}, u32[]{:S(2)}) collective-permute-start(bf16[512,4096]{1,0:T(8,128)(2,1)} %get-tuple-element.201), channel_id=1, source_target_pairs={{0,1},{1,0},{2,3},{3,2},{4,5},{5,4},{6,7},{7,6}} | collective-permute-start | bytes 12582920 | tf_op jit(solution)/shard_map/ppermute | solution.py:474
  321.5 212.3 %all-gather.21.cloned.1.call-start = ((), (), s32[]{:S(2)}) async-start(), calls=%async_computation.4 | async-start | bytes 9437184 | tf_op jit(solution)/shard_map/all_gather | solution.py:477
  349.6 59.1 %collective-permute-start.9 = (bf16[512,4096]{1,0:T(8,128)(2,1)}, bf16[512,4096]{1,0:T(8,128)(2,1)}, u32[]{:S(2)}, u32[]{:S(2)}) collective-permute-start(bf16[512,4096]{1,0:T(8,128)(2,1)} %lead_rows.6), channel_id=1, source_target_pairs={{0,1},{1,0},{2,3},{3,2},{4,5},{5,4},{6,7},{7,6}} | collective-permute-start | bytes 12582920 | tf_op jit(solution)/shard_map/ppermute | solution.py:474
  349.7 41.3 %collective-permute-start.6 = (bf16[256,4096]{1,0:T(8,128)(2,1)}, bf16[256,4096]{1,0:T(8,128)(2,1)S(1)}, u32[]{:S(2)}, u32[]{:S(2)}) collective-permute-start(bf16[256,4096]{1,0:T(8,128)(2,1)} %get-tuple-element.206), channel_id=1, source_target_pairs={{0,2},{1,5},{2,0},{3,7},{4,6},{5,1},{6,4},{7,3}} | collective-permute-start | bytes 6291464 | tf_op jit(solution)/shard_map/ppermute | solution.py:474
  392.4 30.5 %collective-permute-start.8 = (bf16[128,4096]{1,0:T(8,128)(2,1)S(1)}, bf16[128,4096]{1,0:T(8,128)(2,1)S(1)}, u32[]{:S(2)}, u32[]{:S(2)}) collective-permute-start(bf16[128,4096]{1,0:T(8,128)(2,1)S(1)} %add_convert_fusion.10), channel_id=1, source_target_pairs={{0,4},{1,3},{2,6},{3,1},{4,0},{5,7},{6,2},{7,5}} | collective-permute-start | bytes 3145736 | tf_op jit(solution)/shard_map/ppermute | solution.py:474
  428.2 211.2 %all-gather.25.cloned.1.call-start = ((), (), s32[]{:S(2)}) async-start(), calls=%async_computation.6 | async-start | bytes 9437184 | tf_op jit(solution)/shard_map/all_gather | solution.py:477
  455.6 58.7 %collective-permute-start.12 = (bf16[512,4096]{1,0:T(8,128)(2,1)}, bf16[512,4096]{1,0:T(8,128)(2,1)}, u32[]{:S(2)}, u32[]{:S(2)}) collective-permute-start(bf16[512,4096]{1,0:T(8,128)(2,1)} %lead_rows.7), channel_id=1, source_target_pairs={{0,1},{1,0},{2,3},{3,2},{4,5},{5,4},{6,7},{7,6}} | collective-permute-start | bytes 12582920 | tf_op jit(solution)/shard_map/ppermute | solution.py:474
  455.6 41.0 %collective-permute-start.10 = (bf16[256,4096]{1,0:T(8,128)(2,1)}, bf16[256,4096]{1,0:T(8,128)(2,1)S(1)}, u32[]{:S(2)}, u32[]{:S(2)}) collective-permute-start(bf16[256,4096]{1,0:T(8,128)(2,1)} %get-tuple-element.222), channel_id=1, source_target_pairs={{0,2},{1,5},{2,0},{3,7},{4,6},{5,1},{6,4},{7,3}} | collective-permute-start | bytes 6291464 | tf_op jit(solution)/shard_map/ppermute | solution.py:474
  497.9 30.5 %collective-permute-start.11 = (bf16[128,4096]{1,0:T(8,128)(2,1)S(1)}, bf16[128,4096]{1,0:T(8,128)(2,1)S(1)}, u32[]{:S(2)}, u32[]{:S(2)}) collective-permute-start(bf16[128,4096]{1,0:T(8,128)(2,1)S(1)} %add_convert_fusion.9), channel_id=1, source_target_pairs={{0,4},{1,3},{2,6},{3,1},{4,0},{5,7},{6,2},{7,5}} | collective-permute-start | bytes 3145736 | tf_op jit(solution)/shard_map/ppermute | solution.py:474
  533.7 202.8 %all-gather.29.cloned.1.call-start = ((), (), s32[]{:S(2)}) async-start(), calls=%async_computation.8 | async-start | bytes 9437184 | tf_op jit(solution)/shard_map/all_gather | solution.py:477
  561.4 58.4 %collective-permute-start.14 = (bf16[512,4096]{1,0:T(8,128)(2,1)}, bf16[512,4096]{1,0:T(8,128)(2,1)}, u32[]{:S(2)}, u32[]{:S(2)}) collective-permute-start(bf16[512,4096]{1,0:T(8,128)(2,1)} %lead_rows.8), channel_id=1, source_target_pairs={{0,1},{1,0},{2,3},{3,2},{4,5},{5,4},{6,7},{7,6}} | collective-permute-start | bytes 12582920 | tf_op jit(solution)/shard_map/ppermute | solution.py:474
  561.4 40.8 %collective-permute-start.13 = (bf16[256,4096]{1,0:T(8,128)(2,1)}, bf16[256,4096]{1,0:T(8,128)(2,1)S(1)}, u32[]{:S(2)}, u32[]{:S(2)}) collective-permute-start(bf16[256,4096]{1,0:T(8,128)(2,1)} %get-tuple-element.233), channel_id=1, source_target_pairs={{0,2},{1,5},{2,0},{3,7},{4,6},{5,1},{6,4},{7,3}} | collective-permute-start | bytes 6291464 | tf_op jit(solution)/shard_map/ppermute | solution.py:474
  603.5 30.5 %collective-permute-start.16 = (bf16[128,4096]{1,0:T(8,128)(2,1)S(1)}, bf16[128,4096]{1,0:T(8,128)(2,1)S(1)}, u32[]{:S(2)}, u32[]{:S(2)}) collective-permute-start(bf16[128,4096]{1,0:T(8,128)(2,1)S(1)} %add_convert_fusion.8), channel_id=1, source_target_pairs={{0,4},{1,3},{2,6},{3,1},{4,0},{5,7},{6,2},{7,5}} | collective-permute-start | bytes 3145736 | tf_op jit(solution)/shard_map/ppermute | solution.py:474
  639.3 195.1 %all-gather.27.cloned.1.call-start = ((), (), s32[]{:S(2)}) async-start(), calls=%async_computation.7 | async-start | bytes 9437184 | tf_op jit(solution)/shard_map/all_gather | solution.py:477
  688.8 27.9 %collective-permute-start.18 = (bf16[512,4096]{1,0:T(8,128)(2,1)}, bf16[512,4096]{1,0:T(8,128)(2,1)}, u32[]{:S(2)}, u32[]{:S(2)}) collective-permute-start(bf16[512,4096]{1,0:T(8,128)(2,1)} %get-tuple-element.248), channel_id=1, source_target_pairs={{0,1},{1,0},{2,3},{3,2},{4,5},{5,4},{6,7},{7,6}} | collective-permute-start | bytes 12582920 | tf_op jit(solution)/shard_map/ppermute | solution.py:474
  736.5 195.6 %all-gather.31.cloned.1.call-start = ((), (), s32[]{:S(2)}) async-start(), calls=%async_computation.9 | async-start | bytes 9437184 | tf_op jit(solution)/shard_map/all_gather | solution.py:477
  834.4 202.8 %all-gather.35.cloned.1.call-start = ((), (), s32[]{:S(2)}) async-start(), calls=%async_computation.11 | async-start | bytes 9437184 | tf_op jit(solution)/shard_map/all_gather | solution.py:477
  884.3 27.6 %collective-permute-start.23 = (bf16[512,4096]{1,0:T(8,128)(2,1)}, bf16[512,4096]{1,0:T(8,128)(2,1)}, u32[]{:S(2)}, u32[]{:S(2)}) collective-permute-start(bf16[512,4096]{1,0:T(8,128)(2,1)} %get-tuple-element.281), channel_id=1, source_target_pairs={{0,1},{1,0},{2,3},{3,2},{4,5},{5,4},{6,7},{7,6}} | collective-permute-start | bytes 12582920 | tf_op jit(solution)/shard_map/ppermute | solution.py:474
  932.0 161.8 %all-gather.33.cloned.1.call-start = ((), (), s32[]{:S(2)}) async-start(), calls=%async_computation.10 | async-start | bytes 9437184 | tf_op jit(solution)/shard_map/all_gather | solution.py:477
  959.8 57.9 %collective-permute-start.27 = (bf16[512,4096]{1,0:T(8,128)(2,1)}, bf16[512,4096]{1,0:T(8,128)(2,1)}, u32[]{:S(2)}, u32[]{:S(2)}) collective-permute-start(bf16[512,4096]{1,0:T(8,128)(2,1)} %lead_rows.9), channel_id=1, source_target_pairs={{0,1},{1,0},{2,3},{3,2},{4,5},{5,4},{6,7},{7,6}} | collective-permute-start | bytes 12582920 | tf_op jit(solution)/shard_map/ppermute | solution.py:474
  959.8 40.2 %collective-permute-start.24 = (bf16[256,4096]{1,0:T(8,128)(2,1)}, bf16[256,4096]{1,0:T(8,128)(2,1)S(1)}, u32[]{:S(2)}, u32[]{:S(2)}) collective-permute-start(bf16[256,4096]{1,0:T(8,128)(2,1)} %get-tuple-element.286), channel_id=1, source_target_pairs={{0,2},{1,5},{2,0},{3,7},{4,6},{5,1},{6,4},{7,3}} | collective-permute-start | bytes 6291464 | tf_op jit(solution)/shard_map/ppermute | solution.py:474
  1001.4 30.5 %collective-permute-start.26 = (bf16[128,4096]{1,0:T(8,128)(2,1)S(1)}, bf16[128,4096]{1,0:T(8,128)(2,1)S(1)}, u32[]{:S(2)}, u32[]{:S(2)}) collective-permute-start(bf16[128,4096]{1,0:T(8,128)(2,1)S(1)} %add_convert_fusion.4), channel_id=1, source_target_pairs={{0,4},{1,3},{2,6},{3,1},{4,0},{5,7},{6,2},{7,5}} | collective-permute-start | bytes 3145736 | tf_op jit(solution)/shard_map/ppermute | solution.py:474
  1064.4 59.0 %collective-permute-start.30 = (bf16[256,4096]{1,0:T(8,128)(2,1)}, bf16[256,4096]{1,0:T(8,128)(2,1)}, u32[]{:S(2)}, u32[]{:S(2)}) collective-permute-start(bf16[256,4096]{1,0:T(8,128)(2,1)} %get-tuple-element.307), channel_id=1, source_target_pairs={{0,2},{1,5},{2,0},{3,7},{4,6},{5,1},{6,4},{7,3}} | collective-permute-start | bytes 6291464 | tf_op jit(solution)/shard_map/ppermute | solution.py:474
  1120.8 44.4 %collective-permute-start.31 = (bf16[512,4096]{1,0:T(8,128)(2,1)}, bf16[512,4096]{1,0:T(8,128)(2,1)}, u32[]{:S(2)}, u32[]{:S(2)}) collective-permute-start(bf16[512,4096]{1,0:T(8,128)(2,1)} %lead_rows.11), channel_id=1, source_target_pairs={{0,1},{1,0},{2,3},{3,2},{4,5},{5,4},{6,7},{7,6}} | collective-permute-start | bytes 12582920 | tf_op jit(solution)/shard_map/ppermute | solution.py:474
  1174.7 33.1 %collective-permute-start.32 = (bf16[256,2048]{1,0:T(8,128)(2,1)}, bf16[256,2048]{1,0:T(8,128)(2,1)}, u32[]{:S(2)}, u32[]{:S(2)}) collective-permute-start(bf16[256,2048]{1,0:T(8,128)(2,1)} %get-tuple-element.314), channel_id=1, source_target_pairs={{0,2},{1,5},{2,0},{3,7},{4,6},{5,1},{6,4},{7,3}} | collective-permute-start | bytes 3145736 | tf_op jit(solution)/shard_map/ppermute | solution.py:474
  1187.8 27.9 %collective-permute-start.37 = (bf16[128,4096]{1,0:T(8,128)(2,1)}, bf16[128,4096]{1,0:T(8,128)(2,1)}, u32[]{:S(2)}, u32[]{:S(2)}) collective-permute-start(bf16[128,4096]{1,0:T(8,128)(2,1)} %add_convert_fusion.2), channel_id=1, source_target_pairs={{0,4},{1,3},{2,6},{3,1},{4,0},{5,7},{6,2},{7,5}} | collective-permute-start | bytes 3145736 | tf_op jit(solution)/shard_map/ppermute | solution.py:474
  (73 other events, 1317.7 us)
Sparse Core Ops, SparseCore 0:
  10.4 51.4 all-gather.14
  63.7 48.7 all-gather.16
  114.3 48.7 all-gather.12
  224.2 48.8 all-gather.18
  321.7 56.6 all-gather.22
  428.3 55.4 all-gather.20
  533.9 55.3 all-gather.24
  639.4 47.7 all-gather.28
  736.6 47.4 all-gather.26
  834.5 47.3 all-gather.30
  932.1 54.6 all-gather.34
  1037.3 55.6 all-gather.32
